TPU v7x, 128 devices: a whole 4x4x4 slice. The times are simulated.
128 devices in a mesh: px: 8 (over x, z_lo), py: 16 (over z_hi, y, core).
Axes of the slice: x: 4, y: 4, z: 4 (z_hi: 2, z_lo: 2; z = z_hi * 2 + z_lo), core: 2. Of those that a mesh axis runs over, the one named last changes fastest.
Arguments:
- velocity: float32 [3, 8, 512, 2048], P(None, None, 'py', 'px'), may hold values from -6 to 6
- thickness: float32 [8, 512, 2048], P(None, 'py', 'px'), may hold values from 1 to 4
- velocity_tendency: float32 [3, 8, 512, 2048], P(None, None, 'py', 'px'), may hold values from -6 to 6
- thickness_tendency: float32 [8, 512, 2048], P(None, 'py', 'px'), may hold values from -0.5 to 0.5
- cell_distance: float32 [3, 512, 2048], P(None, 'py', 'px'), may hold values from 0.5 to 2
- edge_length: float32 [3, 512, 2048], P(None, 'py', 'px'), may hold values from 0.5 to 2
- cell_area: float32 [512, 2048], P('py', 'px'), may hold values from 1 to 4
- kite_area: float32 [2, 3, 512, 2048], P(None, None, 'py', 'px'), may hold values from 0.2 to 0.8
- coriolis: float32 [2, 512, 2048], P(None, 'py', 'px'), may hold values from -1 to 1
Outputs:
- vertex_potential: float32 [2, 8, 512, 2048], P(None, None, 'py', 'px')
- kinetic_energy: float32 [8, 512, 2048], P(None, 'py', 'px')
- cell_potential: float32 [8, 512, 2048], P(None, 'py', 'px')
- edge_potential: float32 [3, 8, 512, 2048], P(None, None, 'py', 'px')
All inputs are finite; a program needn't handle non-finite values.
Results may differ from a plain program's by a relative error of at most 0.00002.
Values sent between devices are 32-bit elements; how exact they have to be, the bound alone decides.
No kernel may reach another device: no remote copies, remote signals or barrier semaphores. Data moves between devices by JAX's collectives and lax.ppermute only.
A program may use at most 64 MiB of HBM per device.

v0:
```python
import jax
import jax.numpy as jnp
from jax import lax
from jax.sharding import PartitionSpec as P

SECTIONS = 4


SECTION_STEP = (0.0, 0.5, 0.5, 1.0)
SECTION_WEIGHT = (1.0 / 6.0, 1.0 / 3.0, 1.0 / 3.0, 1.0 / 6.0)
UPWIND_FACTOR = 0.5


def with_halo(cells, sides, width):
    for axis, dim in sides:
        count = lax.axis_size(axis)
        head = lax.slice_in_dim(cells, 0, width, axis=dim)
        tail = lax.slice_in_dim(cells, cells.shape[dim] - width, cells.shape[dim], axis=dim)
        cells = jnp.concatenate(
            [
                lax.ppermute(tail, axis, [(i, (i + 1) % count) for i in range(count)]),
                cells,
                lax.ppermute(head, axis, [((i + 1) % count, i) for i in range(count)]),
            ],
            axis=dim,
        )
    return cells


def offset(padded, margin, first_off, second_off):
    row_count = padded.shape[-2] - 2 * margin
    col_count = padded.shape[-1] - 2 * margin
    return padded[
        ...,
        margin + first_off : margin + first_off + row_count,
        margin + second_off : margin + second_off + col_count,
    ]


def cell_mean(vertex_pad, margin):
    return (
        offset(vertex_pad[0], margin, 0, 0)
        + offset(vertex_pad[1], margin, 0, 0)
        + offset(vertex_pad[0], margin, -1, 0)
        + offset(vertex_pad[0], margin, 0, -1)
        + offset(vertex_pad[1], margin, 0, -1)
        + offset(vertex_pad[1], margin, 1, -1)
    ) / 6.0


def local(
    velocity,
    thickness,
    velocity_tendency,
    thickness_tendency,
    cell_distance,
    edge_length,
    cell_area,
    kite_area,
    coriolis,
):
    levels = thickness.shape[0]
    row_count = thickness.shape[1]
    col_count = thickness.shape[2]
    rim_width = 3
    geometry = jnp.concatenate([cell_distance, 0.25 * cell_distance * edge_length], axis=0)
    geometry_pad = with_halo(geometry, (("px", 2), ("py", 1)), rim_width)
    vertex_geometry = jnp.concatenate(
        [kite_area.reshape(6, row_count, col_count), coriolis], axis=0
    )
    vertex_geometry_pad = with_halo(vertex_geometry, (("px", 2), ("py", 1)), 2)
    kite_used = vertex_geometry_pad[0:6].reshape((2, 3, row_count + 4, col_count + 4))
    coriolis_used = vertex_geometry_pad[6:8]
    triangle_area = jnp.sum(kite_used, axis=1)
    padded_shape = (row_count + 2 * rim_width, col_count + 2 * rim_width)
    joined = jnp.concatenate(
        [
            velocity.reshape(3 * levels, row_count, col_count),
            thickness,
            velocity_tendency.reshape(3 * levels, row_count, col_count),
            thickness_tendency,
        ],
        axis=0,
    )
    joined_pad = with_halo(joined, (("px", 2), ("py", 1)), rim_width)
    base_count = 4 * levels
    vertex_total = jnp.zeros((2,) + thickness.shape, jnp.float32)
    energy_total = jnp.zeros(thickness.shape, jnp.float32)
    cell_total = jnp.zeros(thickness.shape, jnp.float32)
    edge_total = jnp.zeros(velocity.shape, jnp.float32)
    for section_index in range(SECTIONS):
        step_size = SECTION_STEP[section_index]
        weight_now = SECTION_WEIGHT[section_index]
        velocity_pad = joined_pad[0 : 3 * levels].reshape(
            (3, levels) + padded_shape
        ) + step_size * joined_pad[base_count : base_count + 3 * levels].reshape(
            (3, levels) + padded_shape
        )
        thickness_pad = (
            joined_pad[3 * levels : base_count] + step_size * joined_pad[base_count + 3 * levels :]
        )
        inner_velocity = offset(velocity_pad, rim_width, 0, 0)
        edge_flux = velocity_pad * geometry_pad[0:3][:, None]
        circulation_first = (
            offset(edge_flux[0], 1, 0, 0)
            + offset(edge_flux[2], 1, 1, 0)
            - offset(edge_flux[1], 1, 0, 0)
        )
        circulation_second = (
            offset(edge_flux[1], 1, 0, 0)
            - offset(edge_flux[2], 1, 0, 0)
            - offset(edge_flux[0], 1, -1, 1)
        )
        height_first = (
            kite_used[0, 0] * offset(thickness_pad, 1, 0, 0)
            + kite_used[0, 1] * offset(thickness_pad, 1, 1, 0)
            + kite_used[0, 2] * offset(thickness_pad, 1, 0, 1)
        ) / triangle_area[0]
        height_second = (
            kite_used[1, 0] * offset(thickness_pad, 1, 0, 0)
            + kite_used[1, 1] * offset(thickness_pad, 1, 0, 1)
            + kite_used[1, 2] * offset(thickness_pad, 1, -1, 1)
        ) / triangle_area[1]
        potential_first = (coriolis_used[0] + circulation_first / triangle_area[0]) / height_first
        potential_second = (
            coriolis_used[1] + circulation_second / triangle_area[1]
        ) / height_second
        energy_pad = geometry_pad[3:6][:, None] * velocity_pad * velocity_pad
        kinetic = (
            offset(energy_pad[0], rim_width, 0, 0)
            + offset(energy_pad[1], rim_width, 0, 0)
            + offset(energy_pad[2], rim_width, 0, 0)
            + offset(energy_pad[0], rim_width, -1, 0)
            + offset(energy_pad[1], rim_width, 0, -1)
            + offset(energy_pad[2], rim_width, 1, -1)
        ) / cell_area
        wide_pair = jnp.stack([potential_first, potential_second])
        vertex_pair = offset(wide_pair, rim_width - 1, 0, 0)
        cell_pad = cell_mean(wide_pair, 1)
        vertex_margin = 2
        cell_value = offset(cell_pad, 1, 0, 0)
        cell_below = offset(cell_pad, 1, 1, 0)
        cell_right = offset(cell_pad, 1, 0, 1)
        cell_diagonal = offset(cell_pad, 1, -1, 1)
        mean_zero = 0.5 * (
            offset(wide_pair[0], vertex_margin, 0, 0) + offset(wide_pair[1], vertex_margin, 1, -1)
        )
        mean_one = 0.5 * (
            offset(wide_pair[0], vertex_margin, 0, 0) + offset(wide_pair[1], vertex_margin, 0, 0)
        )
        mean_two = 0.5 * (
            offset(wide_pair[1], vertex_margin, 0, 0) + offset(wide_pair[0], vertex_margin, -1, 0)
        )
        grad_zero = (cell_below - cell_value) / cell_distance[0]
        grad_one = (cell_right - cell_value) / cell_distance[1]
        grad_two = (cell_diagonal - cell_value) / cell_distance[2]
        section_edge = jnp.stack(
            [
                mean_zero - UPWIND_FACTOR * inner_velocity[0] * grad_zero,
                mean_one - UPWIND_FACTOR * inner_velocity[1] * grad_one,
                mean_two - UPWIND_FACTOR * inner_velocity[2] * grad_two,
            ]
        )
        vertex_total = vertex_total + weight_now * vertex_pair
        energy_total = energy_total + weight_now * kinetic
        cell_total = cell_total + weight_now * cell_value
        edge_total = edge_total + weight_now * section_edge
    return (vertex_total, energy_total, cell_total, edge_total)


def solution(mesh):
    placed = (
        P(None, None, "py", "px"),
        P(None, "py", "px"),
        P(None, None, "py", "px"),
        P(None, "py", "px"),
        P(None, "py", "px"),
        P(None, "py", "px"),
        P("py", "px"),
        P(None, None, "py", "px"),
        P(None, "py", "px"),
    )
    return jax.shard_map(
        local,
        mesh=mesh,
        in_specs=placed,
        out_specs=(
            P(None, None, "py", "px"),
            P(None, "py", "px"),
            P(None, "py", "px"),
            P(None, None, "py", "px"),
        ),
        check_vma=False,
    )
```

profile of v0, /device:TPU:25, one launch (start us, length us, event | category | flops | bytes accessed | tf_op | source)
XLA Modules:
  0.0 79.6 jit_solution(12069018761177559682)
XLA Ops:
  0.6 1.0 %multiply_multiply_fusion.3 = f32[3,32,256]{2,1,0:T(8,128)S(1)} fusion(f32[3,32,256]{2,1,0:T(8,128)} %param.14, f32[3,32,256]{2,1,0:T(8,128)} %param.13), kind=kLoop, calls=%fused_computation.229 | loop fusion | flops 49152 | bytes 294912 | tf_op jit(solution)/shard_map/mul | solution.py:66
  1.7 1.6 %fusion.104 = (f32[6,32,3]{2,1,0:T(8,128)}, f32[6,32,3]{2,1,0:T(8,128)}) fusion(f32[3,32,256]{2,1,0:T(8,128)} %param.13, f32[3,32,256]{2,1,0:T(8,128)S(1)} %multiply_multiply_fusion.3), kind=kLoop, calls=%fused_computation.227 | loop fusion | flops 1152 | bytes 201216 | tf_op jit(solution)/shard_map/concatenate | solution.py:66
  3.3 1.6 %collective-permute-start.8 = (f32[6,32,3]{2,1,0:T(8,128)}, f32[6,32,3]{2,1,0:T(8,128)}, u32[]{:S(2)}, u32[]{:S(2)}) collective-permute-start(f32[6,32,3]{2,1,0:T(8,128)} %get-tuple-element.74), channel_id=1, source_target_pairs={{0,16},{16,32},{32,48},{48,64},{64,80},{80,96},{96,112},{112,0},{1... | collective-permute-start | bytes 6920 | tf_op jit(solution)/shard_map/ppermute | solution.py:21
  4.9 2.2 %collective-permute-start.9 = (f32[6,32,3]{2,1,0:T(8,128)}, f32[6,32,3]{2,1,0:T(8,128)}, u32[]{:S(2)}, u32[]{:S(2)}) collective-permute-start(f32[6,32,3]{2,1,0:T(8,128)} %get-tuple-element.75), channel_id=1, source_target_pairs={{16,0},{32,16},{48,32},{64,48},{80,64},{96,80},{112,96},{0,112},{1... | collective-permute-start | bytes 6920 | tf_op jit(solution)/shard_map/ppermute | solution.py:23
  7.1 1.7 %fusion.103 = (f32[8,32,2]{2,1,0:T(8,128)}, f32[8,32,2]{2,1,0:T(8,128)}) fusion(f32[6,32,256]{2,1,0:T(8,128)} %bitcast.144, f32[2,32,256]{2,1,0:T(8,128)} %param.17), kind=kLoop, calls=%fused_computation.225 | loop fusion | flops 1024 | bytes 266240 | tf_op jit(solution)/shard_map/concatenate | solution.py:68
  8.8 3.6 %collective-permute-start.1 = (f32[8,32,2]{2,1,0:T(8,128)}, f32[8,32,2]{2,1,0:T(8,128)S(1)}, u32[]{:S(2)}, u32[]{:S(2)}) collective-permute-start(f32[8,32,2]{2,1,0:T(8,128)} %get-tuple-element.73), channel_id=1, source_target_pairs={{16,0},{32,16},{48,32},{64,48},{80,64},{96,80},{112,96},{0,112},{1... | collective-permute-start | bytes 6152 | tf_op jit(solution)/shard_map/ppermute | solution.py:23
  12.4 1.4 %pad_maximum_fusion.1 = f32[64,32,256]{2,1,0:T(8,128)S(1)} fusion(f32[8,32,256]{2,1,0:T(8,128)} %param.12, f32[24,32,256]{2,1,0:T(8,128)S(1)} %bitcast.134, f32[8,32,256]{2,1,0:T(8,128)} %param.10, f32[24,32,256]{2,1,0:T(8,128)} %bitcast.137), kind=kLoop, calls=%fused_computation.4 | loop fusion | flops 1572864 | bytes 4194304 | tf_op jit(solution)/shard_map/concatenate | solution.py:76
  14.2 1.2 %copy.30 = f32[64,32,3]{0,1,2:T(8,128)} copy(f32[64,32,3]{2,1,0:T(8,128)S(1)} %get-tuple-element.35) | data formatting | bytes 49152 | tf_op jit(solution)/shard_map/slice | solution.py:17
  16.7 1.5 %collective-permute-start.4 = (f32[64,32,3]{0,1,2:T(8,128)S(1)}, f32[64,32,3]{0,1,2:T(8,128)S(1)}, u32[]{:S(2)}, u32[]{:S(2)}) collective-permute-start(f32[64,32,3]{0,1,2:T(8,128)S(1)} %copy.29), channel_id=1, source_target_pairs={{0,16},{16,32},{32,48},{48,64},{64,80},{80,96},{96,112},{112,0},{1... | collective-permute-start | bytes 73736 | tf_op jit(solution)/shard_map/ppermute | solution.py:21
  18.3 0.9 %pad_maximum_fusion.22 = (f32[8,2,260]{2,1,0:T(2,128)S(1)}, f32[8,2,260]{2,1,0:T(2,128)S(1)}) fusion(f32[8,32,2]{2,1,0:T(8,128)S(1)} %collective-permute-done.1, f32[8,32,2]{2,1,0:T(8,128)S(1)} %collective-permute-done, f32[2,32,256]{2,1,0:T(8,128)} %param.17, f32[6,32,256]{2,1,0:T(8,128)S(1)} %bitcast.145), kind=kLoop, calls=%fused_computation.250 | loop fusion | flops 24960 | bytes 299520 | tf_op jit(solution)/shard_map/slice | solution.py:18
  19.1 5.3 %collective-permute-start.2 = (f32[8,2,260]{2,1,0:T(2,128)S(1)}, f32[8,2,260]{2,1,0:T(2,128)S(1)}, u32[]{:S(2)}, u32[]{:S(2)}) collective-permute-start(f32[8,2,260]{2,1,0:T(2,128)S(1)} %get-tuple-element.56), channel_id=1, source_target_pairs={{0,1},{1,2},{2,3},{3,4},{4,5},{5,6},{6,7},{7,8},{8,9},{9,10},{10,1... | collective-permute-start | bytes 49928 | tf_op jit(solution)/shard_map/ppermute | solution.py:21
  24.5 0.9 %pad_maximum_fusion.18 = (f32[6,3,262]{2,1,0:T(4,128)S(1)}, f32[6,3,262]{2,1,0:T(4,128)S(1)}) fusion(f32[6,32,3]{2,1,0:T(8,128)} %collective-permute-done.9, f32[6,32,3]{2,1,0:T(8,128)} %collective-permute-done.8, f32[3,32,256]{2,1,0:T(8,128)S(1)} %multiply_multiply_fusion.3, f32[3,32,256]{2,1,0:T(8,128)S(1)} %copy-done.3), kind=kLoop, calls=%fused_computation.243 | loop fusion | flops 28296 | bytes 238944 | tf_op jit(solution)/shard_map/slice | solution.py:18
  25.4 5.4 %collective-permute-start.10 = (f32[6,3,262]{2,1,0:T(4,128)S(1)}, f32[6,3,262]{2,1,0:T(4,128)S(1)}, u32[]{:S(2)}, u32[]{:S(2)}) collective-permute-start(f32[6,3,262]{2,1,0:T(4,128)S(1)} %get-tuple-element.58), channel_id=1, source_target_pairs={{0,1},{1,2},{2,3},{3,4},{4,5},{5,6},{6,7},{7,8},{8,9},{9,10},{10,1... | collective-permute-start | bytes 56600 | tf_op jit(solution)/shard_map/ppermute | solution.py:21
  33.1 4.7 %collective-permute-done.11 = f32[6,3,262]{2,1,0:T(4,128)S(1)} collective-permute-done((f32[6,3,262]{2,1,0:T(4,128)S(1)}, f32[6,3,262]{2,1,0:T(4,128)S(1)}, u32[]{:S(2)}, u32[]{:S(2)}) %collective-permute-start.11) | collective-permute-done | bytes 18896 | tf_op jit(solution)/shard_map/ppermute | solution.py:23
  37.8 1.9 %pad_maximum_fusion.12 = f32[6,38,262]{2,1,0:T(8,128)} fusion(f32[6,3,262]{2,1,0:T(4,128)S(1)} %collective-permute-done.11, f32[6,32,3]{2,1,0:T(8,128)} %collective-permute-done.9, f32[3,32,256]{2,1,0:T(8,128)S(1)} %copy-done.7, f32[3,32,256]{2,1,0:T(8,128)S(1)} %copy-done.3, f32[6,32,3]{2,1,0:T(8,128)} %collective-permute-done.8, ...), kind=kLoop, calls=%fused_computation.122 | loop fusion | flops 298680 | bytes 477888 | tf_op jit(solution)/shard_map/concatenate | solution.py:19
  39.7 1.0 %copy.31 = f32[64,32,3]{2,1,0:T(8,128)S(1)} copy(f32[64,32,3]{0,1,2:T(8,128)S(1)} %collective-permute-done.4) | data formatting | bytes 49152 | tf_op jit(solution)/shard_map/ppermute | solution.py:21
  40.7 1.8 %copy.32 = f32[64,32,3]{2,1,0:T(8,128)S(1)} copy(f32[64,32,3]{0,1,2:T(8,128)} %collective-permute-done.5) | data formatting | bytes 49152 | tf_op jit(solution)/shard_map/ppermute | solution.py:23
  42.5 1.7 %pad_maximum_fusion.11 = (f32[64,3,262]{2,1,0:T(4,128)S(1)}, f32[64,3,262]{2,1,0:T(4,128)S(1)}) fusion(f32[64,32,3]{2,1,0:T(8,128)S(1)} %copy.32, f32[64,32,3]{2,1,0:T(8,128)S(1)} %copy.31, f32[8,32,256]{2,1,0:T(8,128)S(1)} %copy-done.4, f32[24,32,256]{2,1,0:T(8,128)S(1)} %bitcast.135, f32[8,32,256]{2,1,0:T(8,128)S(1)} %copy-done.5, f32[24,32,256]{2,1,0:T(8,128)} %bitcast.138), kind=kLoop, calls=%fused_computation.119 | loop fusion | flops 503040 | bytes 2548736 | tf_op jit(solution)/shard_map/slice | solution.py:18
  44.9 4.4 %collective-permute-done.6 = f32[64,3,262]{2,1,0:T(4,128)S(1)} collective-permute-done((f32[64,3,262]{2,1,0:T(4,128)S(1)}, f32[64,3,262]{2,1,0:T(4,128)S(1)}, u32[]{:S(2)}, u32[]{:S(2)}) %collective-permute-start.6) | collective-permute-done | bytes 201248 | tf_op jit(solution)/shard_map/ppermute | solution.py:21
  49.3 6.1 %collective-permute-done.7 = f32[64,3,262]{2,1,0:T(4,128)S(1)} collective-permute-done((f32[64,3,262]{2,1,0:T(4,128)S(1)}, f32[64,3,262]{2,1,0:T(4,128)S(1)}, u32[]{:S(2)}, u32[]{:S(2)}) %collective-permute-start.7) | collective-permute-done | bytes 201248 | tf_op jit(solution)/shard_map/ppermute | solution.py:23
  55.4 6.1 %pad_maximum_fusion = f32[64,38,262]{2,1,0:T(8,128)S(1)} fusion(f32[64,3,262]{2,1,0:T(4,128)S(1)} %collective-permute-done.7, f32[64,32,3]{2,1,0:T(8,128)S(1)} %copy.32, f32[8,32,256]{2,1,0:T(8,128)S(1)} %copy-done.4, f32[24,32,256]{2,1,0:T(8,128)S(1)} %bitcast.136, f32[8,32,256]{2,1,0:T(8,128)S(1)} %copy-done.5, f32[24,32,256]{2,1,0:T(8,128)S(1)} %bitcast.139, ...), kind=kLoop, calls=%fused_computation | loop fusion | flops 4460288 | bytes 5097472 | tf_op jit(solution)/shard_map/concatenate | solution.py:19
  61.8 0.9 %multiply_multiply_fusion.2 = (f32[3,8,38,262]{3,2,1,0:T(8,128)S(1)}, f32[3,8,38,262]{3,2,1,0:T(8,128)S(1)}, f32[3,8,38,262]{3,2,1,0:T(8,128)S(1)}, f32[3,8,38,2...) fusion(f32[3,38,262]{2,1,0:T(8,128)S(1)} %get-tuple-element.67, ...), kind=kLoop, calls=%fused_computation.3 | loop fusion | flops 2628384 | bytes 7765680 | tf_op jit(solution)/shard_map/mul | solution.py:128
  64.1 0.9 %fusion.9 = f32[8,36,260]{2,1,0:T(8,128)S(1)} fusion(f32[8,38,262]{2,1,0:T(8,128)S(1)} %get-tuple-element.17, f32[8,38,262]{2,1,0:T(8,128)S(1)} %get-tuple-element.53, f32[8,38,262]{2,1,0:T(8,128)S(1)} %get-tuple-element.52, f32[8,38,262]{2,1,0:T(8,128)S(1)} %get-tuple-element.51, f32[36,260]{1,0:T(8,128)S(1)} %copy-done.10, f32[36,260]{1,0:T(8,128)S(1)} %copy-done.11, ...), kind=kLoop, calls=%fused_computation.52 | loop fusion | flops 823680 | bytes 2283840 | tf_op jit(solution)/shard_map/div | solution.py:125
  65.1 0.9 %fusion.15 = f32[8,36,260]{2,1,0:T(8,128)S(1)} fusion(f32[8,38,262]{2,1,0:T(8,128)S(1)} %get-tuple-element.17, f32[8,38,262]{2,1,0:T(8,128)S(1)} %get-tuple-element.52, f32[8,38,262]{2,1,0:T(8,128)S(1)} %get-tuple-element.53, f32[8,38,262]{2,1,0:T(8,128)S(1)} %get-tuple-element.51, f32[36,260]{1,0:T(8,128)S(1)} %copy-done.14, f32[36,260]{1,0:T(8,128)S(1)} %copy-done.15, ...), kind=kLoop, calls=%fused_computation.61 | loop fusion | flops 823680 | bytes 2283840 | tf_op jit(solution)/shard_map/div | solution.py:124
  66.0 1.8 %fusion.39 = (f32[8,36,260]{2,1,0:T(8,128)S(1)}, f32[8,36,260]{2,1,0:T(8,128)S(1)}) fusion(f32[8,38,262]{2,1,0:T(8,128)S(1)} %get-tuple-element.16, f32[8,38,262]{2,1,0:T(8,128)S(1)} %get-tuple-element.46, f32[8,38,262]{2,1,0:T(8,128)S(1)} %get-tuple-element.47, f32[8,38,262]{2,1,0:T(8,128)S(1)} %get-tuple-element.45, f32[36,260]{1,0:T(8,128)S(1)} %copy-done.14, ...), kind=kLoop, calls=%fused_computation.101 | loop fusion | flops 1647360 | bytes 4380480 | tf_op jit(solution)/shard_map/div | solution.py:124
  67.7 1.7 %fusion.33 = (f32[8,36,260]{2,1,0:T(8,128)S(1)}, f32[8,36,260]{2,1,0:T(8,128)S(1)}) fusion(f32[8,38,262]{2,1,0:T(8,128)S(1)} %get-tuple-element.16, f32[8,38,262]{2,1,0:T(8,128)S(1)} %get-tuple-element.47, f32[8,38,262]{2,1,0:T(8,128)S(1)} %get-tuple-element.46, f32[8,38,262]{2,1,0:T(8,128)S(1)} %get-tuple-element.45, f32[36,260]{1,0:T(8,128)S(1)} %copy-done.10, ...), kind=kLoop, calls=%fused_computation.92 | loop fusion | flops 1647360 | bytes 4380480 | tf_op jit(solution)/shard_map/div | solution.py:125
  71.6 0.9 %fusion.94 = (f32[1,8,32,256]{3,2,1,0:T(8,128)S(1)}, f32[1,8,32,256]{3,2,1,0:T(8,128)S(1)}, f32[1,8,32,256]{3,2,1,0:T(8,128)S(1)}) fusion(f32[8,34,258]{2,1,0:T(8,128)S(1)} %fusion.7, f32[3,8,38,262]{3,2,1,0:T(8,128)S(1)} %get-tuple-element.9, f32[8,36,260]{2,1,0:T(8,128)S(1)} %get-tuple-element.70, f32[8,36,260]{2,1,0:T(8,128)S(1)} %get-tuple-element.68, ...), kind=kLoop, calls=%fused_computation.195 | loop fusion | flops 1376256 | bytes 3768320 | tf_op jit(solution)/shard_map/stack | solution.py:157
  72.9 0.9 %fusion.77 = (f32[1,8,32,256]{3,2,1,0:T(8,128)S(1)}, f32[1,8,32,256]{3,2,1,0:T(8,128)S(1)}, f32[1,8,32,256]{3,2,1,0:T(8,128)S(1)}) fusion(f32[8,34,258]{2,1,0:T(8,128)S(1)} %fusion.6, f32[3,8,38,262]{3,2,1,0:T(8,128)S(1)} %get-tuple-element.22, f32[8,36,260]{2,1,0:T(8,128)S(1)} %get-tuple-element.71, f32[8,36,260]{2,1,0:T(8,128)S(1)} %get-tuple-element.69, ...), kind=kLoop, calls=%fused_computation.170 | loop fusion | flops 1376256 | bytes 3768320 | tf_op jit(solution)/shard_map/stack | solution.py:157
  73.8 1.0 %fusion.45 = f32[8,32,256]{2,1,0:T(8,128)} fusion(f32[8,34,258]{2,1,0:T(8,128)S(1)} %fusion.5, f32[8,34,258]{2,1,0:T(8,128)S(1)} %fusion.6, f32[8,34,258]{2,1,0:T(8,128)S(1)} %fusion.7), kind=kLoop, calls=%fused_computation.124 | loop fusion | flops 393216 | bytes 1048576 | tf_op jit(solution)/shard_map/add | solution.py:166
  75.1 1.4 %fusion.1 = f32[2,8,32,256]{3,2,1,0:T(8,128)} fusion(f32[1,8,36,260]{3,2,1,0:T(8,128)S(1)} %bitcast.128, f32[1,8,36,260]{3,2,1,0:T(8,128)S(1)} %bitcast.129, f32[1,8,36,260]{3,2,1,0:T(8,128)S(1)} %bitcast.133, f32[1,8,36,260]{3,2,1,0:T(8,128)S(1)} %bitcast.131, f32[1,8,36,260]{3,2,1,0:T(8,128)S(1)} %bitcast.132, f32[1,8,36,260]{3,2,1,0:T(8,128)S(1)} %bitcast.130), kind=kLoop, calls=%fused_computation.16 | loop fusion | flops 1179648 | bytes 2321408 | tf_op jit(solution)/shard_map/add | solution.py:164
  76.5 1.1 %fusion = f32[3,8,32,256]{3,2,1,0:T(8,128)} fusion(f32[1,8,32,256]{3,2,1,0:T(8,128)S(1)} %get-tuple-element.32, f32[1,8,32,256]{3,2,1,0:T(8,128)S(1)} %get-tuple-element.33, f32[1,8,32,256]{3,2,1,0:T(8,128)S(1)} %get-tuple-element.31, f32[1,8,32,256]{3,2,1,0:T(8,128)S(1)} %get-tuple-element.29, f32[1,8,32,256]{3,2,1,0:T(8,128)S(1)} %get-tuple-element.30, ...), kind=kLoop, calls=%fused_computation.8 | loop fusion | flops 2359296 | bytes 3145728 | tf_op jit(solution)/shard_map/add | solution.py:167
  77.6 2.0 %fusion.44 = f32[8,32,256]{2,1,0:T(8,128)} fusion(f32[8,38,262]{2,1,0:T(8,128)S(1)} %get-tuple-element.43, f32[8,38,262]{2,1,0:T(8,128)S(1)} %get-tuple-element.44, f32[8,38,262]{2,1,0:T(8,128)S(1)} %get-tuple-element.42, f32[8,38,262]{2,1,0:T(8,128)S(1)} %get-tuple-element.85, f32[8,38,262]{2,1,0:T(8,128)S(1)} %get-tuple-element.84, ...), kind=kLoop, calls=%fused_computation.123 | loop fusion | flops 1572864 | bytes 5013504 | tf_op jit(solution)/shard_map/add | solution.py:165
  (81 shorter events, 9.1 us)
Async XLA Ops:
  0.6 11.8 %copy-start = (f32[3,8,32,256]{3,2,1,0:T(8,128)S(1)}, f32[3,8,32,256]{3,2,1,0:T(8,128)}, u32[]{:S(2)}) copy-start(f32[3,8,32,256]{3,2,1,0:T(8,128)} %param.11) | copy-start | bytes 2359300
  1.7 22.8 %copy-start.6 = (f32[3,32,256]{2,1,0:T(8,128)}, f32[3,32,256]{2,1,0:T(8,128)S(1)}, u32[]{:S(2)}) copy-start(f32[3,32,256]{2,1,0:T(8,128)S(1)} %multiply_multiply_fusion.3) | copy-start | bytes 294916
  3.3 21.2 %collective-permute-start.8 = (f32[6,32,3]{2,1,0:T(8,128)}, f32[6,32,3]{2,1,0:T(8,128)}, u32[]{:S(2)}, u32[]{:S(2)}) collective-permute-start(f32[6,32,3]{2,1,0:T(8,128)} %get-tuple-element.74), channel_id=1, source_target_pairs={{0,16},{16,32},{32,48},{48,64},{64,80},{80,96},{96,112},{112,0},{1... | collective-permute-start | bytes 6920 | tf_op jit(solution)/shard_map/ppermute | solution.py:21
  4.9 19.5 %collective-permute-start.9 = (f32[6,32,3]{2,1,0:T(8,128)}, f32[6,32,3]{2,1,0:T(8,128)}, u32[]{:S(2)}, u32[]{:S(2)}) collective-permute-start(f32[6,32,3]{2,1,0:T(8,128)} %get-tuple-element.75), channel_id=1, source_target_pairs={{16,0},{32,16},{48,32},{64,48},{80,64},{96,80},{112,96},{0,112},{1... | collective-permute-start | bytes 6920 | tf_op jit(solution)/shard_map/ppermute | solution.py:23
  8.8 7.9 %collective-permute-start = (f32[8,32,2]{2,1,0:T(8,128)}, f32[8,32,2]{2,1,0:T(8,128)S(1)}, u32[]{:S(2)}, u32[]{:S(2)}) collective-permute-start(f32[8,32,2]{2,1,0:T(8,128)} %get-tuple-element.72), channel_id=1, source_target_pairs={{0,16},{16,32},{32,48},{48,64},{64,80},{80,96},{96,112},{112,0},{1... | collective-permute-start | bytes 6152 | tf_op jit(solution)/shard_map/ppermute | solution.py:21
  8.8 9.4 %collective-permute-start.1 = (f32[8,32,2]{2,1,0:T(8,128)}, f32[8,32,2]{2,1,0:T(8,128)S(1)}, u32[]{:S(2)}, u32[]{:S(2)}) collective-permute-start(f32[8,32,2]{2,1,0:T(8,128)} %get-tuple-element.73), channel_id=1, source_target_pairs={{16,0},{32,16},{48,32},{64,48},{80,64},{96,80},{112,96},{0,112},{1... | collective-permute-start | bytes 6152 | tf_op jit(solution)/shard_map/ppermute | solution.py:23
  13.8 1.6 %copy-start.3 = (f32[3,32,256]{2,1,0:T(8,128)S(1)}, f32[3,32,256]{2,1,0:T(8,128)}, u32[]{:S(2)}) copy-start(f32[3,32,256]{2,1,0:T(8,128)} %param.13) | copy-start | bytes 294916
  14.2 4.1 %copy-start.2 = (f32[2,3,32,256]{3,2,1,0:T(8,128)S(1)}, f32[2,3,32,256]{3,2,1,0:T(8,128)}, u32[]{:S(2)}) copy-start(f32[2,3,32,256]{3,2,1,0:T(8,128)} %param.16) | copy-start | bytes 589828
  15.5 15.9 %copy-start.9 = (f32[2,32,256]{2,1,0:T(8,128)S(1)}, f32[2,32,256]{2,1,0:T(8,128)}, u32[]{:S(2)}) copy-start(f32[2,32,256]{2,1,0:T(8,128)} %param.17) | copy-start | bytes 196612
  15.5 25.2 %collective-permute-start.5 = (f32[64,32,3]{0,1,2:T(8,128)}, f32[64,32,3]{0,1,2:T(8,128)}, u32[]{:S(2)}, u32[]{:S(2)}) collective-permute-start(f32[64,32,3]{0,1,2:T(8,128)} %copy.30), channel_id=1, source_target_pairs={{16,0},{32,16},{48,32},{64,48},{80,64},{96,80},{112,96},{0,112},{1... | collective-permute-start | bytes 73736 | tf_op jit(solution)/shard_map/ppermute | solution.py:23
  16.7 22.9 %collective-permute-start.4 = (f32[64,32,3]{0,1,2:T(8,128)S(1)}, f32[64,32,3]{0,1,2:T(8,128)S(1)}, u32[]{:S(2)}, u32[]{:S(2)}) collective-permute-start(f32[64,32,3]{0,1,2:T(8,128)S(1)} %copy.29), channel_id=1, source_target_pairs={{0,16},{16,32},{32,48},{48,64},{64,80},{80,96},{96,112},{112,0},{1... | collective-permute-start | bytes 73736 | tf_op jit(solution)/shard_map/ppermute | solution.py:21
  19.1 11.7 %collective-permute-start.2 = (f32[8,2,260]{2,1,0:T(2,128)S(1)}, f32[8,2,260]{2,1,0:T(2,128)S(1)}, u32[]{:S(2)}, u32[]{:S(2)}) collective-permute-start(f32[8,2,260]{2,1,0:T(2,128)S(1)} %get-tuple-element.56), channel_id=1, source_target_pairs={{0,1},{1,2},{2,3},{3,4},{4,5},{5,6},{6,7},{7,8},{8,9},{9,10},{10,1... | collective-permute-start | bytes 49928 | tf_op jit(solution)/shard_map/ppermute | solution.py:21
  24.5 6.9 %collective-permute-start.3 = (f32[8,2,260]{2,1,0:T(2,128)S(1)}, f32[8,2,260]{2,1,0:T(2,128)S(1)}, u32[]{:S(2)}, u32[]{:S(2)}) collective-permute-start(f32[8,2,260]{2,1,0:T(2,128)S(1)} %get-tuple-element.57), channel_id=1, source_target_pairs={{1,0},{2,1},{3,2},{4,3},{5,4},{6,5},{7,6},{8,7},{9,8},{10,9},{11,1... | collective-permute-start | bytes 49928 | tf_op jit(solution)/shard_map/ppermute | solution.py:23
  25.4 7.8 %collective-permute-start.10 = (f32[6,3,262]{2,1,0:T(4,128)S(1)}, f32[6,3,262]{2,1,0:T(4,128)S(1)}, u32[]{:S(2)}, u32[]{:S(2)}) collective-permute-start(f32[6,3,262]{2,1,0:T(4,128)S(1)} %get-tuple-element.58), channel_id=1, source_target_pairs={{0,1},{1,2},{2,3},{3,4},{4,5},{5,6},{6,7},{7,8},{8,9},{9,10},{10,1... | collective-permute-start | bytes 56600 | tf_op jit(solution)/shard_map/ppermute | solution.py:21
  30.8 7.0 %collective-permute-start.11 = (f32[6,3,262]{2,1,0:T(4,128)S(1)}, f32[6,3,262]{2,1,0:T(4,128)S(1)}, u32[]{:S(2)}, u32[]{:S(2)}) collective-permute-start(f32[6,3,262]{2,1,0:T(4,128)S(1)} %get-tuple-element.59), channel_id=1, source_target_pairs={{1,0},{2,1},{3,2},{4,3},{5,4},{6,5},{7,6},{8,7},{9,8},{10,9},{11,1... | collective-permute-start | bytes 56600 | tf_op jit(solution)/shard_map/ppermute | solution.py:23
  31.6 6.2 %copy-start.7 = (f32[3,32,256]{2,1,0:T(8,128)S(1)}, f32[3,32,256]{2,1,0:T(8,128)}, u32[]{:S(2)}) copy-start(f32[3,32,256]{2,1,0:T(8,128)} %copy-done.6) | copy-start | bytes 294916
  33.1 9.3 %copy-start.4 = (f32[8,32,256]{2,1,0:T(8,128)S(1)}, f32[8,32,256]{2,1,0:T(8,128)}, u32[]{:S(2)}) copy-start(f32[8,32,256]{2,1,0:T(8,128)} %param.12) | copy-start | bytes 786436
  33.1 9.3 %copy-start.5 = (f32[8,32,256]{2,1,0:T(8,128)S(1)}, f32[8,32,256]{2,1,0:T(8,128)}, u32[]{:S(2)}) copy-start(f32[8,32,256]{2,1,0:T(8,128)} %param.10) | copy-start | bytes 786436
  42.5 2.3 %copy-start.8 = (f32[6,38,262]{2,1,0:T(8,128)S(1)}, f32[6,38,262]{2,1,0:T(8,128)}, u32[]{:S(2)}) copy-start(f32[6,38,262]{2,1,0:T(8,128)} %pad_maximum_fusion.12) | copy-start | bytes 716836
  42.5 12.9 %copy-start.1 = (f32[3,8,32,256]{3,2,1,0:T(8,128)S(1)}, f32[3,8,32,256]{3,2,1,0:T(8,128)}, u32[]{:S(2)}) copy-start(f32[3,8,32,256]{3,2,1,0:T(8,128)} %param.9) | copy-start | bytes 2359300
  44.2 5.1 %collective-permute-start.6 = (f32[64,3,262]{2,1,0:T(4,128)S(1)}, f32[64,3,262]{2,1,0:T(4,128)S(1)}, u32[]{:S(2)}, u32[]{:S(2)}) collective-permute-start(f32[64,3,262]{2,1,0:T(4,128)S(1)} %get-tuple-element.14), channel_id=1, source_target_pairs={{0,1},{1,2},{2,3},{3,4},{4,5},{5,6},{6,7},{7,8},{8,9},{9,10},{10,1... | collective-permute-start | bytes 603656 | tf_op jit(solution)/shard_map/ppermute | solution.py:21
  44.6 10.8 %collective-permute-start.7 = (f32[64,3,262]{2,1,0:T(4,128)S(1)}, f32[64,3,262]{2,1,0:T(4,128)S(1)}, u32[]{:S(2)}, u32[]{:S(2)}) collective-permute-start(f32[64,3,262]{2,1,0:T(4,128)S(1)} %get-tuple-element.15), channel_id=1, source_target_pairs={{1,0},{2,1},{3,2},{4,3},{5,4},{6,5},{7,6},{8,7},{9,8},{10,9},{11,1... | collective-permute-start | bytes 603656 | tf_op jit(solution)/shard_map/ppermute | solution.py:23
  63.2 0.9 %copy-start.11 = (f32[36,260]{1,0:T(8,128)S(1)}, f32[36,260]{1,0:T(8,128)}, u32[]{:S(2)}) copy-start(f32[36,260]{1,0:T(8,128)} %get-tuple-element.62) | copy-start | bytes 112324
  63.2 0.9 %copy-start.12 = (f32[36,260]{1,0:T(8,128)S(1)}, f32[36,260]{1,0:T(8,128)}, u32[]{:S(2)}) copy-start(f32[36,260]{1,0:T(8,128)} %get-tuple-element.63) | copy-start | bytes 112324
  63.2 0.9 %copy-start.16 = (f32[36,260]{1,0:T(8,128)S(1)}, f32[36,260]{1,0:T(8,128)}, u32[]{:S(2)}) copy-start(f32[36,260]{1,0:T(8,128)} %get-tuple-element.80) | copy-start | bytes 112324
  63.2 0.9 %copy-start.17 = (f32[36,260]{1,0:T(8,128)S(1)}, f32[36,260]{1,0:T(8,128)}, u32[]{:S(2)}) copy-start(f32[36,260]{1,0:T(8,128)} %get-tuple-element.90) | copy-start | bytes 112324
  64.1 0.9 %copy-start.13 = (f32[36,260]{1,0:T(8,128)S(1)}, f32[36,260]{1,0:T(8,128)}, u32[]{:S(2)}) copy-start(f32[36,260]{1,0:T(8,128)} %get-tuple-element.60) | copy-start | bytes 112324
  64.1 0.9 %copy-start.14 = (f32[36,260]{1,0:T(8,128)S(1)}, f32[36,260]{1,0:T(8,128)}, u32[]{:S(2)}) copy-start(f32[36,260]{1,0:T(8,128)} %get-tuple-element.64) | copy-start | bytes 112324
  64.1 0.9 %copy-start.15 = (f32[36,260]{1,0:T(8,128)S(1)}, f32[36,260]{1,0:T(8,128)}, u32[]{:S(2)}) copy-start(f32[36,260]{1,0:T(8,128)} %get-tuple-element.65) | copy-start | bytes 112324
  64.1 0.9 %copy-start.18 = (f32[36,260]{1,0:T(8,128)S(1)}, f32[36,260]{1,0:T(8,128)}, u32[]{:S(2)}) copy-start(f32[36,260]{1,0:T(8,128)} %get-tuple-element.79) | copy-start | bytes 112324
  64.1 0.9 %copy-start.19 = (f32[36,260]{1,0:T(8,128)S(1)}, f32[36,260]{1,0:T(8,128)}, u32[]{:S(2)}) copy-start(f32[36,260]{1,0:T(8,128)} %get-tuple-element.91) | copy-start | bytes 112324
  76.5 1.1 %copy-start.22 = (f32[32,256]{1,0:T(8,128)S(1)}, f32[32,256]{1,0:T(8,128)}, u32[]{:S(2)}) copy-start(f32[32,256]{1,0:T(8,128)} %param.15) | copy-start | bytes 98308
  (3 other events, 2.4 us)
where the time goes:
time: 80.2 us; the launch traced here: 79.6 us
  other arithmetic  34.3 us (43%)
  starting transfers between devices  20.2 us (25%)
  waiting for transfers between devices  15.7 us (20%)
  local copies, waits for them, and re-layouts  8.22 us (10%)
  between operations  1.05 us (1%)
    ppermute x6, starting transfers between devices, with_halo(): lax.ppermute(tail, axis, [(i, (i + 1) % count) for i in range(count)])  14.2 us
    ppermute x6, waiting for transfers between devices, with_halo(): lax.ppermute(head, axis, [((i + 1) % count, i) for i in range(count)])  11.3 us
    concatenate x3, other arithmetic, with_halo(): jnp.concatenate([lax.ppermute(tail, axis, [(i, (i + 1) % count) for i in...  8.24 us
    ppermute x6, starting transfers between devices, with_halo(): lax.ppermute(head, axis, [((i + 1) % count, i) for i in range(count)])  6.02 us
    ppermute x6, waiting for transfers between devices, with_halo(): lax.ppermute(tail, axis, [(i, (i + 1) % count) for i in range(count)])  4.46 us
    slice x3, other arithmetic, with_halo(): lax.slice_in_dim(cells, cells.shape[dim] - width, cells.shape[dim], axis=...  3.5 us
    div x2, other arithmetic, local(): (coriolis_used[0] + circulation_first / triangle_area[0]) / height_first  2.66 us
    another operation x3, other arithmetic, local(): jnp.stack([mean_zero - UPWIND_FACTOR * inner_velocity[0] * grad_zero, mea...  2.59 us
  transfers between devices with their start and end apart: 12, of which 4 were waited for; matrix products, arithmetic and copies ran while one was open for 16% of the time, Pallas kernels for 0%

commit v1 on v0

v1 whole, which is shorter than its diff:
```python
import jax
import jax.numpy as jnp
from jax import lax
from jax.experimental import pallas as pl
from jax.experimental.pallas import tpu as pltpu
from jax.sharding import PartitionSpec as P

F32 = jnp.float32
LV = 8
BASE = 8
UPB, DNB = BASE - 1, BASE + 32


def iota(shape, dim):
    return lax.broadcasted_iota(jnp.int32, shape, dim)


def left_shift(x, col):
    n = x.shape[1]
    return jnp.where(iota(x.shape, 1) == n - 1, col, pltpu.roll(x, n - 1, 1))


def right_shift(x, col):
    return jnp.where(iota(x.shape, 1) == 0, col, pltpu.roll(x, 1, 1))


def row_up(x, row):
    n = x.shape[0]
    return jnp.where(iota(x.shape, 0) == n - 1, row, pltpu.roll(x, n - 1, 0))


def row_down(x, row):
    return jnp.where(iota(x.shape, 0) == 0, row, pltpu.roll(x, 1, 0))


def section_sums(n0, dn, d0, dd):
    n1, d1 = n0 + dn, d0 + dd
    ns, ds = n0 + n1, d0 + d1
    ends = d0 * d1
    inv = 1.0 / (ends * ds)
    half = ns * ends * inv
    side = ds * inv
    last = n1 * d0 * side
    first = n0 * d1 * side
    return (first + last) * (1.0 / 6.0) + half * (2.0 / 3.0), half * (1.0 / 3.0) + last * (1.0 / 6.0)


def energy(w, v, vt):
    return w * (v * v + v * vt + vt * vt * (1.0 / 3.0))


(RH, RHT, RU0, RU0T, RU1, RU1T, RU2, RU2T, RH1, RH1T, RU01, RU01T) = range(12)
RGEO = 96
(LH, LHT, LU0, LU0T, LU1, LU1T, LU2, LU2T, LE1, LE2) = range(10)
LGEO = 80
(TH, THT, TH1, TH1T, TU0, TU0T, TU1, TU1T, TU11, TU11T, TU2, TU2T, TU21, TU21T, TE2) = range(15)
(BH, BHT, BH1, BH1T, BU0, BU0T, BU01, BU01T, BU1, BU1T, BU11, BU11T, BU2, BU2T, BE0) = range(15, 30)
RAW = 30


def pack_kernel(v, h, vt, ht, d, el, k, f, send_a, send_b, own0, raw):
    odd = lax.rem(lax.axis_index("px"), 2) == 1
    rows, cols = h.shape[1], h.shape[2]
    half = cols - 128
    lanes = iota((rows, 128), 1)
    to_left = jnp.zeros((rows, 128), F32)
    to_right = jnp.zeros((rows, 128), F32)
    first = [d[e, :, 0:128] for e in range(3)]
    last = [d[e, :, half:cols] for e in range(3)]
    weight = [0.25 * last[e] * el[e, :, half:cols] for e in range(3)]
    for lev in range(LV):
        low, high = [], []
        for x in (h, ht):
            low.append((x[lev, :, 0:128], 0))
        low = [(h[lev, :, 0:128], 0), (ht[lev, :, 0:128], 0)]
        high = [h[lev, :, half:cols], ht[lev, :, half:cols]]
        for e in range(3):
            for x in (v, vt):
                low.append((first[e] * x[e, lev, :, 0:128], 0))
                high.append(last[e] * x[e, lev, :, half:cols])
        low += [(low[0][0], 1), (low[1][0], 1), (low[2][0], 1), (low[3][0], 1)]
        for e in (1, 2):
            high.append(energy(weight[e], v[e, lev, :, half:cols], vt[e, lev, :, half:cols]))
        for n, (x, c) in enumerate(low):
            to_left = jnp.where(lanes == LV * n + lev, x[:, c : c + 1], to_left)
        for n, x in enumerate(high):
            to_right = jnp.where(lanes == LV * n + lev, x[:, 127:128], to_right)
    geo_low = [k[a, b, :, 0:128] for a in range(2) for b in range(3)]
    geo_high = [k[a, b, :, half:cols] for a in range(2) for b in range(3)]
    for a in range(2):
        geo_low.append((geo_low[3 * a] + geo_low[3 * a + 1] + geo_low[3 * a + 2]) * f[a, :, 0:128])
        geo_high.append((geo_high[3 * a] + geo_high[3 * a + 1] + geo_high[3 * a + 2]) * f[a, :, half:cols])
    for n in range(8):
        to_left = jnp.where(lanes == RGEO + n, geo_low[n][:, 0:1], to_left)
        to_right = jnp.where(lanes == LGEO + n, geo_high[n][:, 127:128], to_right)
    send_a[...] = jnp.where(odd, to_left, to_right)
    send_b[...] = jnp.where(odd, to_right, to_left)
    own0[...] = to_left

    end = rows - 1
    for x, n in ((h, TH), (ht, THT)):
        raw[n] = x[:, 0, :]
        raw[n + 2] = x[:, 1, :]
    for x, n in ((h, BH), (ht, BHT)):
        raw[n] = x[:, end, :]
        raw[n + 2] = x[:, end - 1, :]
    for x, t in ((v, 0), (vt, 1)):
        for e, r, n in (
            (0, 0, TU0),
            (1, 0, TU1),
            (1, 1, TU11),
            (2, 0, TU2),
            (2, 1, TU21),
            (0, end, BU0),
            (0, end - 1, BU01),
            (1, end, BU1),
            (1, end - 1, BU11),
            (2, end, BU2),
        ):
            raw[n + t] = d[e, r : r + 1, :] * x[e, :, r, :]
    raw[TE2] = energy(0.25 * d[2, 0:1, :] * el[2, 0:1, :], v[2, :, 0, :], vt[2, :, 0, :])
    raw[BE0] = energy(0.25 * d[0, end : end + 1, :] * el[0, end : end + 1, :], v[0, :, end, :], vt[0, :, end, :])


def af_row(k, f, a, r):
    return (k[a, 0, r : r + 1, :] + k[a, 1, r : r + 1, :] + k[a, 2, r : r + 1, :]) * f[a, r : r + 1, :]


def fld(t, n):
    return t[LV * n : LV * n + LV, :]


def column_left(lt, h0, h0t, u00, u00t):
    k = [lt[LGEO + n : LGEO + n + 1, :] for n in range(8)]
    up = lambda x: pltpu.roll(x, 127, 1)
    dn = lambda x: pltpu.roll(x, 1, 1)
    h, hp, u0, u0p, u1, u1p, u2, u2p = (fld(lt, n) for n in range(8))
    q0 = section_sums(
        k[6] + u0 - u1 + up(u2),
        u0p - u1p + up(u2p),
        k[0] * h + k[1] * up(h) + k[2] * h0,
        k[0] * hp + k[1] * up(hp) + k[2] * h0t,
    )
    q1 = section_sums(
        k[7] + u1 - u2 - dn(u00),
        u1p - u2p - dn(u00t),
        k[3] * h + k[4] * h0 + k[5] * dn(h0),
        k[3] * hp + k[4] * h0t + k[5] * dn(h0t),
    )
    return q0, q1


def column_right(rt):
    k = [rt[RGEO + n : RGEO + n + 1, :] for n in range(8)]
    up = lambda x: pltpu.roll(x, 127, 1)
    dn = lambda x: pltpu.roll(x, 1, 1)
    h, hp, u0, u0p, u1, u1p, u2, u2p, h1, h1p, u01, u01p = (fld(rt, n) for n in range(12))
    q0 = section_sums(
        k[6] + u0 - u1 + up(u2),
        u0p - u1p + up(u2p),
        k[0] * h + k[1] * up(h) + k[2] * h1,
        k[0] * hp + k[1] * up(hp) + k[2] * h1p,
    )
    q1 = section_sums(
        k[7] + u1 - u2 - dn(u01),
        u1p - u2p - dn(u01p),
        k[3] * h + k[4] * h1 + k[5] * dn(h1),
        k[3] * hp + k[4] * h1p + k[5] * dn(h1p),
    )
    return q0, q1


def lane_col(x, lane):
    return x[:, lane : lane + 1]


def merge_kernel(slab_a, slab_b, own0, raw, k, f, msg_a, msg_b, ext):
    odd_x = lax.rem(lax.axis_index("px"), 2) == 1
    odd_y = lax.rem(lax.axis_index("py"), 2) == 1
    rows = slab_a.shape[0]
    end = rows - 1
    left = jnp.where(odd_x, slab_a[...], slab_b[...])
    right = jnp.where(odd_x, slab_b[...], slab_a[...])
    ext[0, BASE : BASE + rows, :] = left
    ext[1, BASE : BASE + rows, :] = right
    ext[2, BASE : BASE + rows, :] = own0[...]
    lt, rt, ot = (jnp.transpose(ext[n]) for n in range(3))
    q0l, q1l = column_left(lt, fld(ot, RH), fld(ot, RHT), fld(ot, RU0), fld(ot, RU0T))
    q0r, q1r = column_right(rt)
    r0, r1 = BASE, BASE + 1
    e0, e1 = BASE + end, BASE + end - 1
    krow = lambda a, b, r: k[a, b, r : r + 1, :]

    h_0 = [left_shift(raw[TH + t], lane_col(fld(rt, RH + t), r0)) for t in range(2)]
    h_1 = [left_shift(raw[TH1 + t], lane_col(fld(rt, RH + t), r1)) for t in range(2)]
    u_0 = [left_shift(raw[TU0 + t], lane_col(fld(rt, RU0 + t), r0)) for t in range(2)]
    up0 = section_sums(
        af_row(k, f, 0, 0) + raw[TU0] - raw[TU1] + raw[TU21],
        raw[TU0T] - raw[TU1T] + raw[TU21T],
        *(krow(0, 0, 0) * raw[TH + t] + krow(0, 1, 0) * raw[TH1 + t] + krow(0, 2, 0) * h_0[t] for t in range(2)),
    )
    up1 = section_sums(
        af_row(k, f, 1, 1) + raw[TU11] - raw[TU21] - u_0[0],
        raw[TU11T] - raw[TU21T] - u_0[1],
        *(krow(1, 0, 1) * raw[TH1 + t] + krow(1, 1, 1) * h_1[t] + krow(1, 2, 1) * h_0[t] for t in range(2)),
    )
    up = [
        up0[t] + right_shift(up0[t] + up1[t], lane_col(q0l[t], r0) + lane_col(q1l[t], r1)) for t in range(2)
    ]

    hb_0 = [left_shift(raw[BH + t], lane_col(fld(rt, RH + t), e0)) for t in range(2)]
    hb_1 = [left_shift(raw[BH1 + t], lane_col(fld(rt, RH + t), e1)) for t in range(2)]
    ub_1 = [left_shift(raw[BU01 + t], lane_col(fld(rt, RU0 + t), e1)) for t in range(2)]
    dn1 = section_sums(
        af_row(k, f, 1, end) + raw[BU1] - raw[BU2] - ub_1[0],
        raw[BU1T] - raw[BU2T] - ub_1[1],
        *(krow(1, 0, end) * raw[BH + t] + krow(1, 1, end) * hb_0[t] + krow(1, 2, end) * hb_1[t] for t in range(2)),
    )
    dn0 = section_sums(
        af_row(k, f, 0, end - 1) + raw[BU01] - raw[BU11] + raw[BU2],
        raw[BU01T] - raw[BU11T] + raw[BU2T],
        *(
            krow(0, 0, end - 1) * raw[BH1 + t] + krow(0, 1, end - 1) * raw[BH + t] + krow(0, 2, end - 1) * hb_1[t]
            for t in range(2)
        ),
    )
    down = [
        left_shift(dn1[t] + dn0[t], lane_col(q1r[t], e0) + lane_col(q0r[t], e1)) + dn1[t] for t in range(2)
    ]

    def store(msg_up, msg_down):
        for msg, sums, parts, geo, r in (
            (msg_up, up, (TH, THT, TU1, TU1T, TU2, TU2T, TE2), 1, 0),
            (msg_down, down, (BH, BHT, BU0, BU0T, BU1, BU1T, BE0), 0, end),
        ):
            for n in range(2):
                msg[LV * n : LV * n + LV, :] = sums[n]
            for n, part in enumerate(parts):
                msg[LV * (n + 2) : LV * (n + 3), :] = raw[part]
            for n in range(3):
                msg[72 + n : 73 + n, :] = krow(geo, n, r)
            msg[75:76, :] = af_row(k, f, geo, r)
            msg[76:77, 0:128] = left[r : r + 1, :]
            msg[76:77, 128:256] = right[r : r + 1, :]

    @pl.when(odd_y)
    def _():
        store(msg_a, msg_b)

    @pl.when(jnp.logical_not(odd_y))
    def _():
        store(msg_b, msg_a)


(
    WHB, WHBT, WUB, WUBT, WHA, WHAT, WUA, WUAT,
    WQB, WQBT, WQA, WQAT, WMA, WMAT, WMB, WMBT, WEB, WEA,
) = range(18)
(CY, CYT, CQ, CZ, CP, CPT) = range(6)


def main_kernel(
    v, h, vt, ht, d, el, area, k, f, slab_a, slab_b, own0, raw, msg_a, msg_b,
    vertex, kinetic, cell, edge, ext, msgs, halo, geo,
):
    odd_x = lax.rem(lax.axis_index("px"), 2) == 1
    odd_y = lax.rem(lax.axis_index("py"), 2) == 1
    rows, cols = h.shape[1], h.shape[2]
    end = rows - 1

    @pl.when(odd_y)
    def _():
        msgs[0] = msg_b[...]
        msgs[1] = msg_a[...]

    @pl.when(jnp.logical_not(odd_y))
    def _():
        msgs[0] = msg_a[...]
        msgs[1] = msg_b[...]

    above = lambda n: msgs[0, LV * n : LV * n + LV, :]
    below = lambda n: msgs[1, LV * n : LV * n + LV, :]
    ka = [msgs[0, 72 + n : 73 + n, :] for n in range(4)]
    kb = [msgs[1, 72 + n : 73 + n, :] for n in range(4)]

    left = jnp.where(odd_x, slab_a[...], slab_b[...])
    right = jnp.where(odd_x, slab_b[...], slab_a[...])
    ext[0, BASE : BASE + rows, :] = left
    ext[1, BASE : BASE + rows, :] = right
    ext[2, BASE : BASE + rows, :] = own0[...]
    ext[0, DNB : DNB + 1, :] = msgs[0, 76:77, 0:128]
    ext[1, DNB : DNB + 1, :] = msgs[0, 76:77, 128:256]
    ext[1, UPB : UPB + 1, :] = msgs[1, 76:77, 128:256]
    lt, rt, ot = (jnp.transpose(ext[n]) for n in range(3))
    lanes = iota((LV, 128), 1)
    low = lambda x, row: jnp.where(lanes == UPB, row[:, 0:1], x)
    high = lambda x, row: jnp.where(lanes == DNB, row[:, 0:1], x)
    h0 = [high(low(fld(ot, RH + t), below(2 + t)), above(2 + t)) for t in range(2)]
    u00 = [low(fld(ot, RU0 + t), below(4 + t)) for t in range(2)]
    q0l, q1l = column_left(lt, *h0, *u00)
    q0r, q1r = column_right(rt)
    up = lambda x: pltpu.roll(x, 127, 1)
    dn = lambda x: pltpu.roll(x, 1, 1)
    z = fld(lt, LE1) + up(fld(lt, LE2))
    cols_out = [
        q0l[0] + q1l[0] + up(q1l[0]),
        q0l[1] + q1l[1] + up(q1l[1]),
        up(q1l[0]),
        z,
        q0r[0] + q1r[0] + dn(q0r[0]),
        q0r[1] + q1r[1] + dn(q0r[1]),
    ]
    packed = jnp.concatenate(cols_out + [jnp.zeros((128 - LV * len(cols_out), 128), F32)], axis=0)
    inject = jnp.transpose(packed)[BASE : BASE + rows, :]

    hb1 = [left_shift(below(2 + t), lane_col(fld(rt, RH + t), UPB)) for t in range(2)]
    ub1 = [left_shift(below(4 + t), lane_col(fld(rt, RU0 + t), UPB)) for t in range(2)]
    qb = section_sums(
        kb[3] + below(4) - below(6) + raw[TU2],
        below(5) - below(7) + raw[TU2T],
        *(kb[0] * below(2 + t) + kb[1] * raw[TH + t] + kb[2] * hb1[t] for t in range(2)),
    )
    ha1 = [left_shift(above(2 + t), lane_col(fld(rt, RH + t), DNB)) for t in range(2)]
    he1 = [left_shift(raw[BH + t], lane_col(fld(rt, RH + t), BASE + end)) for t in range(2)]
    ue1 = [left_shift(raw[BU0 + t], lane_col(fld(rt, RU0 + t), BASE + end)) for t in range(2)]
    qa = section_sums(
        ka[3] + above(4) - above(6) - ue1[0],
        above(5) - above(7) - ue1[1],
        *(ka[0] * above(2 + t) + ka[1] * ha1[t] + ka[2] * he1[t] for t in range(2)),
    )
    for t in range(2):
        halo[WHB + t] = hb1[t]
        halo[WUB + t] = ub1[t]
        halo[WHA + t] = above(2 + t)
        halo[WUA + t] = above(6 + t)
        halo[WQB + t] = qb[t]
        halo[WQA + t] = qa[t]
        halo[WMA + t] = above(t) + qa[t] + right_shift(qa[t], lane_col(q1l[t], DNB))
        halo[WMB + t] = below(t) + qb[t] + left_shift(qb[t], lane_col(q0r[t], UPB))
    halo[WEB] = below(8)
    halo[WEA] = above(8)

    for a in range(2):
        geo[a] = (k[a, 0] + k[a, 1] + k[a, 2]) * f[a]
    for e in range(3):
        geo[2 + e] = (1.0 / 12.0) / d[e]
        geo[5 + e] = 0.25 * d[e] * el[e]
    geo[8] = 1.0 / area[...]

    for lev in range(LV):
        row = lambda n, lev=lev: halo[n, lev : lev + 1, :]
        col = lambda n, lev=lev: inject[:, LV * n + lev : LV * n + lev + 1]
        rcol = lambda n, lev=lev: right[:, LV * n + lev : LV * n + lev + 1]
        hh = [x[lev] for x in (h, ht)]
        u = [[d[e] * x[e, lev] for x in (v, vt)] for e in range(3)]
        h1 = [left_shift(hh[t], rcol(RH + t)) for t in range(2)]
        u01 = [left_shift(u[0][t], rcol(RU0 + t)) for t in range(2)]
        n0 = [u[0][t] - u[1][t] + row_up(u[2][t], row(WUA + t)) for t in range(2)]
        n1 = [u[1][t] - u[2][t] - row_down(u01[t], row(WUB + t)) for t in range(2)]
        d0 = [k[0, 0] * hh[t] + k[0, 1] * row_up(hh[t], row(WHA + t)) + k[0, 2] * h1[t] for t in range(2)]
        d1 = [k[1, 0] * hh[t] + k[1, 1] * h1[t] + k[1, 2] * row_down(h1[t], row(WHB + t)) for t in range(2)]
        q0 = section_sums(geo[0] + n0[0], n0[1], *d0)
        q1 = section_sums(geo[1] + n1[0], n1[1], *d1)
        vertex[0, lev] = q0[0]
        vertex[1, lev] = q1[0]
        grads = []
        for t in range(2):
            q0d = row_down(q0[t], row(WQB + t))
            q1u = row_up(q1[t], row(WQA + t))
            both = q0[t] + q1[t]
            p, y = both + q0d, both + q1u
            m = p + right_shift(y, col(CY + t))
            m1 = left_shift(p, col(CP + t)) + y
            grads.append(
                (
                    row_up(m, row(WMA + t) + q0[t]) - m,
                    m1 - m,
                    row_down(m1, row(WMB + t) + q1[t]) - m,
                )
            )
            if t == 0:
                cell[lev] = m * (1.0 / 6.0)
                means = (q0[0] + right_shift(q1u, col(CQ)), both, q1[0] + q0d)
        for e in range(3):
            edge[e, lev] = 0.5 * means[e] - geo[2 + e] * (v[e, lev] * grads[0][e] + vt[e, lev] * grads[1][e])
        en = [energy(geo[5 + e], v[e, lev], vt[e, lev]) for e in range(3)]
        zz = en[1] + row_up(en[2], row(WEA))
        kinetic[lev] = (
            en[0] + en[1] + en[2] + row_down(en[0], row(WEB)) + right_shift(zz, col(CZ))
        ) * geo[8]


def swap(x, axis, start):
    n = lax.axis_size(axis)
    pairs = []
    for i in range(start, n + start, 2):
        a, b = i % n, (i + 1) % n
        pairs += [(a, b), (b, a)]
    return lax.ppermute(x, axis, pairs)


def call(kernel, outs, scratch, *args):
    vmem = pl.BlockSpec(memory_space=pltpu.VMEM)
    return pl.pallas_call(
        kernel,
        out_shape=[jax.ShapeDtypeStruct(s, F32) for s in outs],
        in_specs=[vmem] * len(args),
        out_specs=[vmem] * len(outs),
        scratch_shapes=[pltpu.VMEM(s, F32) for s in scratch],
    )(*args)


def local(v, h, vt, ht, d, el, area, k, f):
    levels, rows, cols = h.shape
    slab = (rows, 128)
    send_a, send_b, own0, raw = call(
        pack_kernel, [slab, slab, slab, (RAW, levels, cols)], [], v, h, vt, ht, d, el, k, f
    )
    slab_a = swap(send_a, "px", 0)
    slab_b = swap(send_b, "px", 1)
    msg_a, msg_b = call(
        merge_kernel, [(80, cols), (80, cols)], [(3, 128, 128)], slab_a, slab_b, own0, raw, k, f
    )
    msg_a = swap(msg_a, "py", 0)
    msg_b = swap(msg_b, "py", 1)
    return tuple(
        call(
            main_kernel,
            [(2, levels, rows, cols), (levels, rows, cols), (levels, rows, cols), (3, levels, rows, cols)],
            [(3, 128, 128), (2, 80, cols), (18, levels, cols), (9, rows, cols)],
            v, h, vt, ht, d, el, area, k, f, slab_a, slab_b, own0, raw, msg_a, msg_b,
        )
    )


def solution(mesh):
    field = P(None, "py", "px")
    pair = P(None, None, "py", "px")
    return jax.shard_map(
        local,
        mesh=mesh,
        in_specs=(pair, field, pair, field, field, field, P("py", "px"), pair, field),
        out_specs=(pair, field, field, pair),
        check_vma=False,
    )
```

time: 80.2 us -> 29.6 us (0.37)
  other arithmetic: 34.3 us -> 0 us
  starting transfers between devices: 20.2 us -> 8.83 us
  Pallas kernels: 0 us -> 10.9 us
  waiting for transfers between devices: 15.7 us -> 7.52 us
  local copies, waits for them, and re-layouts: 8.22 us -> 1.23 us
    concatenate x6 -> x0, other arithmetic: 13 us -> none  [the longest x3 8.24 us: with_halo(): jnp.concatenate([lax.ppermute(tail, axis, [(i, (i + 1) % count) for i in...]
    ppermute x12 -> x4, starting transfers between devices: 20.2 us -> 8.83 us  [swap(): return lax.ppermute(x, axis, pairs)]
    pallas_call x0 -> x3, Pallas kernels: none -> 10.9 us  [call(): pl.pallas_call(kernel, out_shape=[jax.ShapeDtypeStruct(s, F32) for s in o...]
    ppermute x12 -> x4, waiting for transfers between devices: 15.7 us -> 7.52 us  [swap(): return lax.ppermute(x, axis, pairs)]
    div x8 -> x0, other arithmetic: 7.43 us -> none  [the longest x2 2.66 us: local(): (coriolis_used[0] + circulation_first / triangle_area[0]) / height_first]
    add x5 -> x0, other arithmetic: 5.6 us -> none  [the longest x1 2 us: local(): energy_total = energy_total + weight_now * kinetic]
    slice x3 -> x0, other arithmetic: 3.5 us -> none  [with_halo(): lax.slice_in_dim(cells, cells.shape[dim] - width, cells.shape[dim], axis=...]
    ppermute x2 -> x0, local copies, waits for them, and re-layouts: 2.75 us -> none  [the longest x1 1.76 us: with_halo(): lax.ppermute(head, axis, [((i + 1) % count, i) for i in range(count)])]
  transfers between devices with their start and end apart: 12 -> 4, of which waited for: 4 -> 2; matrix products, arithmetic and copies ran while one was open for 16% -> 0% of each run, Pallas kernels for 0% -> 0%
where the time goes in v1:
time: 29.6 us; the launch traced here: 29.1 us
  Pallas kernels  10.9 us (37%)
  starting transfers between devices  8.83 us (30%)
  waiting for transfers between devices  7.52 us (25%)
  local copies, waits for them, and re-layouts  1.23 us (4%)
  between operations  0.64 us (2%)
    pallas_call x3, Pallas kernels, call(): pl.pallas_call(kernel, out_shape=[jax.ShapeDtypeStruct(s, F32) for s in o...  10.9 us
    ppermute x4, starting transfers between devices, swap(): return lax.ppermute(x, axis, pairs)  8.83 us
    ppermute x4, waiting for transfers between devices, swap(): return lax.ppermute(x, axis, pairs)  7.52 us
    unnamed x8, local copies, waits for them, and re-layouts  1.23 us
  transfers between devices with their start and end apart: 4, of which 2 were waited for; matrix products, arithmetic and copies ran while one was open for 0% of the time, Pallas kernels for 0%

profile of v1, /device:TPU:25, one launch (start us, length us, event | category | flops | bytes accessed | tf_op | source)
XLA Modules:
  0.0 29.1 jit_solution(3832708428888624781)
XLA Ops:
  0.6 3.3 %shard_map.120 = (f32[32,128]{1,0:T(8,128)}, f32[32,128]{1,0:T(8,128)}, f32[32,128]{1,0:T(8,128)}, f32[30,8,256]{2,1,0:T(8,128)}) custom-call(f32[3,8,32,256]{3,2,1,0:T(8,128)} %v.3, f32[8,32,256]{2,1,0:T(8,128)} %h.3, f32[3,8,32,256]{3,2,1,0:T(8,128)} %vt.3, f32[8,32,256]{2,1,0:T(8,128)} %ht.3, f32[3,32,256]{2,1,0:T(8,128)} %d.3, f32[3,32,256]{2,1,0:T(8,128)} %el.3, ...), custom_call_target="tpu_custom_call" | custom-call | tf_op jit(solution)/shard_map/pallas_call | solution.py:404
  3.9 1.6 %collective-permute-start = (f32[32,128]{1,0:T(8,128)}, f32[32,128]{1,0:T(8,128)S(1)}, u32[]{:S(2)}, u32[]{:S(2)}) collective-permute-start(f32[32,128]{1,0:T(8,128)} %get-tuple-element.10), channel_id=1, source_target_pairs={{0,16},{16,0},{32,48},{48,32},{64,80},{80,64},{96,112},{112,96},{1... | collective-permute-start | bytes 49160 | tf_op jit(solution)/shard_map/ppermute | solution.py:399
  5.6 2.2 %collective-permute-start.1 = (f32[32,128]{1,0:T(8,128)}, f32[32,128]{1,0:T(8,128)S(1)}, u32[]{:S(2)}, u32[]{:S(2)}) collective-permute-start(f32[32,128]{1,0:T(8,128)} %get-tuple-element.11), channel_id=1, source_target_pairs={{16,32},{32,16},{48,64},{64,48},{80,96},{96,80},{112,0},{0,112},{1... | collective-permute-start | bytes 49160 | tf_op jit(solution)/shard_map/ppermute | solution.py:399
  7.8 0.0 collective-permute-done.slab_a
  7.8 0.0 copy-start.2
  7.8 2.7 %collective-permute-done.1.slab_b = f32[32,128]{1,0:T(8,128)S(1)} collective-permute-done((f32[32,128]{1,0:T(8,128)}, f32[32,128]{1,0:T(8,128)S(1)}, u32[]{:S(2)}, u32[]{:S(2)}) %collective-permute-start.1) | collective-permute-done | bytes 16416 | tf_op jit(solution)/shard_map/ppermute | solution.py:399
  10.5 0.0 copy-start.3
  10.5 0.0 copy-done.2
  10.5 0.6 %copy-done.3 = f32[32,128]{1,0:T(8,128)} copy-done((f32[32,128]{1,0:T(8,128)}, f32[32,128]{1,0:T(8,128)S(1)}, u32[]{:S(2)}) %copy-start.3) | copy-done | bytes 16408
  11.1 2.1 %shard_map.121 = (f32[80,256]{1,0:T(8,128)}, f32[80,256]{1,0:T(8,128)}) custom-call(f32[32,128]{1,0:T(8,128)} %copy-done.2, f32[32,128]{1,0:T(8,128)} %copy-done.3, f32[32,128]{1,0:T(8,128)} %get-tuple-element.12.own0, f32[30,8,256]{2,1,0:T(8,128)} %get-tuple-element.13.raw, f32[2,3,32,256]{3,2,1,0:T(8,128)} %k.5, f32[2,32,256]{2,1,0:T(8,128)} %f.5), custom_call_target="tpu_custom_call" | custom-call | tf_op jit(solution)/shard_map/pallas_call | solution.py:404
  13.2 2.1 %collective-permute-start.2 = (f32[80,256]{1,0:T(8,128)}, f32[80,256]{1,0:T(8,128)S(1)}, u32[]{:S(2)}, u32[]{:S(2)}) collective-permute-start(f32[80,256]{1,0:T(8,128)} %get-tuple-element.14), channel_id=1, source_target_pairs={{0,1},{1,0},{2,3},{3,2},{4,5},{5,4},{6,7},{7,6},{8,9},{9,8},{10,11... | collective-permute-start | bytes 245768 | tf_op jit(solution)/shard_map/ppermute | solution.py:399
  15.3 2.8 %collective-permute-start.3 = (f32[80,256]{1,0:T(8,128)}, f32[80,256]{1,0:T(8,128)S(1)}, u32[]{:S(2)}, u32[]{:S(2)}) collective-permute-start(f32[80,256]{1,0:T(8,128)} %get-tuple-element.15), channel_id=1, source_target_pairs={{1,2},{2,1},{3,4},{4,3},{5,6},{6,5},{7,8},{8,7},{9,10},{10,9},{11,... | collective-permute-start | bytes 245768 | tf_op jit(solution)/shard_map/ppermute | solution.py:399
  18.2 0.0 collective-permute-done.2.msg_a
  18.2 0.0 copy-start
  18.2 4.8 %collective-permute-done.3.msg_b = f32[80,256]{1,0:T(8,128)S(1)} collective-permute-done((f32[80,256]{1,0:T(8,128)}, f32[80,256]{1,0:T(8,128)S(1)}, u32[]{:S(2)}, u32[]{:S(2)}) %collective-permute-start.3) | collective-permute-done | bytes 81952 | tf_op jit(solution)/shard_map/ppermute | solution.py:399
  23.0 0.0 copy-done
  23.0 0.0 copy-start.1
  23.0 0.6 %copy-done.1 = f32[80,256]{1,0:T(8,128)} copy-done((f32[80,256]{1,0:T(8,128)}, f32[80,256]{1,0:T(8,128)S(1)}, u32[]{:S(2)}) %copy-start.1) | copy-done | bytes 81944
  23.6 5.5 %shard_map.122 = (f32[2,8,32,256]{3,2,1,0:T(8,128)}, f32[8,32,256]{2,1,0:T(8,128)}, f32[8,32,256]{2,1,0:T(8,128)}, f32[3,8,32,256]{3,2,1,0:T(8,128)}) custom-call(f32[3,8,32,256]{3,2,1,0:T(8,128)} %v.3, f32[8,32,256]{2,1,0:T(8,128)} %h.3, f32[3,8,32,256]{3,2,1,0:T(8,128)} %vt.3, f32[8,32,256]{2,1,0:T(8,128)} %ht.3, f32[3,32,256]{2,1,0:T(8,128)} %d.3, ...), custom_call_target="tpu_custom_call" | custom-call | tf_op jit(solution)/shard_map/pallas_call | solution.py:404
Async XLA Ops:
  3.9 3.9 %collective-permute-start = (f32[32,128]{1,0:T(8,128)}, f32[32,128]{1,0:T(8,128)S(1)}, u32[]{:S(2)}, u32[]{:S(2)}) collective-permute-start(f32[32,128]{1,0:T(8,128)} %get-tuple-element.10), channel_id=1, source_target_pairs={{0,16},{16,0},{32,48},{48,32},{64,80},{80,64},{96,112},{112,96},{1... | collective-permute-start | bytes 49160 | tf_op jit(solution)/shard_map/ppermute | solution.py:399
  5.6 4.9 %collective-permute-start.1 = (f32[32,128]{1,0:T(8,128)}, f32[32,128]{1,0:T(8,128)S(1)}, u32[]{:S(2)}, u32[]{:S(2)}) collective-permute-start(f32[32,128]{1,0:T(8,128)} %get-tuple-element.11), channel_id=1, source_target_pairs={{16,32},{32,16},{48,64},{64,48},{80,96},{96,80},{112,0},{0,112},{1... | collective-permute-start | bytes 49160 | tf_op jit(solution)/shard_map/ppermute | solution.py:399
  7.8 2.7 %copy-start.2 = (f32[32,128]{1,0:T(8,128)}, f32[32,128]{1,0:T(8,128)S(1)}, u32[]{:S(2)}) copy-start(f32[32,128]{1,0:T(8,128)S(1)} %collective-permute-done.slab_a) | copy-start | bytes 49156
  10.5 0.6 %copy-start.3 = (f32[32,128]{1,0:T(8,128)}, f32[32,128]{1,0:T(8,128)S(1)}, u32[]{:S(2)}) copy-start(f32[32,128]{1,0:T(8,128)S(1)} %collective-permute-done.1.slab_b) | copy-start | bytes 49156
  13.2 5.0 %collective-permute-start.2 = (f32[80,256]{1,0:T(8,128)}, f32[80,256]{1,0:T(8,128)S(1)}, u32[]{:S(2)}, u32[]{:S(2)}) collective-permute-start(f32[80,256]{1,0:T(8,128)} %get-tuple-element.14), channel_id=1, source_target_pairs={{0,1},{1,0},{2,3},{3,2},{4,5},{5,4},{6,7},{7,6},{8,9},{9,8},{10,11... | collective-permute-start | bytes 245768 | tf_op jit(solution)/shard_map/ppermute | solution.py:399
  15.3 7.7 %collective-permute-start.3 = (f32[80,256]{1,0:T(8,128)}, f32[80,256]{1,0:T(8,128)S(1)}, u32[]{:S(2)}, u32[]{:S(2)}) collective-permute-start(f32[80,256]{1,0:T(8,128)} %get-tuple-element.15), channel_id=1, source_target_pairs={{1,2},{2,1},{3,4},{4,3},{5,6},{6,5},{7,8},{8,7},{9,10},{10,9},{11,... | collective-permute-start | bytes 245768 | tf_op jit(solution)/shard_map/ppermute | solution.py:399
  18.2 4.8 %copy-start = (f32[80,256]{1,0:T(8,128)}, f32[80,256]{1,0:T(8,128)S(1)}, u32[]{:S(2)}) copy-start(f32[80,256]{1,0:T(8,128)S(1)} %collective-permute-done.2.msg_a) | copy-start | bytes 245764
  23.0 0.6 %copy-start.1 = (f32[80,256]{1,0:T(8,128)}, f32[80,256]{1,0:T(8,128)S(1)}, u32[]{:S(2)}) copy-start(f32[80,256]{1,0:T(8,128)S(1)} %collective-permute-done.3.msg_b) | copy-start | bytes 245764

commit v2 on v1

--- a/solution.py
+++ b/solution.py
@@ -58,46 +58,71 @@
 RAW = 30
 
 
-def pack_kernel(v, h, vt, ht, d, el, k, f, send_a, send_b, own0, raw):
+def pack_kernel(
+    v, h, vt, ht, d, el, area, k, f, send_a, send_b, own0, vo, ho, vto, hto, do, eo, ao, ko, fo, sems
+):
     odd = lax.rem(lax.axis_index("px"), 2) == 1
     rows, cols = h.shape[1], h.shape[2]
     half = cols - 128
+    started = []
+
+    def start(src, dst):
+        copy = pltpu.make_async_copy(src, dst, sems.at[len(started)])
+        copy.start()
+        started.append(copy)
+        return copy
+
+    fixed = [start(x, y) for x, y in ((d, do), (el, eo), (k, ko), (f, fo))]
+    by_level = [
+        [start(x.at[lev], y.at[lev]) for x, y in ((h, ho), (ht, hto))]
+        + [start(x.at[:, lev], y.at[:, lev]) for x, y in ((v, vo), (vt, vto))]
+        for lev in range(LV)
+    ]
+    area_copy = start(area, ao)
+    for copy in fixed:
+        copy.wait()
+
     lanes = iota((rows, 128), 1)
     to_left = jnp.zeros((rows, 128), F32)
     to_right = jnp.zeros((rows, 128), F32)
-    first = [d[e, :, 0:128] for e in range(3)]
-    last = [d[e, :, half:cols] for e in range(3)]
-    weight = [0.25 * last[e] * el[e, :, half:cols] for e in range(3)]
+    geo_low = [ko[a, b, :, 0:128] for a in range(2) for b in range(3)]
+    geo_high = [ko[a, b, :, half:cols] for a in range(2) for b in range(3)]
+    for a in range(2):
+        geo_low.append((geo_low[3 * a] + geo_low[3 * a + 1] + geo_low[3 * a + 2]) * fo[a, :, 0:128])
+        geo_high.append((geo_high[3 * a] + geo_high[3 * a + 1] + geo_high[3 * a + 2]) * fo[a, :, half:cols])
+    for n in range(8):
+        to_left = jnp.where(lanes == RGEO + n, geo_low[n][:, 0:1], to_left)
+        to_right = jnp.where(lanes == LGEO + n, geo_high[n][:, 127:128], to_right)
+    first = [do[e, :, 0:128] for e in range(3)]
+    last = [do[e, :, half:cols] for e in range(3)]
+    weight = [0.25 * last[e] * eo[e, :, half:cols] for e in range(3)]
     for lev in range(LV):
-        low, high = [], []
-        for x in (h, ht):
-            low.append((x[lev, :, 0:128], 0))
-        low = [(h[lev, :, 0:128], 0), (ht[lev, :, 0:128], 0)]
-        high = [h[lev, :, half:cols], ht[lev, :, half:cols]]
+        for copy in by_level[lev]:
+            copy.wait()
+        low = [(ho[lev, :, 0:128], 0), (hto[lev, :, 0:128], 0)]
+        high = [ho[lev, :, half:cols], hto[lev, :, half:cols]]
         for e in range(3):
-            for x in (v, vt):
+            for x in (vo, vto):
                 low.append((first[e] * x[e, lev, :, 0:128], 0))
                 high.append(last[e] * x[e, lev, :, half:cols])
-        low += [(low[0][0], 1), (low[1][0], 1), (low[2][0], 1), (low[3][0], 1)]
+        low += [(x, 1) for x, _ in low[:4]]
         for e in (1, 2):
-            high.append(energy(weight[e], v[e, lev, :, half:cols], vt[e, lev, :, half:cols]))
+            high.append(energy(weight[e], vo[e, lev, :, half:cols], vto[e, lev, :, half:cols]))
         for n, (x, c) in enumerate(low):
             to_left = jnp.where(lanes == LV * n + lev, x[:, c : c + 1], to_left)
         for n, x in enumerate(high):
             to_right = jnp.where(lanes == LV * n + lev, x[:, 127:128], to_right)
-    geo_low = [k[a, b, :, 0:128] for a in range(2) for b in range(3)]
-    geo_high = [k[a, b, :, half:cols] for a in range(2) for b in range(3)]
-    for a in range(2):
-        geo_low.append((geo_low[3 * a] + geo_low[3 * a + 1] + geo_low[3 * a + 2]) * f[a, :, 0:128])
-        geo_high.append((geo_high[3 * a] + geo_high[3 * a + 1] + geo_high[3 * a + 2]) * f[a, :, half:cols])
-    for n in range(8):
-        to_left = jnp.where(lanes == RGEO + n, geo_low[n][:, 0:1], to_left)
-        to_right = jnp.where(lanes == LGEO + n, geo_high[n][:, 127:128], to_right)
     send_a[...] = jnp.where(odd, to_left, to_right)
     send_b[...] = jnp.where(odd, to_right, to_left)
     own0[...] = to_left
-
-    end = rows - 1
+    area_copy.wait()
+
+
+PACK_COPIES = 4 + 4 * LV + 1
+
+
+def prep_kernel(v, h, vt, ht, d, el, area, k, f, raw, geo):
+    end = h.shape[1] - 1
     for x, n in ((h, TH), (ht, THT)):
         raw[n] = x[:, 0, :]
         raw[n + 2] = x[:, 1, :]
@@ -120,6 +145,12 @@
             raw[n + t] = d[e, r : r + 1, :] * x[e, :, r, :]
     raw[TE2] = energy(0.25 * d[2, 0:1, :] * el[2, 0:1, :], v[2, :, 0, :], vt[2, :, 0, :])
     raw[BE0] = energy(0.25 * d[0, end : end + 1, :] * el[0, end : end + 1, :], v[0, :, end, :], vt[0, :, end, :])
+    for a in range(2):
+        geo[a] = (k[a, 0] + k[a, 1] + k[a, 2]) * f[a]
+    for e in range(3):
+        geo[2 + e] = (1.0 / 12.0) / d[e]
+        geo[5 + e] = 0.25 * d[e] * el[e]
+    geo[8] = 1.0 / area[...]
 
 
 def af_row(k, f, a, r):
@@ -252,20 +283,45 @@
         store(msg_b, msg_a)
 
 
-(
-    WHB, WHBT, WUB, WUBT, WHA, WHAT, WUA, WUAT,
-    WQB, WQBT, WQA, WQAT, WMA, WMAT, WMB, WMBT, WEB, WEA,
-) = range(18)
-(CY, CYT, CQ, CZ, CP, CPT) = range(6)
-
-
-def main_kernel(
-    v, h, vt, ht, d, el, area, k, f, slab_a, slab_b, own0, raw, msg_a, msg_b,
-    vertex, kinetic, cell, edge, ext, msgs, halo, geo,
+(WQB, WQBT, WQA, WQAT, WMA, WMAT, WMB, WMBT, WE0, WE0T, WF1, WF1T, WEB, WEA) = range(14)
+(CY, CYT, CQ, CP, CPT) = range(5)
+
+
+def vertex_kernel(v, h, vt, ht, d, k, geo, slab_a, slab_b, q, kin):
+    odd_x = lax.rem(lax.axis_index("px"), 2) == 1
+    left = jnp.where(odd_x, slab_a[...], slab_b[...])
+    right = jnp.where(odd_x, slab_b[...], slab_a[...])
+    z = left + row_up(pltpu.roll(left, 128 - LV, 1), 0.0)
+    for lev in range(LV):
+        rcol = lambda n, lev=lev: right[:, LV * n + lev : LV * n + lev + 1]
+        hh = [x[lev] for x in (h, ht)]
+        u = [[d[e] * x[e, lev] for x in (v, vt)] for e in range(3)]
+        h1 = [left_shift(hh[t], rcol(RH + t)) for t in range(2)]
+        u01 = [left_shift(u[0][t], rcol(RU0 + t)) for t in range(2)]
+        up = lambda x: pltpu.roll(x, x.shape[0] - 1, 0)
+        dn = lambda x: pltpu.roll(x, 1, 0)
+        n0 = [u[0][t] - u[1][t] + up(u[2][t]) for t in range(2)]
+        n1 = [u[1][t] - u[2][t] - dn(u01[t]) for t in range(2)]
+        d0 = [k[0, 0] * hh[t] + k[0, 1] * up(hh[t]) + k[0, 2] * h1[t] for t in range(2)]
+        d1 = [k[1, 0] * hh[t] + k[1, 1] * h1[t] + k[1, 2] * dn(h1[t]) for t in range(2)]
+        q0 = section_sums(geo[0] + n0[0], n0[1], *d0)
+        q1 = section_sums(geo[1] + n1[0], n1[1], *d1)
+        for t in range(2):
+            q[t, 0, lev] = q0[t]
+            q[t, 1, lev] = q1[t]
+        en = [energy(geo[5 + e], v[e, lev], vt[e, lev]) for e in range(3)]
+        zz = en[1] + row_up(en[2], 0.0)
+        zcol = z[:, LV * LE1 + lev : LV * LE1 + lev + 1]
+        kin[lev] = en[0] + en[1] + en[2] + row_down(en[0], 0.0) + right_shift(zz, zcol)
+
+
+def last_kernel(
+    v, vt, k, f, geo, slab_a, slab_b, own0, raw, q, kin, msg_a, msg_b,
+    vertex, kinetic, cell, edge, ext, msgs, halo, vertex_v, kinetic_v, cell_v, edge_v, sems,
 ):
     odd_x = lax.rem(lax.axis_index("px"), 2) == 1
     odd_y = lax.rem(lax.axis_index("py"), 2) == 1
-    rows, cols = h.shape[1], h.shape[2]
+    rows = kin.shape[1]
     end = rows - 1
 
     @pl.when(odd_y)
@@ -282,6 +338,7 @@
     below = lambda n: msgs[1, LV * n : LV * n + LV, :]
     ka = [msgs[0, 72 + n : 73 + n, :] for n in range(4)]
     kb = [msgs[1, 72 + n : 73 + n, :] for n in range(4)]
+    krow = lambda a, b, r: k[a, b, r : r + 1, :]
 
     left = jnp.where(odd_x, slab_a[...], slab_b[...])
     right = jnp.where(odd_x, slab_b[...], slab_a[...])
@@ -301,12 +358,10 @@
     q0r, q1r = column_right(rt)
     up = lambda x: pltpu.roll(x, 127, 1)
     dn = lambda x: pltpu.roll(x, 1, 1)
-    z = fld(lt, LE1) + up(fld(lt, LE2))
     cols_out = [
         q0l[0] + q1l[0] + up(q1l[0]),
         q0l[1] + q1l[1] + up(q1l[1]),
         up(q1l[0]),
-        z,
         q0r[0] + q1r[0] + dn(q0r[0]),
         q0r[1] + q1r[1] + dn(q0r[1]),
     ]
@@ -315,10 +370,16 @@
 
     hb1 = [left_shift(below(2 + t), lane_col(fld(rt, RH + t), UPB)) for t in range(2)]
     ub1 = [left_shift(below(4 + t), lane_col(fld(rt, RU0 + t), UPB)) for t in range(2)]
+    h01 = [left_shift(raw[TH + t], lane_col(fld(rt, RH + t), BASE)) for t in range(2)]
     qb = section_sums(
         kb[3] + below(4) - below(6) + raw[TU2],
         below(5) - below(7) + raw[TU2T],
         *(kb[0] * below(2 + t) + kb[1] * raw[TH + t] + kb[2] * hb1[t] for t in range(2)),
+    )
+    q1f = section_sums(
+        af_row(k, f, 1, 0) + raw[TU1] - raw[TU2] - ub1[0],
+        raw[TU1T] - raw[TU2T] - ub1[1],
+        *(krow(1, 0, 0) * raw[TH + t] + krow(1, 1, 0) * h01[t] + krow(1, 2, 0) * hb1[t] for t in range(2)),
     )
     ha1 = [left_shift(above(2 + t), lane_col(fld(rt, RH + t), DNB)) for t in range(2)]
     he1 = [left_shift(raw[BH + t], lane_col(fld(rt, RH + t), BASE + end)) for t in range(2)]
@@ -328,66 +389,59 @@
         above(5) - above(7) - ue1[1],
         *(ka[0] * above(2 + t) + ka[1] * ha1[t] + ka[2] * he1[t] for t in range(2)),
     )
+    q0e = section_sums(
+        af_row(k, f, 0, end) + raw[BU0] - raw[BU1] + above(6),
+        raw[BU0T] - raw[BU1T] + above(7),
+        *(krow(0, 0, end) * raw[BH + t] + krow(0, 1, end) * above(2 + t) + krow(0, 2, end) * he1[t] for t in range(2)),
+    )
     for t in range(2):
-        halo[WHB + t] = hb1[t]
-        halo[WUB + t] = ub1[t]
-        halo[WHA + t] = above(2 + t)
-        halo[WUA + t] = above(6 + t)
         halo[WQB + t] = qb[t]
         halo[WQA + t] = qa[t]
-        halo[WMA + t] = above(t) + qa[t] + right_shift(qa[t], lane_col(q1l[t], DNB))
-        halo[WMB + t] = below(t) + qb[t] + left_shift(qb[t], lane_col(q0r[t], UPB))
+        halo[WMA + t] = above(t) + qa[t] + right_shift(qa[t], lane_col(q1l[t], DNB)) + q0e[t]
+        halo[WMB + t] = below(t) + qb[t] + left_shift(qb[t], lane_col(q0r[t], UPB)) + q1f[t]
+        halo[WE0 + t] = q0e[t]
+        halo[WF1 + t] = q1f[t]
     halo[WEB] = below(8)
-    halo[WEA] = above(8)
-
-    for a in range(2):
-        geo[a] = (k[a, 0] + k[a, 1] + k[a, 2]) * f[a]
-    for e in range(3):
-        geo[2 + e] = (1.0 / 12.0) / d[e]
-        geo[5 + e] = 0.25 * d[e] * el[e]
-    geo[8] = 1.0 / area[...]
-
+    halo[WEA] = right_shift(above(8), lane_col(fld(lt, LE2), DNB))
+
+    copies = []
     for lev in range(LV):
         row = lambda n, lev=lev: halo[n, lev : lev + 1, :]
         col = lambda n, lev=lev: inject[:, LV * n + lev : LV * n + lev + 1]
-        rcol = lambda n, lev=lev: right[:, LV * n + lev : LV * n + lev + 1]
-        hh = [x[lev] for x in (h, ht)]
-        u = [[d[e] * x[e, lev] for x in (v, vt)] for e in range(3)]
-        h1 = [left_shift(hh[t], rcol(RH + t)) for t in range(2)]
-        u01 = [left_shift(u[0][t], rcol(RU0 + t)) for t in range(2)]
-        n0 = [u[0][t] - u[1][t] + row_up(u[2][t], row(WUA + t)) for t in range(2)]
-        n1 = [u[1][t] - u[2][t] - row_down(u01[t], row(WUB + t)) for t in range(2)]
-        d0 = [k[0, 0] * hh[t] + k[0, 1] * row_up(hh[t], row(WHA + t)) + k[0, 2] * h1[t] for t in range(2)]
-        d1 = [k[1, 0] * hh[t] + k[1, 1] * h1[t] + k[1, 2] * row_down(h1[t], row(WHB + t)) for t in range(2)]
-        q0 = section_sums(geo[0] + n0[0], n0[1], *d0)
-        q1 = section_sums(geo[1] + n1[0], n1[1], *d1)
-        vertex[0, lev] = q0[0]
-        vertex[1, lev] = q1[0]
+        spot = iota(kin.shape[1:], 0)
         grads = []
         for t in range(2):
-            q0d = row_down(q0[t], row(WQB + t))
-            q1u = row_up(q1[t], row(WQA + t))
-            both = q0[t] + q1[t]
+            q0 = jnp.where(spot == end, row(WE0 + t), q[t, 0, lev])
+            q1 = jnp.where(spot == 0, row(WF1 + t), q[t, 1, lev])
+            q0d = row_down(q0, row(WQB + t))
+            q1u = row_up(q1, row(WQA + t))
+            both = q0 + q1
             p, y = both + q0d, both + q1u
             m = p + right_shift(y, col(CY + t))
             m1 = left_shift(p, col(CP + t)) + y
-            grads.append(
-                (
-                    row_up(m, row(WMA + t) + q0[t]) - m,
-                    m1 - m,
-                    row_down(m1, row(WMB + t) + q1[t]) - m,
-                )
+            grads.append((row_up(m, row(WMA + t)) - m, m1 - m, row_down(m1, row(WMB + t)) - m))
+            if t == 0:
+                cell_v[lev] = m * (1.0 / 6.0)
+                vertex_v[0, lev] = q0
+                vertex_v[1, lev] = q1
+                means = (q0 + right_shift(q1u, col(CQ)), both, q1 + q0d)
+        for e in range(3):
+            edge_v[e, lev] = 0.5 * means[e] - geo[2 + e] * (v[e, lev] * grads[0][e] + vt[e, lev] * grads[1][e])
+        rim = jnp.where(spot == 0, row(WEB), 0.0) + jnp.where(spot == end, row(WEA), 0.0)
+        kinetic_v[lev] = (kin[lev] + rim) * geo[8]
+        for n, (src, dst) in enumerate(
+            (
+                (vertex_v.at[:, lev], vertex.at[:, lev]),
+                (kinetic_v.at[lev], kinetic.at[lev]),
+                (cell_v.at[lev], cell.at[lev]),
+                (edge_v.at[:, lev], edge.at[:, lev]),
             )
-            if t == 0:
-                cell[lev] = m * (1.0 / 6.0)
-                means = (q0[0] + right_shift(q1u, col(CQ)), both, q1[0] + q0d)
-        for e in range(3):
-            edge[e, lev] = 0.5 * means[e] - geo[2 + e] * (v[e, lev] * grads[0][e] + vt[e, lev] * grads[1][e])
-        en = [energy(geo[5 + e], v[e, lev], vt[e, lev]) for e in range(3)]
-        zz = en[1] + row_up(en[2], row(WEA))
-        kinetic[lev] = (
-            en[0] + en[1] + en[2] + row_down(en[0], row(WEB)) + right_shift(zz, col(CZ))
-        ) * geo[8]
+        ):
+            copy = pltpu.make_async_copy(src, dst, sems.at[4 * lev + n])
+            copy.start()
+            copies.append(copy)
+    for copy in copies:
+        copy.wait()
 
 
 def swap(x, axis, start):
@@ -399,36 +453,57 @@
     return lax.ppermute(x, axis, pairs)
 
 
-def call(kernel, outs, scratch, *args):
-    vmem = pl.BlockSpec(memory_space=pltpu.VMEM)
+VM = pl.BlockSpec(memory_space=pltpu.VMEM)
+ANY = pl.BlockSpec(memory_space=pl.ANY)
+
+
+def call(kernel, args, outs, scratch=(), sems=0, hbm_in=False, hbm_out=False, flops=0):
+    args = [pltpu.with_memory_space_constraint(x, pltpu.HBM if hbm_in else pltpu.VMEM) for x in args]
+    shape = (lambda s: jax.ShapeDtypeStruct(s, F32)) if hbm_out else (lambda s: pltpu.VMEM(s, F32))
     return pl.pallas_call(
         kernel,
-        out_shape=[jax.ShapeDtypeStruct(s, F32) for s in outs],
-        in_specs=[vmem] * len(args),
-        out_specs=[vmem] * len(outs),
-        scratch_shapes=[pltpu.VMEM(s, F32) for s in scratch],
+        out_shape=[shape(s) for s in outs],
+        in_specs=[ANY if hbm_in else VM] * len(args),
+        out_specs=[ANY if hbm_out else VM] * len(outs),
+        scratch_shapes=[pltpu.VMEM(s, F32) for s in scratch]
+        + ([pltpu.SemaphoreType.DMA((sems,))] if sems else []),
+        compiler_params=pltpu.CompilerParams(vmem_limit_bytes=16 * 2**20),
+        cost_estimate=pl.CostEstimate(flops=flops, transcendentals=0, bytes_accessed=0) if flops else None,
     )(*args)
 
 
-def local(v, h, vt, ht, d, el, area, k, f):
-    levels, rows, cols = h.shape
+def local(*args):
+    levels, rows, cols = args[1].shape
     slab = (rows, 128)
-    send_a, send_b, own0, raw = call(
-        pack_kernel, [slab, slab, slab, (RAW, levels, cols)], [], v, h, vt, ht, d, el, k, f
-    )
+    send_a, send_b, own0, *held = call(
+        pack_kernel, args, [slab, slab, slab] + [x.shape for x in args], sems=PACK_COPIES, hbm_in=True
+    )
+    v, h, vt, ht, d, el, area, k, f = held
     slab_a = swap(send_a, "px", 0)
     slab_b = swap(send_b, "px", 1)
+    raw, geo = call(prep_kernel, held, [(RAW, levels, cols), (9, rows, cols)], flops=20_000_000)
     msg_a, msg_b = call(
-        merge_kernel, [(80, cols), (80, cols)], [(3, 128, 128)], slab_a, slab_b, own0, raw, k, f
+        merge_kernel, [slab_a, slab_b, own0, raw, k, f], [(80, cols), (80, cols)], [(3, 128, 128)]
     )
     msg_a = swap(msg_a, "py", 0)
     msg_b = swap(msg_b, "py", 1)
+    q, kin = call(
+        vertex_kernel,
+        [v, h, vt, ht, d, k, geo, slab_a, slab_b],
+        [(2, 2, levels, rows, cols), (levels, rows, cols)],
+        flops=40_000_000,
+    )
     return tuple(
         call(
-            main_kernel,
+            last_kernel,
+            [v, vt, k, f, geo, slab_a, slab_b, own0, raw, q, kin, msg_a, msg_b],
             [(2, levels, rows, cols), (levels, rows, cols), (levels, rows, cols), (3, levels, rows, cols)],
-            [(3, 128, 128), (2, 80, cols), (18, levels, cols), (9, rows, cols)],
-            v, h, vt, ht, d, el, area, k, f, slab_a, slab_b, own0, raw, msg_a, msg_b,
+            [
+                (3, 128, 128), (2, 80, cols), (14, levels, cols),
+                (2, levels, rows, cols), (levels, rows, cols), (levels, rows, cols), (3, levels, rows, cols),
+            ],
+            sems=4 * LV,
+            hbm_out=True,
         )
     )
 

time: 29.6 us -> 22.9 us (0.77)
  Pallas kernels: 10.9 us -> 7.18 us
  waiting for transfers between devices: 7.52 us -> 5.49 us
  local copies, waits for them, and re-layouts: 1.23 us -> 0 us
  starting transfers between devices: 8.83 us -> 9.16 us
    pallas_call x3 -> x5, Pallas kernels: 10.9 us -> 7.18 us  [call(): pl.pallas_call(kernel, out_shape=[shape(s) for s in outs], in_specs=[ANY...]
    ppermute x4, waiting for transfers between devices: 7.52 us -> 5.49 us  [swap(): return lax.ppermute(x, axis, pairs)]
    unnamed x8 -> x0, local copies, waits for them, and re-layouts: 1.23 us -> none
    ppermute x4, starting transfers between devices: 8.83 us -> 9.16 us  [swap(): return lax.ppermute(x, axis, pairs)]
  transfers between devices with their start and end apart: 4 -> 4, of which waited for: 2 -> 2; matrix products, arithmetic and copies ran while one was open for 0% -> 0% of each run, Pallas kernels for 0% -> 6%
where the time goes in v2:
time: 22.9 us; the launch traced here: 22.5 us
  starting transfers between devices  9.16 us (40%)
  Pallas kernels  7.18 us (31%)
  waiting for transfers between devices  5.49 us (24%)
  between operations  0.67 us (3%)
    ppermute x4, starting transfers between devices, swap(): return lax.ppermute(x, axis, pairs)  9.16 us
    pallas_call x5, Pallas kernels, call(): pl.pallas_call(kernel, out_shape=[shape(s) for s in outs], in_specs=[ANY...  7.18 us
    ppermute x4, waiting for transfers between devices, swap(): return lax.ppermute(x, axis, pairs)  5.49 us
  transfers between devices with their start and end apart: 4, of which 2 were waited for; matrix products, arithmetic and copies ran while one was open for 0% of the time, Pallas kernels for 6%

profile of v2, /device:TPU:25, one launch (start us, length us, event | category | flops | bytes accessed | tf_op | source)
XLA Modules:
  0.0 22.5 jit_solution(4669672383826351692)
XLA Ops:
  0.6 2.9 %shard_map.120 = (f32[32,128]{1,0:T(8,128)S(1)}, f32[32,128]{1,0:T(8,128)S(1)}, f32[32,128]{1,0:T(8,128)S(1)}, f32[3,8,32,256]{3,2,1,0:T(8,128)S(1)}, f32[8,32,2...) custom-call(f32[3,8,32,256]{3,2,1,0:T(8,128)} %v.1, ...), custom_call_target="tpu_custom_call" | custom-call | tf_op jit(solution)/shard_map/pallas_call | solution.py:463
  3.5 1.7 %collective-permute-start = (f32[32,128]{1,0:T(8,128)S(1)}, f32[32,128]{1,0:T(8,128)S(1)}, u32[]{:S(2)}, u32[]{:S(2)}) collective-permute-start(f32[32,128]{1,0:T(8,128)S(1)} %get-tuple-element.32), channel_id=1, source_target_pairs={{0,16},{16,0},{32,48},{48,32},{64,80},{80,64},{96,112},{112,96},{1... | collective-permute-start | bytes 49160 | tf_op jit(solution)/shard_map/ppermute | solution.py:453
  5.2 2.3 %collective-permute-start.1 = (f32[32,128]{1,0:T(8,128)S(1)}, f32[32,128]{1,0:T(8,128)S(1)}, u32[]{:S(2)}, u32[]{:S(2)}) collective-permute-start(f32[32,128]{1,0:T(8,128)S(1)} %get-tuple-element.33), channel_id=1, source_target_pairs={{16,32},{32,16},{48,64},{64,48},{80,96},{96,80},{112,0},{0,112},{1... | collective-permute-start | bytes 49160 | tf_op jit(solution)/shard_map/ppermute | solution.py:453
  7.5 0.1 shard_map.121
  7.7 0.0 collective-permute-done.slab_a
  7.7 2.3 %collective-permute-done.1.slab_b = f32[32,128]{1,0:T(8,128)S(1)} collective-permute-done((f32[32,128]{1,0:T(8,128)S(1)}, f32[32,128]{1,0:T(8,128)S(1)}, u32[]{:S(2)}, u32[]{:S(2)}) %collective-permute-start.1) | collective-permute-done | bytes 16416 | tf_op jit(solution)/shard_map/ppermute | solution.py:453
  9.9 0.4 %shard_map.123 = (f32[80,256]{1,0:T(8,128)S(1)}, f32[80,256]{1,0:T(8,128)S(1)}) custom-call(f32[32,128]{1,0:T(8,128)S(1)} %collective-permute-done.slab_a, f32[32,128]{1,0:T(8,128)S(1)} %collective-permute-done.1.slab_b, f32[32,128]{1,0:T(8,128)S(1)} %get-tuple-element.34.own0, f32[30,8,256]{2,1,0:T(8,128)S(1)} %get-tuple-element.35.raw, ...), custom_call_target="tpu_custom_call" | custom-call | tf_op jit(solution)/shard_map/pallas_call | solution.py:463
  10.3 2.2 %collective-permute-start.2 = (f32[80,256]{1,0:T(8,128)S(1)}, f32[80,256]{1,0:T(8,128)S(1)}, u32[]{:S(2)}, u32[]{:S(2)}) collective-permute-start(f32[80,256]{1,0:T(8,128)S(1)} %get-tuple-element.38), channel_id=1, source_target_pairs={{0,1},{1,0},{2,3},{3,2},{4,5},{5,4},{6,7},{7,6},{8,9},{9,8},{10,11... | collective-permute-start | bytes 245768 | tf_op jit(solution)/shard_map/ppermute | solution.py:453
  12.5 2.9 %collective-permute-start.3 = (f32[80,256]{1,0:T(8,128)S(1)}, f32[80,256]{1,0:T(8,128)S(1)}, u32[]{:S(2)}, u32[]{:S(2)}) collective-permute-start(f32[80,256]{1,0:T(8,128)S(1)} %get-tuple-element.39), channel_id=1, source_target_pairs={{1,2},{2,1},{3,4},{4,3},{5,6},{6,5},{7,8},{8,7},{9,10},{10,9},{11,... | collective-permute-start | bytes 245768 | tf_op jit(solution)/shard_map/ppermute | solution.py:453
  15.4 1.3 %shard_map.122 = (f32[2,2,8,32,256]{4,3,2,1,0:T(8,128)S(1)}, f32[8,32,256]{2,1,0:T(8,128)S(1)}) custom-call(f32[3,8,32,256]{3,2,1,0:T(8,128)S(1)} %get-tuple-element.22.v, f32[8,32,256]{2,1,0:T(8,128)S(1)} %get-tuple-element.26.h, f32[3,8,32,256]{3,2,1,0:T(8,128)S(1)} %get-tuple-element.23.vt, f32[8,32,256]{2,1,0:T(8,128)S(1)} %get-tuple-element.27.ht, ...), custom_call_target="tpu_custom_call" | custom-call | flops 40000000 | tf_op jit(solution)/shard_map/pallas_call | solution.py:463
  16.8 0.0 collective-permute-done.2.msg_a
  16.8 3.2 %collective-permute-done.3.msg_b = f32[80,256]{1,0:T(8,128)S(1)} collective-permute-done((f32[80,256]{1,0:T(8,128)S(1)}, f32[80,256]{1,0:T(8,128)S(1)}, u32[]{:S(2)}, u32[]{:S(2)}) %collective-permute-start.3) | collective-permute-done | bytes 81952 | tf_op jit(solution)/shard_map/ppermute | solution.py:453
  20.0 2.5 %shard_map.124 = (f32[2,8,32,256]{3,2,1,0:T(8,128)}, f32[8,32,256]{2,1,0:T(8,128)}, f32[8,32,256]{2,1,0:T(8,128)}, f32[3,8,32,256]{3,2,1,0:T(8,128)}) custom-call(f32[3,8,32,256]{3,2,1,0:T(8,128)S(1)} %get-tuple-element.22.v, f32[3,8,32,256]{3,2,1,0:T(8,128)S(1)} %get-tuple-element.23.vt, f32[2,3,32,256]{3,2,1,0:T(8,128)S(1)} %get-tuple-element.24.k, ...), custom_call_target="tpu_custom_call" | custom-call | tf_op jit(solution)/shard_map/pallas_call | solution.py:463
Async XLA Ops:
  3.5 4.1 %collective-permute-start = (f32[32,128]{1,0:T(8,128)S(1)}, f32[32,128]{1,0:T(8,128)S(1)}, u32[]{:S(2)}, u32[]{:S(2)}) collective-permute-start(f32[32,128]{1,0:T(8,128)S(1)} %get-tuple-element.32), channel_id=1, source_target_pairs={{0,16},{16,0},{32,48},{48,32},{64,80},{80,64},{96,112},{112,96},{1... | collective-permute-start | bytes 49160 | tf_op jit(solution)/shard_map/ppermute | solution.py:453
  5.2 4.7 %collective-permute-start.1 = (f32[32,128]{1,0:T(8,128)S(1)}, f32[32,128]{1,0:T(8,128)S(1)}, u32[]{:S(2)}, u32[]{:S(2)}) collective-permute-start(f32[32,128]{1,0:T(8,128)S(1)} %get-tuple-element.33), channel_id=1, source_target_pairs={{16,32},{32,16},{48,64},{64,48},{80,96},{96,80},{112,0},{0,112},{1... | collective-permute-start | bytes 49160 | tf_op jit(solution)/shard_map/ppermute | solution.py:453
  10.3 6.5 %collective-permute-start.2 = (f32[80,256]{1,0:T(8,128)S(1)}, f32[80,256]{1,0:T(8,128)S(1)}, u32[]{:S(2)}, u32[]{:S(2)}) collective-permute-start(f32[80,256]{1,0:T(8,128)S(1)} %get-tuple-element.38), channel_id=1, source_target_pairs={{0,1},{1,0},{2,3},{3,2},{4,5},{5,4},{6,7},{7,6},{8,9},{9,8},{10,11... | collective-permute-start | bytes 245768 | tf_op jit(solution)/shard_map/ppermute | solution.py:453
  12.5 7.5 %collective-permute-start.3 = (f32[80,256]{1,0:T(8,128)S(1)}, f32[80,256]{1,0:T(8,128)S(1)}, u32[]{:S(2)}, u32[]{:S(2)}) collective-permute-start(f32[80,256]{1,0:T(8,128)S(1)} %get-tuple-element.39), channel_id=1, source_target_pairs={{1,2},{2,1},{3,4},{4,3},{5,6},{6,5},{7,8},{8,7},{9,10},{10,9},{11,... | collective-permute-start | bytes 245768 | tf_op jit(solution)/shard_map/ppermute | solution.py:453

commit v3 on v2

--- a/solution.py
+++ b/solution.py
@@ -49,19 +49,16 @@
     return w * (v * v + v * vt + vt * vt * (1.0 / 3.0))
 
 
-(RH, RHT, RU0, RU0T, RU1, RU1T, RU2, RU2T, RH1, RH1T, RU01, RU01T) = range(12)
 RGEO = 96
-(LH, LHT, LU0, LU0T, LU1, LU1T, LU2, LU2T, LE1, LE2) = range(10)
-LGEO = 80
-(TH, THT, TH1, TH1T, TU0, TU0T, TU1, TU1T, TU11, TU11T, TU2, TU2T, TU21, TU21T, TE2) = range(15)
-(BH, BHT, BH1, BH1T, BU0, BU0T, BU01, BU01T, BU1, BU1T, BU11, BU11T, BU2, BU2T, BE0) = range(15, 30)
+LGEO, LEN, LFLD = 40, 48, 64
+(TH, THT, TH1, _, TU0, TU0T, TU1, TU1T, TU11, TU11T, TU2, TU2T, TU21, TU21T, TE2) = range(15)
+(BH, BHT, BH1, _, BU0, BU0T, BU01, BU01T, BU1, BU1T, BU11, BU11T, BU2, BU2T, BE0) = range(15, 30)
 RAW = 30
 
 
 def pack_kernel(
-    v, h, vt, ht, d, el, area, k, f, send_a, send_b, own0, vo, ho, vto, hto, do, eo, ao, ko, fo, sems
+    v, h, vt, ht, d, el, area, k, f, send_right, send_left, vo, ho, vto, hto, do, eo, ao, ko, fo, sems
 ):
-    odd = lax.rem(lax.axis_index("px"), 2) == 1
     rows, cols = h.shape[1], h.shape[2]
     half = cols - 128
     started = []
@@ -83,38 +80,53 @@
         copy.wait()
 
     lanes = iota((rows, 128), 1)
-    to_left = jnp.zeros((rows, 128), F32)
-    to_right = jnp.zeros((rows, 128), F32)
-    geo_low = [ko[a, b, :, 0:128] for a in range(2) for b in range(3)]
-    geo_high = [ko[a, b, :, half:cols] for a in range(2) for b in range(3)]
-    for a in range(2):
-        geo_low.append((geo_low[3 * a] + geo_low[3 * a + 1] + geo_low[3 * a + 2]) * fo[a, :, 0:128])
-        geo_high.append((geo_high[3 * a] + geo_high[3 * a + 1] + geo_high[3 * a + 2]) * fo[a, :, half:cols])
-    for n in range(8):
-        to_left = jnp.where(lanes == RGEO + n, geo_low[n][:, 0:1], to_left)
-        to_right = jnp.where(lanes == LGEO + n, geo_high[n][:, 127:128], to_right)
-    first = [do[e, :, 0:128] for e in range(3)]
-    last = [do[e, :, half:cols] for e in range(3)]
-    weight = [0.25 * last[e] * eo[e, :, half:cols] for e in range(3)]
+
+    def grow(x, y, n):
+        return jnp.where(lanes < n, x, pltpu.roll(y, n, 1))
+
+    def grow_back(x, y, n):
+        return jnp.where(lanes >= 128 - n, y, pltpu.roll(x, 128 - n, 1))
+
+    def tree(join, items, n):
+        while len(items) > 1:
+            items = [join(x, y, n) for x, y in zip(items[::2], items[1::2])]
+            n *= 2
+        return items[0]
+
+    def geometry(part):
+        out = [ko[a, b, :, part] for a in range(2) for b in range(3)]
+        return out + [(out[3 * a] + out[3 * a + 1] + out[3 * a + 2]) * fo[a, :, part] for a in range(2)]
+
+    low, high = slice(0, 128), slice(half, cols)
+    geo_left = tree(grow, geometry(low), 1)
+    geo_right = tree(grow_back, geometry(high), 1)
+    first = [do[e, :, low] for e in range(3)]
+    last = [do[e, :, high] for e in range(3)]
+    weight = [0.25 * last[e] * eo[e, :, high] for e in range(3)]
+    kinds = [(grow, 2)] * 4 + [(grow, 1)] * 4 + [(grow_back, 1)] * 10
+    stacks = [[] for _ in kinds]
     for lev in range(LV):
         for copy in by_level[lev]:
             copy.wait()
-        low = [(ho[lev, :, 0:128], 0), (hto[lev, :, 0:128], 0)]
-        high = [ho[lev, :, half:cols], hto[lev, :, half:cols]]
-        for e in range(3):
-            for x in (vo, vto):
-                low.append((first[e] * x[e, lev, :, 0:128], 0))
-                high.append(last[e] * x[e, lev, :, half:cols])
-        low += [(x, 1) for x, _ in low[:4]]
+        for part, dist, base in ((low, first, 0), (high, last, 8)):
+            fields = [ho[lev, :, part], hto[lev, :, part]]
+            fields += [dist[e] * x[e, lev, :, part] for e in range(3) for x in (vo, vto)]
+            for n, x in enumerate(fields):
+                stacks[base + n].append((1, x))
         for e in (1, 2):
-            high.append(energy(weight[e], vo[e, lev, :, half:cols], vto[e, lev, :, half:cols]))
-        for n, (x, c) in enumerate(low):
-            to_left = jnp.where(lanes == LV * n + lev, x[:, c : c + 1], to_left)
-        for n, x in enumerate(high):
-            to_right = jnp.where(lanes == LV * n + lev, x[:, 127:128], to_right)
-    send_a[...] = jnp.where(odd, to_left, to_right)
-    send_b[...] = jnp.where(odd, to_right, to_left)
-    own0[...] = to_left
+            stacks[15 + e].append((1, energy(weight[e], vo[e, lev, :, high], vto[e, lev, :, high])))
+        for stack, (join, width) in zip(stacks, kinds):
+            while len(stack) > 1 and stack[-1][0] == stack[-2][0]:
+                (count, x), (_, y) = stack[-2:]
+                stack[-2:] = [(2 * count, join(x, y, count * width))]
+    done = [stack[0][1] for stack in stacks]
+    to_left = grow(tree(grow, done[0:4], 16), tree(grow, done[4:8], 8), 64)
+    to_left = jnp.where(lanes < RGEO, to_left, pltpu.roll(geo_left, RGEO, 1))
+    to_right = tree(grow_back, done[8:16], 8)
+    to_right = grow_back(grow_back(done[16], done[17], 8), to_right, 64)
+    to_right = jnp.where(lanes < LEN, pltpu.roll(geo_right, LEN, 1), to_right)
+    send_right[...] = to_right
+    send_left[...] = to_left
     area_copy.wait()
 
 
@@ -157,15 +169,21 @@
     return (k[a, 0, r : r + 1, :] + k[a, 1, r : r + 1, :] + k[a, 2, r : r + 1, :]) * f[a, r : r + 1, :]
 
 
-def fld(t, n):
-    return t[LV * n : LV * n + LV, :]
+def left_field(t, n):
+    return t[LFLD + LV * n : LFLD + LV * n + LV, :]
+
+
+def right_field(t, n, c=0):
+    if n >= 4:
+        return t[32 + LV * n : 32 + LV * n + LV, :]
+    return t[pl.ds(16 * n + c, LV, stride=2), :]
 
 
 def column_left(lt, h0, h0t, u00, u00t):
     k = [lt[LGEO + n : LGEO + n + 1, :] for n in range(8)]
     up = lambda x: pltpu.roll(x, 127, 1)
     dn = lambda x: pltpu.roll(x, 1, 1)
-    h, hp, u0, u0p, u1, u1p, u2, u2p = (fld(lt, n) for n in range(8))
+    h, hp, u0, u0p, u1, u1p, u2, u2p = (left_field(lt, n) for n in range(8))
     q0 = section_sums(
         k[6] + u0 - u1 + up(u2),
         u0p - u1p + up(u2p),
@@ -185,7 +203,8 @@
     k = [rt[RGEO + n : RGEO + n + 1, :] for n in range(8)]
     up = lambda x: pltpu.roll(x, 127, 1)
     dn = lambda x: pltpu.roll(x, 1, 1)
-    h, hp, u0, u0p, u1, u1p, u2, u2p, h1, h1p, u01, u01p = (fld(rt, n) for n in range(12))
+    h, hp, u0, u0p, u1, u1p, u2, u2p = (right_field(rt, n) for n in range(8))
+    h1, h1p, u01, u01p = (right_field(rt, n, 1) for n in range(4))
     q0 = section_sums(
         k[6] + u0 - u1 + up(u2),
         u0p - u1p + up(u2p),
@@ -205,26 +224,26 @@
     return x[:, lane : lane + 1]
 
 
-def merge_kernel(slab_a, slab_b, own0, raw, k, f, msg_a, msg_b, ext):
-    odd_x = lax.rem(lax.axis_index("px"), 2) == 1
+def merge_kernel(slab_l, slab_r, own0, raw, k, f, msg_a, msg_b, ext, turned):
     odd_y = lax.rem(lax.axis_index("py"), 2) == 1
-    rows = slab_a.shape[0]
+    rows = slab_l.shape[0]
     end = rows - 1
-    left = jnp.where(odd_x, slab_a[...], slab_b[...])
-    right = jnp.where(odd_x, slab_b[...], slab_a[...])
+    left, right = slab_l[...], slab_r[...]
     ext[0, BASE : BASE + rows, :] = left
     ext[1, BASE : BASE + rows, :] = right
     ext[2, BASE : BASE + rows, :] = own0[...]
-    lt, rt, ot = (jnp.transpose(ext[n]) for n in range(3))
-    q0l, q1l = column_left(lt, fld(ot, RH), fld(ot, RHT), fld(ot, RU0), fld(ot, RU0T))
+    for n in range(3):
+        turned[n] = jnp.transpose(ext[n])
+    lt, rt, ot = (turned.at[n] for n in range(3))
+    q0l, q1l = column_left(lt, *(right_field(ot, n) for n in range(4)))
     q0r, q1r = column_right(rt)
     r0, r1 = BASE, BASE + 1
     e0, e1 = BASE + end, BASE + end - 1
     krow = lambda a, b, r: k[a, b, r : r + 1, :]
 
-    h_0 = [left_shift(raw[TH + t], lane_col(fld(rt, RH + t), r0)) for t in range(2)]
-    h_1 = [left_shift(raw[TH1 + t], lane_col(fld(rt, RH + t), r1)) for t in range(2)]
-    u_0 = [left_shift(raw[TU0 + t], lane_col(fld(rt, RU0 + t), r0)) for t in range(2)]
+    h_0 = [left_shift(raw[TH + t], lane_col(right_field(rt, t), r0)) for t in range(2)]
+    h_1 = [left_shift(raw[TH1 + t], lane_col(right_field(rt, t), r1)) for t in range(2)]
+    u_0 = [left_shift(raw[TU0 + t], lane_col(right_field(rt, 2 + t), r0)) for t in range(2)]
     up0 = section_sums(
         af_row(k, f, 0, 0) + raw[TU0] - raw[TU1] + raw[TU21],
         raw[TU0T] - raw[TU1T] + raw[TU21T],
@@ -239,9 +258,9 @@
         up0[t] + right_shift(up0[t] + up1[t], lane_col(q0l[t], r0) + lane_col(q1l[t], r1)) for t in range(2)
     ]
 
-    hb_0 = [left_shift(raw[BH + t], lane_col(fld(rt, RH + t), e0)) for t in range(2)]
-    hb_1 = [left_shift(raw[BH1 + t], lane_col(fld(rt, RH + t), e1)) for t in range(2)]
-    ub_1 = [left_shift(raw[BU01 + t], lane_col(fld(rt, RU0 + t), e1)) for t in range(2)]
+    hb_0 = [left_shift(raw[BH + t], lane_col(right_field(rt, t), e0)) for t in range(2)]
+    hb_1 = [left_shift(raw[BH1 + t], lane_col(right_field(rt, t), e1)) for t in range(2)]
+    ub_1 = [left_shift(raw[BU01 + t], lane_col(right_field(rt, 2 + t), e1)) for t in range(2)]
     dn1 = section_sums(
         af_row(k, f, 1, end) + raw[BU1] - raw[BU2] - ub_1[0],
         raw[BU1T] - raw[BU2T] - ub_1[1],
@@ -283,21 +302,19 @@
         store(msg_b, msg_a)
 
 
-(WQB, WQBT, WQA, WQAT, WMA, WMAT, WMB, WMBT, WE0, WE0T, WF1, WF1T, WEB, WEA) = range(14)
-(CY, CYT, CQ, CP, CPT) = range(5)
-
-
-def vertex_kernel(v, h, vt, ht, d, k, geo, slab_a, slab_b, q, kin):
-    odd_x = lax.rem(lax.axis_index("px"), 2) == 1
-    left = jnp.where(odd_x, slab_a[...], slab_b[...])
-    right = jnp.where(odd_x, slab_b[...], slab_a[...])
+(WQB, _, WQA, _, WMA, _, WMB, _, WE0, _, WF1, _, WEB, WEA) = range(14)
+(CY, _, CQ, CP, _) = range(5)
+
+
+def vertex_kernel(v, h, vt, ht, d, k, geo, slab_l, slab_r, q, kin):
+    left, right = slab_l[...], slab_r[...]
     z = left + row_up(pltpu.roll(left, 128 - LV, 1), 0.0)
     for lev in range(LV):
-        rcol = lambda n, lev=lev: right[:, LV * n + lev : LV * n + lev + 1]
+        rcol = lambda n, lev=lev: right[:, 16 * n + 2 * lev : 16 * n + 2 * lev + 1]
         hh = [x[lev] for x in (h, ht)]
         u = [[d[e] * x[e, lev] for x in (v, vt)] for e in range(3)]
-        h1 = [left_shift(hh[t], rcol(RH + t)) for t in range(2)]
-        u01 = [left_shift(u[0][t], rcol(RU0 + t)) for t in range(2)]
+        h1 = [left_shift(hh[t], rcol(t)) for t in range(2)]
+        u01 = [left_shift(u[0][t], rcol(2 + t)) for t in range(2)]
         up = lambda x: pltpu.roll(x, x.shape[0] - 1, 0)
         dn = lambda x: pltpu.roll(x, 1, 0)
         n0 = [u[0][t] - u[1][t] + up(u[2][t]) for t in range(2)]
@@ -311,15 +328,14 @@
             q[t, 1, lev] = q1[t]
         en = [energy(geo[5 + e], v[e, lev], vt[e, lev]) for e in range(3)]
         zz = en[1] + row_up(en[2], 0.0)
-        zcol = z[:, LV * LE1 + lev : LV * LE1 + lev + 1]
+        zcol = z[:, LEN + lev : LEN + lev + 1]
         kin[lev] = en[0] + en[1] + en[2] + row_down(en[0], 0.0) + right_shift(zz, zcol)
 
 
 def last_kernel(
-    v, vt, k, f, geo, slab_a, slab_b, own0, raw, q, kin, msg_a, msg_b,
-    vertex, kinetic, cell, edge, ext, msgs, halo, vertex_v, kinetic_v, cell_v, edge_v, sems,
+    v, vt, k, f, geo, slab_l, slab_r, own0, raw, q, kin, msg_a, msg_b,
+    vertex, kinetic, cell, edge, ext, turned, msgs, halo, vertex_v, kinetic_v, cell_v, edge_v, sems,
 ):
-    odd_x = lax.rem(lax.axis_index("px"), 2) == 1
     odd_y = lax.rem(lax.axis_index("py"), 2) == 1
     rows = kin.shape[1]
     end = rows - 1
@@ -340,20 +356,21 @@
     kb = [msgs[1, 72 + n : 73 + n, :] for n in range(4)]
     krow = lambda a, b, r: k[a, b, r : r + 1, :]
 
-    left = jnp.where(odd_x, slab_a[...], slab_b[...])
-    right = jnp.where(odd_x, slab_b[...], slab_a[...])
+    left, right = slab_l[...], slab_r[...]
     ext[0, BASE : BASE + rows, :] = left
     ext[1, BASE : BASE + rows, :] = right
     ext[2, BASE : BASE + rows, :] = own0[...]
     ext[0, DNB : DNB + 1, :] = msgs[0, 76:77, 0:128]
     ext[1, DNB : DNB + 1, :] = msgs[0, 76:77, 128:256]
     ext[1, UPB : UPB + 1, :] = msgs[1, 76:77, 128:256]
-    lt, rt, ot = (jnp.transpose(ext[n]) for n in range(3))
+    for n in range(3):
+        turned[n] = jnp.transpose(ext[n])
+    lt, rt, ot = (turned.at[n] for n in range(3))
     lanes = iota((LV, 128), 1)
     low = lambda x, row: jnp.where(lanes == UPB, row[:, 0:1], x)
     high = lambda x, row: jnp.where(lanes == DNB, row[:, 0:1], x)
-    h0 = [high(low(fld(ot, RH + t), below(2 + t)), above(2 + t)) for t in range(2)]
-    u00 = [low(fld(ot, RU0 + t), below(4 + t)) for t in range(2)]
+    h0 = [high(low(right_field(ot, t), below(2 + t)), above(2 + t)) for t in range(2)]
+    u00 = [low(right_field(ot, 2 + t), below(4 + t)) for t in range(2)]
     q0l, q1l = column_left(lt, *h0, *u00)
     q0r, q1r = column_right(rt)
     up = lambda x: pltpu.roll(x, 127, 1)
@@ -368,9 +385,9 @@
     packed = jnp.concatenate(cols_out + [jnp.zeros((128 - LV * len(cols_out), 128), F32)], axis=0)
     inject = jnp.transpose(packed)[BASE : BASE + rows, :]
 
-    hb1 = [left_shift(below(2 + t), lane_col(fld(rt, RH + t), UPB)) for t in range(2)]
-    ub1 = [left_shift(below(4 + t), lane_col(fld(rt, RU0 + t), UPB)) for t in range(2)]
-    h01 = [left_shift(raw[TH + t], lane_col(fld(rt, RH + t), BASE)) for t in range(2)]
+    hb1 = [left_shift(below(2 + t), lane_col(right_field(rt, t), UPB)) for t in range(2)]
+    ub1 = [left_shift(below(4 + t), lane_col(right_field(rt, 2 + t), UPB)) for t in range(2)]
+    h01 = [left_shift(raw[TH + t], lane_col(right_field(rt, t), BASE)) for t in range(2)]
     qb = section_sums(
         kb[3] + below(4) - below(6) + raw[TU2],
         below(5) - below(7) + raw[TU2T],
@@ -381,9 +398,9 @@
         raw[TU1T] - raw[TU2T] - ub1[1],
         *(krow(1, 0, 0) * raw[TH + t] + krow(1, 1, 0) * h01[t] + krow(1, 2, 0) * hb1[t] for t in range(2)),
     )
-    ha1 = [left_shift(above(2 + t), lane_col(fld(rt, RH + t), DNB)) for t in range(2)]
-    he1 = [left_shift(raw[BH + t], lane_col(fld(rt, RH + t), BASE + end)) for t in range(2)]
-    ue1 = [left_shift(raw[BU0 + t], lane_col(fld(rt, RU0 + t), BASE + end)) for t in range(2)]
+    ha1 = [left_shift(above(2 + t), lane_col(right_field(rt, t), DNB)) for t in range(2)]
+    he1 = [left_shift(raw[BH + t], lane_col(right_field(rt, t), BASE + end)) for t in range(2)]
+    ue1 = [left_shift(raw[BU0 + t], lane_col(right_field(rt, 2 + t), BASE + end)) for t in range(2)]
     qa = section_sums(
         ka[3] + above(4) - above(6) - ue1[0],
         above(5) - above(7) - ue1[1],
@@ -402,7 +419,7 @@
         halo[WE0 + t] = q0e[t]
         halo[WF1 + t] = q1f[t]
     halo[WEB] = below(8)
-    halo[WEA] = right_shift(above(8), lane_col(fld(lt, LE2), DNB))
+    halo[WEA] = right_shift(above(8), lane_col(lt[LEN + LV : LEN + 2 * LV, :], DNB))
 
     copies = []
     for lev in range(LV):
@@ -444,6 +461,11 @@
         copy.wait()
 
 
+def shift(x, axis, by):
+    n = lax.axis_size(axis)
+    return lax.ppermute(x, axis, [(i, (i + by) % n) for i in range(n)])
+
+
 def swap(x, axis, start):
     n = lax.axis_size(axis)
     pairs = []
@@ -472,34 +494,34 @@
     )(*args)
 
 
-def local(*args):
+def step(*args):
     levels, rows, cols = args[1].shape
     slab = (rows, 128)
-    send_a, send_b, own0, *held = call(
-        pack_kernel, args, [slab, slab, slab] + [x.shape for x in args], sems=PACK_COPIES, hbm_in=True
-    )
-    v, h, vt, ht, d, el, area, k, f = held
-    slab_a = swap(send_a, "px", 0)
-    slab_b = swap(send_b, "px", 1)
+    send_right, send_left, *held = call(
+        pack_kernel, args, [slab, slab] + [x.shape for x in args], sems=PACK_COPIES, hbm_in=True
+    )
+    v, h, vt, ht, d, _, _, k, f = held
+    slab_l = shift(send_right, "px", 1)
+    slab_r = shift(send_left, "px", -1)
     raw, geo = call(prep_kernel, held, [(RAW, levels, cols), (9, rows, cols)], flops=20_000_000)
     msg_a, msg_b = call(
-        merge_kernel, [slab_a, slab_b, own0, raw, k, f], [(80, cols), (80, cols)], [(3, 128, 128)]
-    )
+        merge_kernel, [slab_l, slab_r, send_left, raw, k, f], [(80, cols), (80, cols)], [(3, 128, 128), (3, 128, 128)]
+    )
+    msg_b = swap(msg_b, "py", 1)
     msg_a = swap(msg_a, "py", 0)
-    msg_b = swap(msg_b, "py", 1)
     q, kin = call(
         vertex_kernel,
-        [v, h, vt, ht, d, k, geo, slab_a, slab_b],
+        [v, h, vt, ht, d, k, geo, slab_l, slab_r],
         [(2, 2, levels, rows, cols), (levels, rows, cols)],
         flops=40_000_000,
     )
     return tuple(
         call(
             last_kernel,
-            [v, vt, k, f, geo, slab_a, slab_b, own0, raw, q, kin, msg_a, msg_b],
+            [v, vt, k, f, geo, slab_l, slab_r, send_left, raw, q, kin, msg_a, msg_b],
             [(2, levels, rows, cols), (levels, rows, cols), (levels, rows, cols), (3, levels, rows, cols)],
             [
-                (3, 128, 128), (2, 80, cols), (14, levels, cols),
+                (3, 128, 128), (3, 128, 128), (2, 80, cols), (14, levels, cols),
                 (2, levels, rows, cols), (levels, rows, cols), (levels, rows, cols), (3, levels, rows, cols),
             ],
             sems=4 * LV,
@@ -512,7 +534,7 @@
     field = P(None, "py", "px")
     pair = P(None, None, "py", "px")
     return jax.shard_map(
-        local,
+        step,
         mesh=mesh,
         in_specs=(pair, field, pair, field, field, field, P("py", "px"), pair, field),
         out_specs=(pair, field, field, pair),

time: 22.9 us -> 21.1 us (0.921)
  the two profiles are of different devices: /device:TPU:25 before, /device:TPU:0 now
where the time goes in v3:
time: 21.1 us; the launch traced here: 20.9 us
  starting transfers between devices  10.9 us (52%)
  Pallas kernels  7.03 us (33%)
  waiting for transfers between devices  2.32 us (11%)
  between operations  0.68 us (3%)
    pallas_call x5, Pallas kernels, call(): pl.pallas_call(kernel, out_shape=[shape(s) for s in outs], in_specs=[ANY...  7.03 us
    ppermute x2, starting transfers between devices, swap(): return lax.ppermute(x, axis, pairs)  6.53 us
    ppermute x2, starting transfers between devices, shift(): return lax.ppermute(x, axis, [(i, (i + by) % n) for i in range(n)])  4.37 us
    ppermute x2, waiting for transfers between devices, shift(): return lax.ppermute(x, axis, [(i, (i + by) % n) for i in range(n)])  1.51 us
    ppermute x2, waiting for transfers between devices, swap(): return lax.ppermute(x, axis, pairs)  0.81 us
  transfers between devices with their start and end apart: 4, of which 2 were waited for; matrix products, arithmetic and copies ran while one was open for 0% of the time, Pallas kernels for 7%

profile of v3, /device:TPU:0, one launch (start us, length us, event | category | flops | bytes accessed | tf_op | source)
XLA Modules:
  0.0 20.9 jit_solution(4518429595495268002)
XLA Ops:
  0.6 2.7 %shard_map.120 = (f32[32,128]{1,0:T(8,128)S(1)}, f32[32,128]{1,0:T(8,128)S(1)}, f32[3,8,32,256]{3,2,1,0:T(8,128)S(1)}, f32[8,32,256]{2,1,0:T(8,128)S(1)}, f32[3,...) custom-call(f32[3,8,32,256]{3,2,1,0:T(8,128)} %v.1, ...), custom_call_target="tpu_custom_call" | custom-call | tf_op jit(solution)/shard_map/pallas_call | solution.py:485
  3.4 2.1 %collective-permute-start = (f32[32,128]{1,0:T(8,128)S(1)}, f32[32,128]{1,0:T(8,128)S(1)}, u32[]{:S(2)}, u32[]{:S(2)}) collective-permute-start(f32[32,128]{1,0:T(8,128)S(1)} %get-tuple-element.31), channel_id=1, source_target_pairs={{0,16},{16,32},{32,48},{48,64},{64,80},{80,96},{96,112},{112,0},{1... | collective-permute-start | bytes 49160 | tf_op jit(solution)/shard_map/ppermute | solution.py:466
  5.5 2.3 %collective-permute-start.1 = (f32[32,128]{1,0:T(8,128)S(1)}, f32[32,128]{1,0:T(8,128)S(1)}, u32[]{:S(2)}, u32[]{:S(2)}) collective-permute-start(f32[32,128]{1,0:T(8,128)S(1)} %get-tuple-element.32.own0), channel_id=1, source_target_pairs={{0,112},{16,0},{32,16},{48,32},{64,48},{80,64},{96,80},{112,96},{1... | collective-permute-start | bytes 49160 | tf_op jit(solution)/shard_map/ppermute | solution.py:466
  7.7 0.1 shard_map.121
  7.9 1.5 %collective-permute-done.slab_l = f32[32,128]{1,0:T(8,128)S(1)} collective-permute-done((f32[32,128]{1,0:T(8,128)S(1)}, f32[32,128]{1,0:T(8,128)S(1)}, u32[]{:S(2)}, u32[]{:S(2)}) %collective-permute-start) | collective-permute-done | bytes 16416 | tf_op jit(solution)/shard_map/ppermute | solution.py:466
  9.4 0.0 collective-permute-done.1.slab_r
  9.4 0.4 %shard_map.123 = (f32[80,256]{1,0:T(8,128)S(1)}, f32[80,256]{1,0:T(8,128)S(1)}) custom-call(f32[32,128]{1,0:T(8,128)S(1)} %collective-permute-done.slab_l, f32[32,128]{1,0:T(8,128)S(1)} %collective-permute-done.1.slab_r, f32[32,128]{1,0:T(8,128)S(1)} %get-tuple-element.32.own0, f32[30,8,256]{2,1,0:T(8,128)S(1)} %get-tuple-element.33.raw, ...), custom_call_target="tpu_custom_call" | custom-call | tf_op jit(solution)/shard_map/pallas_call | solution.py:485
  9.8 0.1 collective-permute-start.2
  9.9 6.4 %collective-permute-start.3 = (f32[80,256]{1,0:T(8,128)S(1)}, f32[80,256]{1,0:T(8,128)S(1)}, u32[]{:S(2)}, u32[]{:S(2)}) collective-permute-start(f32[80,256]{1,0:T(8,128)S(1)} %get-tuple-element.37), channel_id=1, source_target_pairs={{1,2},{2,1},{3,4},{4,3},{5,6},{6,5},{7,8},{8,7},{9,10},{10,9},{11,... | collective-permute-start | bytes 245768 | tf_op jit(solution)/shard_map/ppermute | solution.py:475
  16.3 1.3 %shard_map.122 = (f32[2,2,8,32,256]{4,3,2,1,0:T(8,128)S(1)}, f32[8,32,256]{2,1,0:T(8,128)S(1)}) custom-call(f32[3,8,32,256]{3,2,1,0:T(8,128)S(1)} %get-tuple-element.21.v, f32[8,32,256]{2,1,0:T(8,128)S(1)} %get-tuple-element.25.h, f32[3,8,32,256]{3,2,1,0:T(8,128)S(1)} %get-tuple-element.22.vt, f32[8,32,256]{2,1,0:T(8,128)S(1)} %get-tuple-element.26.ht, ...), custom_call_target="tpu_custom_call" | custom-call | flops 40000000 | tf_op jit(solution)/shard_map/pallas_call | solution.py:485
  17.6 0.0 collective-permute-done.2.msg_a
  17.6 0.8 %collective-permute-done.3.msg_b = f32[80,256]{1,0:T(8,128)S(1)} collective-permute-done((f32[80,256]{1,0:T(8,128)S(1)}, f32[80,256]{1,0:T(8,128)S(1)}, u32[]{:S(2)}, u32[]{:S(2)}) %collective-permute-start.3) | collective-permute-done | bytes 81952 | tf_op jit(solution)/shard_map/ppermute | solution.py:475
  18.4 2.5 %shard_map.124 = (f32[2,8,32,256]{3,2,1,0:T(8,128)}, f32[8,32,256]{2,1,0:T(8,128)}, f32[8,32,256]{2,1,0:T(8,128)}, f32[3,8,32,256]{3,2,1,0:T(8,128)}) custom-call(f32[3,8,32,256]{3,2,1,0:T(8,128)S(1)} %get-tuple-element.21.v, f32[3,8,32,256]{3,2,1,0:T(8,128)S(1)} %get-tuple-element.22.vt, f32[2,3,32,256]{3,2,1,0:T(8,128)S(1)} %get-tuple-element.23.k, ...), custom_call_target="tpu_custom_call" | custom-call | tf_op jit(solution)/shard_map/pallas_call | solution.py:485
Async XLA Ops:
  3.4 6.0 %collective-permute-start = (f32[32,128]{1,0:T(8,128)S(1)}, f32[32,128]{1,0:T(8,128)S(1)}, u32[]{:S(2)}, u32[]{:S(2)}) collective-permute-start(f32[32,128]{1,0:T(8,128)S(1)} %get-tuple-element.31), channel_id=1, source_target_pairs={{0,16},{16,32},{32,48},{48,64},{64,80},{80,96},{96,112},{112,0},{1... | collective-permute-start | bytes 49160 | tf_op jit(solution)/shard_map/ppermute | solution.py:466
  5.5 3.9 %collective-permute-start.1 = (f32[32,128]{1,0:T(8,128)S(1)}, f32[32,128]{1,0:T(8,128)S(1)}, u32[]{:S(2)}, u32[]{:S(2)}) collective-permute-start(f32[32,128]{1,0:T(8,128)S(1)} %get-tuple-element.32.own0), channel_id=1, source_target_pairs={{0,112},{16,0},{32,16},{48,32},{64,48},{80,64},{96,80},{112,96},{1... | collective-permute-start | bytes 49160 | tf_op jit(solution)/shard_map/ppermute | solution.py:466
  9.8 7.8 %collective-permute-start.2 = (f32[80,256]{1,0:T(8,128)S(1)}, f32[80,256]{1,0:T(8,128)S(1)}, u32[]{:S(2)}, u32[]{:S(2)}) collective-permute-start(f32[80,256]{1,0:T(8,128)S(1)} %get-tuple-element.36), channel_id=1, source_target_pairs={{0,1},{1,0},{2,3},{3,2},{4,5},{5,4},{6,7},{7,6},{8,9},{9,8},{10,11... | collective-permute-start | bytes 245768 | tf_op jit(solution)/shard_map/ppermute | solution.py:475
  9.9 8.6 %collective-permute-start.3 = (f32[80,256]{1,0:T(8,128)S(1)}, f32[80,256]{1,0:T(8,128)S(1)}, u32[]{:S(2)}, u32[]{:S(2)}) collective-permute-start(f32[80,256]{1,0:T(8,128)S(1)} %get-tuple-element.37), channel_id=1, source_target_pairs={{1,2},{2,1},{3,4},{4,3},{5,6},{6,5},{7,8},{8,7},{9,10},{10,9},{11,... | collective-permute-start | bytes 245768 | tf_op jit(solution)/shard_map/ppermute | solution.py:475

commit v4 on v3

--- a/solution.py
+++ b/solution.py
@@ -53,7 +53,8 @@
 LGEO, LEN, LFLD = 40, 48, 64
 (TH, THT, TH1, _, TU0, TU0T, TU1, TU1T, TU11, TU11T, TU2, TU2T, TU21, TU21T, TE2) = range(15)
 (BH, BHT, BH1, _, BU0, BU0T, BU01, BU01T, BU1, BU1T, BU11, BU11T, BU2, BU2T, BE0) = range(15, 30)
-RAW = 30
+RIM = ((0, 0), (1, 0), (2, 0), (2, 1), (0, -2), (0, -1), (1, -1), (2, -1))
+RAW = 30 + 2 * len(RIM)
 
 
 def pack_kernel(
@@ -70,71 +71,73 @@
         return copy
 
     fixed = [start(x, y) for x, y in ((d, do), (el, eo), (k, ko), (f, fo))]
-    by_level = [
-        [start(x.at[lev], y.at[lev]) for x, y in ((h, ho), (ht, hto))]
-        + [start(x.at[:, lev], y.at[:, lev]) for x, y in ((v, vo), (vt, vto))]
-        for lev in range(LV)
-    ]
+    by_level = []
+    for lev in range(0, LV, LV // 2):
+        cut = slice(lev, lev + LV // 2)
+        by_level.append([start(x.at[cut], y.at[cut]) for x, y in ((h, ho), (ht, hto))])
+        by_level[-1] += [start(x.at[:, cut], y.at[:, cut]) for x, y in ((v, vo), (vt, vto))]
     area_copy = start(area, ao)
     for copy in fixed:
         copy.wait()
 
     lanes = iota((rows, 128), 1)
 
-    def grow(x, y, n):
-        return jnp.where(lanes < n, x, pltpu.roll(y, n, 1))
-
-    def grow_back(x, y, n):
-        return jnp.where(lanes >= 128 - n, y, pltpu.roll(x, 128 - n, 1))
-
-    def tree(join, items, n):
-        while len(items) > 1:
-            items = [join(x, y, n) for x, y in zip(items[::2], items[1::2])]
-            n *= 2
-        return items[0]
+    def push(stack, x, wide=1, first=0):
+        if stack is None:
+            return x
+        back = pltpu.roll(stack, 128 - wide, 1)
+        return jnp.where(lanes == 127, x, back) if first else jnp.where(lanes < wide, x, back)
+
+    def place(slab, stack, by, start, stop):
+        moved = pltpu.roll(stack, by % 128, 1) if by % 128 else stack
+        return jnp.where((lanes >= start) & (lanes < stop), moved, slab)
 
     def geometry(part):
         out = [ko[a, b, :, part] for a in range(2) for b in range(3)]
         return out + [(out[3 * a] + out[3 * a + 1] + out[3 * a + 2]) * fo[a, :, part] for a in range(2)]
 
     low, high = slice(0, 128), slice(half, cols)
-    geo_left = tree(grow, geometry(low), 1)
-    geo_right = tree(grow_back, geometry(high), 1)
-    first = [do[e, :, low] for e in range(3)]
-    last = [do[e, :, high] for e in range(3)]
-    weight = [0.25 * last[e] * eo[e, :, high] for e in range(3)]
-    kinds = [(grow, 2)] * 4 + [(grow, 1)] * 4 + [(grow_back, 1)] * 10
-    stacks = [[] for _ in kinds]
+    geo_left = geo_right = None
+    for x, y in zip(geometry(low), geometry(high)):
+        geo_left = push(geo_left, x)
+        geo_right = push(geo_right, y, 1, 127)
+    near = [do[e, :, low] for e in range(3)]
+    far = [do[e, :, high] for e in range(3)]
+    weight = [0.25 * far[e] * eo[e, :, high] for e in range(3)]
+    left, right = [None] * 8, [None] * 10
     for lev in range(LV):
-        for copy in by_level[lev]:
-            copy.wait()
-        for part, dist, base in ((low, first, 0), (high, last, 8)):
+        if lev % (LV // 2) == 0:
+            for copy in by_level[lev // (LV // 2)]:
+                copy.wait()
+        for part, dist, stacks in ((low, near, left), (high, far, right)):
             fields = [ho[lev, :, part], hto[lev, :, part]]
             fields += [dist[e] * x[e, lev, :, part] for e in range(3) for x in (vo, vto)]
+            if part is high:
+                fields += [energy(weight[e], vo[e, lev, :, part], vto[e, lev, :, part]) for e in (1, 2)]
             for n, x in enumerate(fields):
-                stacks[base + n].append((1, x))
-        for e in (1, 2):
-            stacks[15 + e].append((1, energy(weight[e], vo[e, lev, :, high], vto[e, lev, :, high])))
-        for stack, (join, width) in zip(stacks, kinds):
-            while len(stack) > 1 and stack[-1][0] == stack[-2][0]:
-                (count, x), (_, y) = stack[-2:]
-                stack[-2:] = [(2 * count, join(x, y, count * width))]
-    done = [stack[0][1] for stack in stacks]
-    to_left = grow(tree(grow, done[0:4], 16), tree(grow, done[4:8], 8), 64)
-    to_left = jnp.where(lanes < RGEO, to_left, pltpu.roll(geo_left, RGEO, 1))
-    to_right = tree(grow_back, done[8:16], 8)
-    to_right = grow_back(grow_back(done[16], done[17], 8), to_right, 64)
-    to_right = jnp.where(lanes < LEN, pltpu.roll(geo_right, LEN, 1), to_right)
+                stacks[n] = push(stacks[n], x, *((1, 127) if part is high else (2,) if n < 4 else (1,)))
+    to_left = jnp.zeros((rows, 128), F32)
+    to_right = right[7]
+    for n in range(4):
+        to_left = place(to_left, left[n], 16 * n + 14, 16 * n, 16 * n + 16)
+        to_left = place(to_left, left[n + 4], 64 + LV * n + 7, 64 + LV * n, 72 + LV * n)
+    to_left = place(to_left, geo_left, RGEO + 7, RGEO, RGEO + 8)
+    for n in range(7):
+        to_right = place(to_right, right[n], LFLD + LV * n - 120, LFLD + LV * n, LFLD + LV * n + LV)
+    for n in range(2):
+        to_right = place(to_right, right[8 + n], LEN + LV * n - 120, LEN + LV * n, LEN + LV * n + LV)
+    to_right = place(to_right, geo_right, LGEO - 120, LGEO, LGEO + 8)
     send_right[...] = to_right
     send_left[...] = to_left
     area_copy.wait()
 
 
-PACK_COPIES = 4 + 4 * LV + 1
-
-
-def prep_kernel(v, h, vt, ht, d, el, area, k, f, raw, geo):
-    end = h.shape[1] - 1
+PACK_COPIES = 4 + 4 * 2 + 1
+
+
+def vertex_kernel(v, h, vt, ht, d, el, area, k, f, raw, geo, q, kin):
+    rows = h.shape[1]
+    end = rows - 1
     for x, n in ((h, TH), (ht, THT)):
         raw[n] = x[:, 0, :]
         raw[n + 2] = x[:, 1, :]
@@ -163,6 +166,30 @@
         geo[2 + e] = (1.0 / 12.0) / d[e]
         geo[5 + e] = 0.25 * d[e] * el[e]
     geo[8] = 1.0 / area[...]
+    for n, (e, r) in enumerate(RIM):
+        for x, t in ((v, 0), (vt, 1)):
+            raw[30 + 2 * n + t] = x[e, :, r % rows, :]
+
+    up = lambda x: pltpu.roll(x, rows - 1, 0)
+    dn = lambda x: pltpu.roll(x, 1, 0)
+    right = lambda x: pltpu.roll(x, x.shape[1] - 1, 1)
+    for lev in range(LV):
+        hh = [x[lev] for x in (h, ht)]
+        u = [[d[e] * x[e, lev] for x in (v, vt)] for e in range(3)]
+        h1 = [right(x) for x in hh]
+        u01 = [right(x) for x in u[0]]
+        n0 = [u[0][t] - u[1][t] + up(u[2][t]) for t in range(2)]
+        n1 = [u[1][t] - u[2][t] - dn(u01[t]) for t in range(2)]
+        d0 = [k[0, 0] * hh[t] + k[0, 1] * up(hh[t]) + k[0, 2] * h1[t] for t in range(2)]
+        d1 = [k[1, 0] * hh[t] + k[1, 1] * h1[t] + k[1, 2] * dn(h1[t]) for t in range(2)]
+        q0 = section_sums(geo[0] + n0[0], n0[1], *d0)
+        q1 = section_sums(geo[1] + n1[0], n1[1], *d1)
+        for t in range(2):
+            q[t, 0, lev] = q0[t]
+            q[t, 1, lev] = q1[t]
+        en = [energy(geo[5 + e], v[e, lev], vt[e, lev]) for e in range(3)]
+        zz = en[1] + row_up(en[2], 0.0)
+        kin[lev] = en[0] + en[1] + en[2] + row_down(en[0], 0.0) + right_shift(zz, 0.0)
 
 
 def af_row(k, f, a, r):
@@ -232,9 +259,7 @@
     ext[0, BASE : BASE + rows, :] = left
     ext[1, BASE : BASE + rows, :] = right
     ext[2, BASE : BASE + rows, :] = own0[...]
-    for n in range(3):
-        turned[n] = jnp.transpose(ext[n])
-    lt, rt, ot = (turned.at[n] for n in range(3))
+    lt, rt, ot = turn(turned, *(ext[n] for n in range(3)))
     q0l, q1l = column_left(lt, *(right_field(ot, n) for n in range(4)))
     q0r, q1r = column_right(rt)
     r0, r1 = BASE, BASE + 1
@@ -302,43 +327,94 @@
         store(msg_b, msg_a)
 
 
-(WQB, _, WQA, _, WMA, _, WMB, _, WE0, _, WF1, _, WEB, WEA) = range(14)
-(CY, _, CQ, CP, _) = range(5)
-
-
-def vertex_kernel(v, h, vt, ht, d, k, geo, slab_l, slab_r, q, kin):
-    left, right = slab_l[...], slab_r[...]
-    z = left + row_up(pltpu.roll(left, 128 - LV, 1), 0.0)
+(CY, _, CQ, CZ, CP, _, C0, _, C1, _) = range(10)
+(K00, _, K11, _, K0B, _, K1E, _, KM1, _, KMB, _, KMR, _) = range(14)
+
+
+def turn(turned, *slabs):
+    for n, x in enumerate(slabs):
+        turned[n] = jnp.transpose(x)
+    return [turned.at[n] for n in range(len(slabs))]
+
+
+def middle_kernel(v, vt, geo, q, kin, slab_l, slab_r, own_l, own_r, vertex, kinetic, cell, edge, keep, ext, turned):
+    rows = kin.shape[1]
+    end = rows - 1
+    for n, x in enumerate((slab_l, slab_r, own_l, own_r)):
+        ext[n, BASE : BASE + rows, :] = x[...]
+    lt, rt, ot, et = turn(turned, *(ext[n] for n in range(4)))
+    q0l, q1l = column_left(lt, *(right_field(ot, n) for n in range(4)))
+    q0r, q1r = column_right(rt)
+    q0c, q1c = column_left(et, *(right_field(rt, n) for n in range(4)))
+    up = lambda x: pltpu.roll(x, 127, 1)
+    dn = lambda x: pltpu.roll(x, 1, 1)
+    columns = [
+        q0l[0] + q1l[0] + up(q1l[0]),
+        q0l[1] + q1l[1] + up(q1l[1]),
+        up(q1l[0]),
+        lt[LEN : LEN + LV, :] + jnp.where(iota((LV, 128), 1) < BASE + end, up(lt[LEN + LV : LEN + 2 * LV, :]), 0.0),
+        q0r[0] + q1r[0] + dn(q0r[0]),
+        q0r[1] + q1r[1] + dn(q0r[1]),
+        *q0c,
+        *q1c,
+    ]
+    packed = jnp.concatenate(columns + [jnp.zeros((128 - LV * len(columns), 128), F32)], axis=0)
+    inject = jnp.transpose(packed)[BASE : BASE + rows, :]
+    side = iota(kin.shape[1:], 1)
     for lev in range(LV):
-        rcol = lambda n, lev=lev: right[:, 16 * n + 2 * lev : 16 * n + 2 * lev + 1]
-        hh = [x[lev] for x in (h, ht)]
-        u = [[d[e] * x[e, lev] for x in (v, vt)] for e in range(3)]
-        h1 = [left_shift(hh[t], rcol(t)) for t in range(2)]
-        u01 = [left_shift(u[0][t], rcol(2 + t)) for t in range(2)]
-        up = lambda x: pltpu.roll(x, x.shape[0] - 1, 0)
-        dn = lambda x: pltpu.roll(x, 1, 0)
-        n0 = [u[0][t] - u[1][t] + up(u[2][t]) for t in range(2)]
-        n1 = [u[1][t] - u[2][t] - dn(u01[t]) for t in range(2)]
-        d0 = [k[0, 0] * hh[t] + k[0, 1] * up(hh[t]) + k[0, 2] * h1[t] for t in range(2)]
-        d1 = [k[1, 0] * hh[t] + k[1, 1] * h1[t] + k[1, 2] * dn(h1[t]) for t in range(2)]
-        q0 = section_sums(geo[0] + n0[0], n0[1], *d0)
-        q1 = section_sums(geo[1] + n1[0], n1[1], *d1)
+        col = lambda n, lev=lev: inject[:, LV * n + lev : LV * n + lev + 1]
+        put = lambda n, x, r, lev=lev: keep.__setitem__((n, slice(lev, lev + 1), slice(None)), x[r : r + 1, :])
+        grads = []
         for t in range(2):
-            q[t, 0, lev] = q0[t]
-            q[t, 1, lev] = q1[t]
-        en = [energy(geo[5 + e], v[e, lev], vt[e, lev]) for e in range(3)]
-        zz = en[1] + row_up(en[2], 0.0)
-        zcol = z[:, LEN + lev : LEN + lev + 1]
-        kin[lev] = en[0] + en[1] + en[2] + row_down(en[0], 0.0) + right_shift(zz, zcol)
+            q0 = jnp.where(side == kin.shape[2] - 1, col(C0 + t), q[t, 0, lev])
+            q1 = jnp.where(side == kin.shape[2] - 1, col(C1 + t), q[t, 1, lev])
+            q0d = pltpu.roll(q0, 1, 0)
+            q1u = pltpu.roll(q1, end, 0)
+            both = q0 + q1
+            p, y = both + q0d, both + q1u
+            m = p + right_shift(y, col(CY + t))
+            m1 = left_shift(p, col(CP + t)) + y
+            grads.append((pltpu.roll(m, end, 0) - m, m1 - m, pltpu.roll(m1, 1, 0) - m))
+            put(K00 + t, q0, 0)
+            put(K11 + t, q1, 1)
+            put(K0B + t, q0, end - 1)
+            put(K1E + t, q1, end)
+            put(KM1 + t, m, 1)
+            put(KMB + t, m, end - 1)
+            put(KMR + t, m1, end - 1)
+            if t == 0:
+                cell[lev] = m * (1.0 / 6.0)
+                vertex[0, lev] = q0
+                vertex[1, lev] = q1
+                means = (q0 + right_shift(q1u, col(CQ)), both, q1 + q0d)
+        for e in range(3):
+            edge[e, lev] = 0.5 * means[e] - geo[2 + e] * (v[e, lev] * grads[0][e] + vt[e, lev] * grads[1][e])
+        kinetic[lev] = (kin[lev] + jnp.where(side == 0, col(CZ), 0.0)) * geo[8]
 
 
 def last_kernel(
-    v, vt, k, f, geo, slab_l, slab_r, own0, raw, q, kin, msg_a, msg_b,
-    vertex, kinetic, cell, edge, ext, turned, msgs, halo, vertex_v, kinetic_v, cell_v, edge_v, sems,
+    k, f, geo, slab_l, slab_r, own0, raw, keep, vertex_v, kinetic_v, cell_v, edge_v, msg_a, msg_b,
+    vertex, kinetic, cell, edge, ext, turned, msgs, rim, tiles, sems,
 ):
     odd_y = lax.rem(lax.axis_index("py"), 2) == 1
-    rows = kin.shape[1]
+    rows = kinetic_v.shape[1]
     end = rows - 1
+    arrays = (
+        [(vertex_v.at[n], vertex.at[n]) for n in range(2)]
+        + [(kinetic_v, kinetic), (cell_v, cell)]
+        + [(edge_v.at[n], edge.at[n]) for n in range(3)]
+    )
+    copies = []
+
+    def start(src, dst):
+        copy = pltpu.make_async_copy(src, dst, sems.at[len(copies)])
+        copy.start()
+        copies.append(copy)
+
+    top, bottom = slice(0, 8), slice(rows - 8, rows)
+    for n, (src, dst) in enumerate(arrays):
+        inner = slice(0 if n == 0 else 8, rows if n == 1 else rows - 8)
+        start(src.at[:, inner], dst.at[:, inner])
 
     @pl.when(odd_y)
     def _():
@@ -356,16 +432,12 @@
     kb = [msgs[1, 72 + n : 73 + n, :] for n in range(4)]
     krow = lambda a, b, r: k[a, b, r : r + 1, :]
 
-    left, right = slab_l[...], slab_r[...]
-    ext[0, BASE : BASE + rows, :] = left
-    ext[1, BASE : BASE + rows, :] = right
-    ext[2, BASE : BASE + rows, :] = own0[...]
+    for n, x in enumerate((slab_l, slab_r, own0)):
+        ext[n, BASE : BASE + rows, :] = x[...]
     ext[0, DNB : DNB + 1, :] = msgs[0, 76:77, 0:128]
     ext[1, DNB : DNB + 1, :] = msgs[0, 76:77, 128:256]
     ext[1, UPB : UPB + 1, :] = msgs[1, 76:77, 128:256]
-    for n in range(3):
-        turned[n] = jnp.transpose(ext[n])
-    lt, rt, ot = (turned.at[n] for n in range(3))
+    lt, rt, ot = turn(turned, *(ext[n] for n in range(3)))
     lanes = iota((LV, 128), 1)
     low = lambda x, row: jnp.where(lanes == UPB, row[:, 0:1], x)
     high = lambda x, row: jnp.where(lanes == DNB, row[:, 0:1], x)
@@ -375,15 +447,9 @@
     q0r, q1r = column_right(rt)
     up = lambda x: pltpu.roll(x, 127, 1)
     dn = lambda x: pltpu.roll(x, 1, 1)
-    cols_out = [
-        q0l[0] + q1l[0] + up(q1l[0]),
-        q0l[1] + q1l[1] + up(q1l[1]),
-        up(q1l[0]),
-        q0r[0] + q1r[0] + dn(q0r[0]),
-        q0r[1] + q1r[1] + dn(q0r[1]),
-    ]
-    packed = jnp.concatenate(cols_out + [jnp.zeros((128 - LV * len(cols_out), 128), F32)], axis=0)
-    inject = jnp.transpose(packed)[BASE : BASE + rows, :]
+    ycol = [q0l[t] + q1l[t] + up(q1l[t]) for t in range(2)]
+    pcol = [q0r[t] + q1r[t] + dn(q0r[t]) for t in range(2)]
+    r0, re = BASE, BASE + end
 
     hb1 = [left_shift(below(2 + t), lane_col(right_field(rt, t), UPB)) for t in range(2)]
     ub1 = [left_shift(below(4 + t), lane_col(right_field(rt, 2 + t), UPB)) for t in range(2)]
@@ -399,8 +465,8 @@
         *(krow(1, 0, 0) * raw[TH + t] + krow(1, 1, 0) * h01[t] + krow(1, 2, 0) * hb1[t] for t in range(2)),
     )
     ha1 = [left_shift(above(2 + t), lane_col(right_field(rt, t), DNB)) for t in range(2)]
-    he1 = [left_shift(raw[BH + t], lane_col(right_field(rt, t), BASE + end)) for t in range(2)]
-    ue1 = [left_shift(raw[BU0 + t], lane_col(right_field(rt, 2 + t), BASE + end)) for t in range(2)]
+    he1 = [left_shift(raw[BH + t], lane_col(right_field(rt, t), re)) for t in range(2)]
+    ue1 = [left_shift(raw[BU0 + t], lane_col(right_field(rt, 2 + t), re)) for t in range(2)]
     qa = section_sums(
         ka[3] + above(4) - above(6) - ue1[0],
         above(5) - above(7) - ue1[1],
@@ -411,54 +477,72 @@
         raw[BU0T] - raw[BU1T] + above(7),
         *(krow(0, 0, end) * raw[BH + t] + krow(0, 1, end) * above(2 + t) + krow(0, 2, end) * he1[t] for t in range(2)),
     )
+    grads = []
     for t in range(2):
-        halo[WQB + t] = qb[t]
-        halo[WQA + t] = qa[t]
-        halo[WMA + t] = above(t) + qa[t] + right_shift(qa[t], lane_col(q1l[t], DNB)) + q0e[t]
-        halo[WMB + t] = below(t) + qb[t] + left_shift(qb[t], lane_col(q0r[t], UPB)) + q1f[t]
-        halo[WE0 + t] = q0e[t]
-        halo[WF1 + t] = q1f[t]
-    halo[WEB] = below(8)
-    halo[WEA] = right_shift(above(8), lane_col(lt[LEN + LV : LEN + 2 * LV, :], DNB))
-
-    copies = []
-    for lev in range(LV):
-        row = lambda n, lev=lev: halo[n, lev : lev + 1, :]
-        col = lambda n, lev=lev: inject[:, LV * n + lev : LV * n + lev + 1]
-        spot = iota(kin.shape[1:], 0)
-        grads = []
-        for t in range(2):
-            q0 = jnp.where(spot == end, row(WE0 + t), q[t, 0, lev])
-            q1 = jnp.where(spot == 0, row(WF1 + t), q[t, 1, lev])
-            q0d = row_down(q0, row(WQB + t))
-            q1u = row_up(q1, row(WQA + t))
-            both = q0 + q1
-            p, y = both + q0d, both + q1u
-            m = p + right_shift(y, col(CY + t))
-            m1 = left_shift(p, col(CP + t)) + y
-            grads.append((row_up(m, row(WMA + t)) - m, m1 - m, row_down(m1, row(WMB + t)) - m))
-            if t == 0:
-                cell_v[lev] = m * (1.0 / 6.0)
-                vertex_v[0, lev] = q0
-                vertex_v[1, lev] = q1
-                means = (q0 + right_shift(q1u, col(CQ)), both, q1 + q0d)
-        for e in range(3):
-            edge_v[e, lev] = 0.5 * means[e] - geo[2 + e] * (v[e, lev] * grads[0][e] + vt[e, lev] * grads[1][e])
-        rim = jnp.where(spot == 0, row(WEB), 0.0) + jnp.where(spot == end, row(WEA), 0.0)
-        kinetic_v[lev] = (kin[lev] + rim) * geo[8]
-        for n, (src, dst) in enumerate(
+        p0, y0 = keep[K00 + t] + q1f[t] + qb[t], keep[K00 + t] + q1f[t] + keep[K11 + t]
+        pe, ye = q0e[t] + keep[K1E + t] + keep[K0B + t], q0e[t] + keep[K1E + t] + qa[t]
+        m0 = p0 + right_shift(y0, lane_col(ycol[t], r0))
+        m0r = left_shift(p0, lane_col(pcol[t], r0)) + y0
+        me = pe + right_shift(ye, lane_col(ycol[t], re))
+        mer = left_shift(pe, lane_col(pcol[t], re)) + ye
+        m_above = above(t) + qa[t] + right_shift(qa[t], lane_col(q1l[t], DNB)) + q0e[t]
+        m_below = below(t) + qb[t] + left_shift(qb[t], lane_col(q0r[t], UPB)) + q1f[t]
+        grads.append(
             (
-                (vertex_v.at[:, lev], vertex.at[:, lev]),
-                (kinetic_v.at[lev], kinetic.at[lev]),
-                (cell_v.at[lev], cell.at[lev]),
-                (edge_v.at[:, lev], edge.at[:, lev]),
+                keep[KM1 + t] - m0,
+                m0r - m0,
+                m_below - m0,
+                m0r - keep[KM1 + t],
+                me - keep[KMB + t],
+                m_above - me,
+                mer - me,
+                keep[KMR + t] - me,
             )
-        ):
-            copy = pltpu.make_async_copy(src, dst, sems.at[4 * lev + n])
-            copy.start()
-            copies.append(copy)
+        )
+        if t == 0:
+            rim[8] = q1f[0]
+            rim[9] = m0 * (1.0 / 6.0)
+            rim[10] = q0e[0]
+            rim[11] = me * (1.0 / 6.0)
+            means = (
+                keep[K00] + right_shift(keep[K11], lane_col(q1l[0], r0 + 1)),
+                keep[K00] + q1f[0],
+                q1f[0] + qb[0],
+                keep[K11] + keep[K00],
+                keep[K0B] + right_shift(keep[K1E], lane_col(q1l[0], re)),
+                q0e[0] + right_shift(qa[0], lane_col(q1l[0], DNB)),
+                q0e[0] + keep[K1E],
+                keep[K1E] + keep[K0B],
+            )
+    for n, (e, r) in enumerate(RIM):
+        r = r % rows
+        rim[n] = 0.5 * means[n] - geo[2 + e, r : r + 1, :] * (
+            raw[30 + 2 * n] * grads[0][n] + raw[31 + 2 * n] * grads[1][n]
+        )
+    rim[12] = below(8) * geo[8, 0:1, :]
+    rim[13] = right_shift(above(8), lane_col(lt[LEN + LV : LEN + 2 * LV, :], DNB)) * geo[8, end : end + 1, :]
+
+    spot = iota((8, kinetic_v.shape[2]), 0)
+    tile = 0
+    for part, patches in (
+        (top, ((1, ((0, 8),)), (2, ((0, 12),)), (3, ((0, 9),)), (4, ((0, 0),)), (5, ((0, 1),)), (6, ((0, 2), (1, 3))))),
+        (bottom, ((0, ((7, 10),)), (2, ((7, 13),)), (3, ((7, 11),)), (4, ((6, 4), (7, 5))), (5, ((7, 6),)), (6, ((7, 7),)))),
+    ):
+        for n, changes in patches:
+            src, dst = arrays[n]
+            for lev in range(LV):
+                x = src[lev, part, :]
+                for r, m in changes:
+                    new = rim[m, lev : lev + 1, :]
+                    x = jnp.where(spot == r, x + new if n == 2 else new, x)
+                tiles[tile, lev] = x
+            start(tiles.at[tile], dst.at[:, part])
+            tile += 1
     for copy in copies:
         copy.wait()
+
+
+LAST_COPIES = 7 + 12
 
 
 def shift(x, axis, by):
@@ -500,31 +584,36 @@
     send_right, send_left, *held = call(
         pack_kernel, args, [slab, slab] + [x.shape for x in args], sems=PACK_COPIES, hbm_in=True
     )
-    v, h, vt, ht, d, _, _, k, f = held
+    v, _, vt, _, _, _, _, k, f = held
     slab_l = shift(send_right, "px", 1)
     slab_r = shift(send_left, "px", -1)
-    raw, geo = call(prep_kernel, held, [(RAW, levels, cols), (9, rows, cols)], flops=20_000_000)
+    whole = [(2, levels, rows, cols), (levels, rows, cols), (levels, rows, cols), (3, levels, rows, cols)]
+    raw, geo, q, kin = call(
+        vertex_kernel,
+        held,
+        [(RAW, levels, cols), (9, rows, cols), (2, 2, levels, rows, cols), (levels, rows, cols)],
+        flops=40_000_000,
+    )
+    turned = [(4, 128, 128), (4, 128, 128)]
     msg_a, msg_b = call(
-        merge_kernel, [slab_l, slab_r, send_left, raw, k, f], [(80, cols), (80, cols)], [(3, 128, 128), (3, 128, 128)]
+        merge_kernel, [slab_l, slab_r, send_left, raw, k, f], [(80, cols), (80, cols)], turned
     )
     msg_b = swap(msg_b, "py", 1)
     msg_a = swap(msg_a, "py", 0)
-    q, kin = call(
-        vertex_kernel,
-        [v, h, vt, ht, d, k, geo, slab_l, slab_r],
-        [(2, 2, levels, rows, cols), (levels, rows, cols)],
+    *parts, keep = call(
+        middle_kernel,
+        [v, vt, geo, q, kin, slab_l, slab_r, send_left, send_right],
+        whole + [(14, levels, cols)],
+        turned,
         flops=40_000_000,
     )
     return tuple(
         call(
             last_kernel,
-            [v, vt, k, f, geo, slab_l, slab_r, send_left, raw, q, kin, msg_a, msg_b],
-            [(2, levels, rows, cols), (levels, rows, cols), (levels, rows, cols), (3, levels, rows, cols)],
-            [
-                (3, 128, 128), (3, 128, 128), (2, 80, cols), (14, levels, cols),
-                (2, levels, rows, cols), (levels, rows, cols), (levels, rows, cols), (3, levels, rows, cols),
-            ],
-            sems=4 * LV,
+            [k, f, geo, slab_l, slab_r, send_left, raw, keep, *parts, msg_a, msg_b],
+            whole,
+            turned + [(2, 80, cols), (14, levels, cols), (12, levels, 8, cols)],
+            sems=LAST_COPIES,
             hbm_out=True,
         )
     )

time: 21.1 us -> 19.7 us (0.934)
  waiting for transfers between devices: 2.32 us -> 0.43 us
  Pallas kernels: 7.03 us -> 7.54 us
    ppermute x2, waiting for transfers between devices: 1.51 us -> 0.31 us  [shift(): return lax.ppermute(x, axis, [(i, (i + by) % n) for i in range(n)])]
    ppermute x2, waiting for transfers between devices: 0.81 us -> 0.12 us  [swap(): return lax.ppermute(x, axis, pairs)]
    pallas_call x5, Pallas kernels: 7.03 us -> 7.54 us  [call(): pl.pallas_call(kernel, out_shape=[shape(s) for s in outs], in_specs=[ANY...]
  transfers between devices with their start and end apart: 4 -> 4, of which waited for: 2 -> 2; matrix products, arithmetic and copies ran while one was open for 0% -> 0% of each run, Pallas kernels for 7% -> 17%
where the time goes in v4:
time: 19.7 us; the launch traced here: 19.6 us
  starting transfers between devices  10.9 us (55%)
  Pallas kernels  7.54 us (38%)
  between operations  0.68 us (3%)
  waiting for transfers between devices  0.43 us (2%)
    pallas_call x5, Pallas kernels, call(): pl.pallas_call(kernel, out_shape=[shape(s) for s in outs], in_specs=[ANY...  7.54 us
    ppermute x2, starting transfers between devices, swap(): return lax.ppermute(x, axis, pairs)  6.53 us
    ppermute x2, starting transfers between devices, shift(): return lax.ppermute(x, axis, [(i, (i + by) % n) for i in range(n)])  4.37 us
  transfers between devices with their start and end apart: 4, of which 2 were waited for; matrix products, arithmetic and copies ran while one was open for 0% of the time, Pallas kernels for 17%

profile of v4, /device:TPU:0, one launch (start us, length us, event | category | flops | bytes accessed | tf_op | source)
XLA Modules:
  0.0 19.6 jit_solution(11764885625153274931)
XLA Ops:
  0.6 2.4 %shard_map.120 = (f32[32,128]{1,0:T(8,128)S(1)}, f32[32,128]{1,0:T(8,128)S(1)}, f32[3,8,32,256]{3,2,1,0:T(8,128)S(1)}, f32[8,32,256]{2,1,0:T(8,128)S(1)}, f32[3,...) custom-call(f32[3,8,32,256]{3,2,1,0:T(8,128)} %v.1, ...), custom_call_target="tpu_custom_call" | custom-call | tf_op jit(solution)/shard_map/pallas_call | solution.py:569
  3.0 2.1 %collective-permute-start = (f32[32,128]{1,0:T(8,128)S(1)}, f32[32,128]{1,0:T(8,128)S(1)}, u32[]{:S(2)}, u32[]{:S(2)}) collective-permute-start(f32[32,128]{1,0:T(8,128)S(1)} %get-tuple-element.36.own_r), channel_id=1, source_target_pairs={{0,16},{16,32},{32,48},{48,64},{64,80},{80,96},{96,112},{112,0},{1... | collective-permute-start | bytes 49160 | tf_op jit(solution)/shard_map/ppermute | solution.py:550
  5.1 2.3 %collective-permute-start.1 = (f32[32,128]{1,0:T(8,128)S(1)}, f32[32,128]{1,0:T(8,128)S(1)}, u32[]{:S(2)}, u32[]{:S(2)}) collective-permute-start(f32[32,128]{1,0:T(8,128)S(1)} %get-tuple-element.37.own_l.own0), channel_id=1, source_target_pairs={{0,112},{16,0},{32,16},{48,32},{64,48},{80,64},{96,80},{112,96},{1... | collective-permute-start | bytes 49160 | tf_op jit(solution)/shard_map/ppermute | solution.py:550
  7.4 1.3 %shard_map.121 = (f32[46,8,256]{2,1,0:T(8,128)S(1)}, f32[9,32,256]{2,1,0:T(8,128)S(1)}, f32[2,2,8,32,256]{4,3,2,1,0:T(8,128)S(1)}, f32[8,32,256]{2,1,0:T(8,128)S(1)}) custom-call(f32[3,8,32,256]{3,2,1,0:T(8,128)S(1)} %get-tuple-element.28.v, f32[8,32,256]{2,1,0:T(8,128)S(1)} %get-tuple-element.29.h, f32[3,8,32,256]{3,2,1,0:T(8,128)S(1)} %get-tuple-element.30.vt, ...), custom_call_target="tpu_custom_call" | custom-call | flops 40000000 | tf_op jit(solution)/shard_map/pallas_call | solution.py:569
  8.7 0.3 %collective-permute-done.slab_l = f32[32,128]{1,0:T(8,128)S(1)} collective-permute-done((f32[32,128]{1,0:T(8,128)S(1)}, f32[32,128]{1,0:T(8,128)S(1)}, u32[]{:S(2)}, u32[]{:S(2)}) %collective-permute-start) | collective-permute-done | bytes 16416 | tf_op jit(solution)/shard_map/ppermute | solution.py:550
  9.1 0.0 collective-permute-done.1.slab_r
  9.1 0.4 %shard_map.123 = (f32[80,256]{1,0:T(8,128)S(1)}, f32[80,256]{1,0:T(8,128)S(1)}) custom-call(f32[32,128]{1,0:T(8,128)S(1)} %collective-permute-done.slab_l, f32[32,128]{1,0:T(8,128)S(1)} %collective-permute-done.1.slab_r, f32[32,128]{1,0:T(8,128)S(1)} %get-tuple-element.37.own_l.own0, f32[46,8,256]{2,1,0:T(8,128)S(1)} %get-tuple-element.38.raw, ...), custom_call_target="tpu_custom_call" | custom-call | tf_op jit(solution)/shard_map/pallas_call | solution.py:569
  9.4 0.1 collective-permute-start.2
  9.5 6.4 %collective-permute-start.3 = (f32[80,256]{1,0:T(8,128)S(1)}, f32[80,256]{1,0:T(8,128)S(1)}, u32[]{:S(2)}, u32[]{:S(2)}) collective-permute-start(f32[80,256]{1,0:T(8,128)S(1)} %get-tuple-element.47), channel_id=1, source_target_pairs={{1,2},{2,1},{3,4},{4,3},{5,6},{6,5},{7,8},{8,7},{9,10},{10,9},{11,... | collective-permute-start | bytes 245768 | tf_op jit(solution)/shard_map/ppermute | solution.py:559
  16.0 2.0 %shard_map.122 = (f32[2,8,32,256]{3,2,1,0:T(8,128)S(1)}, f32[8,32,256]{2,1,0:T(8,128)S(1)}, f32[8,32,256]{2,1,0:T(8,128)S(1)}, f32[3,8,32,256]{3,2,1,0:T(8,128)S(1)}, f32[14,8,256]{2,1,0:T(8,128)S(1)}) custom-call(f32[3,8,32,256]{3,2,1,0:T(8,128)S(1)} %get-tuple-element.28.v, f32[3,8,32,256]{3,2,1,0:T(8,128)S(1)} %get-tuple-element.30.vt, ...), custom_call_target="tpu_custom_call" | custom-call | flops 40000000 | tf_op jit(solution)/shard_map/pallas_call | solution.py:569
  18.0 0.0 collective-permute-done.2.msg_a
  18.0 0.1 collective-permute-done.3.msg_b
  18.1 1.5 %shard_map.124 = (f32[2,8,32,256]{3,2,1,0:T(8,128)}, f32[8,32,256]{2,1,0:T(8,128)}, f32[8,32,256]{2,1,0:T(8,128)}, f32[3,8,32,256]{3,2,1,0:T(8,128)}) custom-call(f32[2,3,32,256]{3,2,1,0:T(8,128)S(1)} %get-tuple-element.26.k, f32[2,32,256]{2,1,0:T(8,128)S(1)} %get-tuple-element.27.f, f32[9,32,256]{2,1,0:T(8,128)S(1)} %get-tuple-element.35.geo, ...), custom_call_target="tpu_custom_call" | custom-call | tf_op jit(solution)/shard_map/pallas_call | solution.py:569
Async XLA Ops:
  3.0 6.0 %collective-permute-start = (f32[32,128]{1,0:T(8,128)S(1)}, f32[32,128]{1,0:T(8,128)S(1)}, u32[]{:S(2)}, u32[]{:S(2)}) collective-permute-start(f32[32,128]{1,0:T(8,128)S(1)} %get-tuple-element.36.own_r), channel_id=1, source_target_pairs={{0,16},{16,32},{32,48},{48,64},{64,80},{80,96},{96,112},{112,0},{1... | collective-permute-start | bytes 49160 | tf_op jit(solution)/shard_map/ppermute | solution.py:550
  5.1 3.9 %collective-permute-start.1 = (f32[32,128]{1,0:T(8,128)S(1)}, f32[32,128]{1,0:T(8,128)S(1)}, u32[]{:S(2)}, u32[]{:S(2)}) collective-permute-start(f32[32,128]{1,0:T(8,128)S(1)} %get-tuple-element.37.own_l.own0), channel_id=1, source_target_pairs={{0,112},{16,0},{32,16},{48,32},{64,48},{80,64},{96,80},{112,96},{1... | collective-permute-start | bytes 49160 | tf_op jit(solution)/shard_map/ppermute | solution.py:550
  9.4 8.5 %collective-permute-start.2 = (f32[80,256]{1,0:T(8,128)S(1)}, f32[80,256]{1,0:T(8,128)S(1)}, u32[]{:S(2)}, u32[]{:S(2)}) collective-permute-start(f32[80,256]{1,0:T(8,128)S(1)} %get-tuple-element.46), channel_id=1, source_target_pairs={{0,1},{1,0},{2,3},{3,2},{4,5},{5,4},{6,7},{7,6},{8,9},{9,8},{10,11... | collective-permute-start | bytes 245768 | tf_op jit(solution)/shard_map/ppermute | solution.py:559
  9.5 8.6 %collective-permute-start.3 = (f32[80,256]{1,0:T(8,128)S(1)}, f32[80,256]{1,0:T(8,128)S(1)}, u32[]{:S(2)}, u32[]{:S(2)}) collective-permute-start(f32[80,256]{1,0:T(8,128)S(1)} %get-tuple-element.47), channel_id=1, source_target_pairs={{1,2},{2,1},{3,4},{4,3},{5,6},{6,5},{7,8},{8,7},{9,10},{10,9},{11,... | collective-permute-start | bytes 245768 | tf_op jit(solution)/shard_map/ppermute | solution.py:559

commit v5 on v4

--- a/solution.py
+++ b/solution.py
@@ -1,3 +1,5 @@
+import functools
+
 import jax
 import jax.numpy as jnp
 from jax import lax
@@ -51,8 +53,8 @@
 
 RGEO = 96
 LGEO, LEN, LFLD = 40, 48, 64
-(TH, THT, TH1, _, TU0, TU0T, TU1, TU1T, TU11, TU11T, TU2, TU2T, TU21, TU21T, TE2) = range(15)
-(BH, BHT, BH1, _, BU0, BU0T, BU01, BU01T, BU1, BU1T, BU11, BU11T, BU2, BU2T, BE0) = range(15, 30)
+(TH, THT, TH1, _, TU0, TU0T, TU1, TU1T, TU11, TU11T, TU2, TU2T, TU21, TU21T, TG2) = range(15)
+(BH, BHT, BH1, _, BU0, BU0T, BU01, BU01T, BU1, BU1T, BU11, BU11T, BU2, BU2T, BG0) = range(15, 30)
 RIM = ((0, 0), (1, 0), (2, 0), (2, 1), (0, -2), (0, -1), (1, -1), (2, -1))
 RAW = 30 + 2 * len(RIM)
 
@@ -135,7 +137,7 @@
 PACK_COPIES = 4 + 4 * 2 + 1
 
 
-def vertex_kernel(v, h, vt, ht, d, el, area, k, f, raw, geo, q, kin):
+def vertex_kernel(v, h, vt, ht, d, el, area, k, f, raw, geo, q):
     rows = h.shape[1]
     end = rows - 1
     for x, n in ((h, TH), (ht, THT)):
@@ -158,8 +160,8 @@
             (2, end, BU2),
         ):
             raw[n + t] = d[e, r : r + 1, :] * x[e, :, r, :]
-    raw[TE2] = energy(0.25 * d[2, 0:1, :] * el[2, 0:1, :], v[2, :, 0, :], vt[2, :, 0, :])
-    raw[BE0] = energy(0.25 * d[0, end : end + 1, :] * el[0, end : end + 1, :], v[0, :, end, :], vt[0, :, end, :])
+    for e, r, n in ((2, 0, TG2), (0, end, BG0)):
+        raw[n] = jnp.broadcast_to(0.25 * el[e, r : r + 1, :] / d[e, r : r + 1, :], raw.shape[1:])
     for a in range(2):
         geo[a] = (k[a, 0] + k[a, 1] + k[a, 2]) * f[a]
     for e in range(3):
@@ -187,9 +189,6 @@
         for t in range(2):
             q[t, 0, lev] = q0[t]
             q[t, 1, lev] = q1[t]
-        en = [energy(geo[5 + e], v[e, lev], vt[e, lev]) for e in range(3)]
-        zz = en[1] + row_up(en[2], 0.0)
-        kin[lev] = en[0] + en[1] + en[2] + row_down(en[0], 0.0) + right_shift(zz, 0.0)
 
 
 def af_row(k, f, a, r):
@@ -305,18 +304,20 @@
 
     def store(msg_up, msg_down):
         for msg, sums, parts, geo, r in (
-            (msg_up, up, (TH, THT, TU1, TU1T, TU2, TU2T, TE2), 1, 0),
-            (msg_down, down, (BH, BHT, BU0, BU0T, BU1, BU1T, BE0), 0, end),
+            (msg_up, up, (TH, THT, TU1, TU1T, TU2, TU2T, TG2), 1, 0),
+            (msg_down, down, (BH, BHT, BU0, BU0T, BU1, BU1T, BG0), 0, end),
         ):
             for n in range(2):
                 msg[LV * n : LV * n + LV, :] = sums[n]
-            for n, part in enumerate(parts):
+            for n, part in enumerate(parts[:6]):
                 msg[LV * (n + 2) : LV * (n + 3), :] = raw[part]
             for n in range(3):
-                msg[72 + n : 73 + n, :] = krow(geo, n, r)
-            msg[75:76, :] = af_row(k, f, geo, r)
-            msg[76:77, 0:128] = left[r : r + 1, :]
-            msg[76:77, 128:256] = right[r : r + 1, :]
+                msg[64 + n : 65 + n, :] = krow(geo, n, r)
+            msg[67:68, :] = af_row(k, f, geo, r)
+            msg[68:69, 0:128] = left[r : r + 1, :]
+            msg[68:69, 128:256] = right[r : r + 1, :]
+            msg[69:70, :] = raw[parts[6], 0:1, :]
+            msg[70:72, :] = jnp.zeros((2, msg.shape[1]), F32)
 
     @pl.when(odd_y)
     def _():
@@ -337,8 +338,14 @@
     return [turned.at[n] for n in range(len(slabs))]
 
 
-def middle_kernel(v, vt, geo, q, kin, slab_l, slab_r, own_l, own_r, vertex, kinetic, cell, edge, keep, ext, turned):
-    rows = kin.shape[1]
+def middle_kernel(parity, *refs):
+    @pl.when(lax.rem(lax.axis_index("py"), 2) == parity)
+    def _():
+        middle(*refs[:8], *refs[-7:])
+
+
+def middle(v, vt, geo, q, slab_l, slab_r, own_l, own_r, vertex, kinetic, cell, edge, keep, ext, turned):
+    rows = kinetic.shape[1]
     end = rows - 1
     for n, x in enumerate((slab_l, slab_r, own_l, own_r)):
         ext[n, BASE : BASE + rows, :] = x[...]
@@ -360,14 +367,18 @@
     ]
     packed = jnp.concatenate(columns + [jnp.zeros((128 - LV * len(columns), 128), F32)], axis=0)
     inject = jnp.transpose(packed)[BASE : BASE + rows, :]
-    side = iota(kin.shape[1:], 1)
+    moving = [pltpu.roll(inject, ((0 if n <= CZ else 127) - LV * n) % 128, 1) for n in range(len(columns))]
+    side = iota(kinetic.shape[1:], 1)
+    final = kinetic.shape[2] - 1
     for lev in range(LV):
-        col = lambda n, lev=lev: inject[:, LV * n + lev : LV * n + lev + 1]
+        if lev:
+            moving = [pltpu.roll(x, 127, 1) for x in moving]
+        col = lambda n: jnp.concatenate([moving[n]] * 2, axis=1)
         put = lambda n, x, r, lev=lev: keep.__setitem__((n, slice(lev, lev + 1), slice(None)), x[r : r + 1, :])
         grads = []
         for t in range(2):
-            q0 = jnp.where(side == kin.shape[2] - 1, col(C0 + t), q[t, 0, lev])
-            q1 = jnp.where(side == kin.shape[2] - 1, col(C1 + t), q[t, 1, lev])
+            q0 = jnp.where(side == final, col(C0 + t), q[t, 0, lev])
+            q1 = jnp.where(side == final, col(C1 + t), q[t, 1, lev])
             q0d = pltpu.roll(q0, 1, 0)
             q1u = pltpu.roll(q1, end, 0)
             both = q0 + q1
@@ -389,7 +400,9 @@
                 means = (q0 + right_shift(q1u, col(CQ)), both, q1 + q0d)
         for e in range(3):
             edge[e, lev] = 0.5 * means[e] - geo[2 + e] * (v[e, lev] * grads[0][e] + vt[e, lev] * grads[1][e])
-        kinetic[lev] = (kin[lev] + jnp.where(side == 0, col(CZ), 0.0)) * geo[8]
+        en = [energy(geo[5 + e], v[e, lev], vt[e, lev]) for e in range(3)]
+        zz = right_shift(en[1] + row_up(en[2], 0.0), col(CZ))
+        kinetic[lev] = (en[0] + en[1] + en[2] + row_down(en[0], 0.0) + zz) * geo[8]
 
 
 def last_kernel(
@@ -428,15 +441,15 @@
 
     above = lambda n: msgs[0, LV * n : LV * n + LV, :]
     below = lambda n: msgs[1, LV * n : LV * n + LV, :]
-    ka = [msgs[0, 72 + n : 73 + n, :] for n in range(4)]
-    kb = [msgs[1, 72 + n : 73 + n, :] for n in range(4)]
+    ka = [msgs[0, 64 + n : 65 + n, :] for n in range(4)]
+    kb = [msgs[1, 64 + n : 65 + n, :] for n in range(4)]
     krow = lambda a, b, r: k[a, b, r : r + 1, :]
 
     for n, x in enumerate((slab_l, slab_r, own0)):
         ext[n, BASE : BASE + rows, :] = x[...]
-    ext[0, DNB : DNB + 1, :] = msgs[0, 76:77, 0:128]
-    ext[1, DNB : DNB + 1, :] = msgs[0, 76:77, 128:256]
-    ext[1, UPB : UPB + 1, :] = msgs[1, 76:77, 128:256]
+    ext[0, DNB : DNB + 1, :] = msgs[0, 68:69, 0:128]
+    ext[1, DNB : DNB + 1, :] = msgs[0, 68:69, 128:256]
+    ext[1, UPB : UPB + 1, :] = msgs[1, 68:69, 128:256]
     lt, rt, ot = turn(turned, *(ext[n] for n in range(3)))
     lanes = iota((LV, 128), 1)
     low = lambda x, row: jnp.where(lanes == UPB, row[:, 0:1], x)
@@ -519,8 +532,8 @@
         rim[n] = 0.5 * means[n] - geo[2 + e, r : r + 1, :] * (
             raw[30 + 2 * n] * grads[0][n] + raw[31 + 2 * n] * grads[1][n]
         )
-    rim[12] = below(8) * geo[8, 0:1, :]
-    rim[13] = right_shift(above(8), lane_col(lt[LEN + LV : LEN + 2 * LV, :], DNB)) * geo[8, end : end + 1, :]
+    rim[12] = energy(msgs[1, 69:70, :], below(4), below(5)) * geo[8, 0:1, :]
+    rim[13] = right_shift(energy(msgs[0, 69:70, :], above(6), above(7)), lane_col(lt[LEN + LV : LEN + 2 * LV, :], DNB)) * geo[8, end : end + 1, :]
 
     spot = iota((8, kinetic_v.shape[2]), 0)
     tile = 0
@@ -563,7 +576,7 @@
 ANY = pl.BlockSpec(memory_space=pl.ANY)
 
 
-def call(kernel, args, outs, scratch=(), sems=0, hbm_in=False, hbm_out=False, flops=0):
+def call(kernel, args, outs, scratch=(), sems=0, hbm_in=False, hbm_out=False, flops=0, alias=None):
     args = [pltpu.with_memory_space_constraint(x, pltpu.HBM if hbm_in else pltpu.VMEM) for x in args]
     shape = (lambda s: jax.ShapeDtypeStruct(s, F32)) if hbm_out else (lambda s: pltpu.VMEM(s, F32))
     return pl.pallas_call(
@@ -573,6 +586,7 @@
         out_specs=[ANY if hbm_out else VM] * len(outs),
         scratch_shapes=[pltpu.VMEM(s, F32) for s in scratch]
         + ([pltpu.SemaphoreType.DMA((sems,))] if sems else []),
+        input_output_aliases=alias or {},
         compiler_params=pltpu.CompilerParams(vmem_limit_bytes=16 * 2**20),
         cost_estimate=pl.CostEstimate(flops=flops, transcendentals=0, bytes_accessed=0) if flops else None,
     )(*args)
@@ -588,31 +602,35 @@
     slab_l = shift(send_right, "px", 1)
     slab_r = shift(send_left, "px", -1)
     whole = [(2, levels, rows, cols), (levels, rows, cols), (levels, rows, cols), (3, levels, rows, cols)]
-    raw, geo, q, kin = call(
+    raw, geo, q = call(
         vertex_kernel,
         held,
-        [(RAW, levels, cols), (9, rows, cols), (2, 2, levels, rows, cols), (levels, rows, cols)],
+        [(RAW, levels, cols), (9, rows, cols), (2, 2, levels, rows, cols)],
         flops=40_000_000,
     )
     turned = [(4, 128, 128), (4, 128, 128)]
     msg_a, msg_b = call(
-        merge_kernel, [slab_l, slab_r, send_left, raw, k, f], [(80, cols), (80, cols)], turned
+        merge_kernel, [slab_l, slab_r, send_left, raw, k, f], [(72, cols), (72, cols)], turned
     )
     msg_b = swap(msg_b, "py", 1)
     msg_a = swap(msg_a, "py", 0)
+    sources = [v, vt, geo, q, slab_l, slab_r, send_left, send_right]
+    results = whole + [(14, levels, cols)]
+    parts = call(functools.partial(middle_kernel, 1), sources, results, turned, flops=40_000_000)
     *parts, keep = call(
-        middle_kernel,
-        [v, vt, geo, q, kin, slab_l, slab_r, send_left, send_right],
-        whole + [(14, levels, cols)],
+        functools.partial(middle_kernel, 0),
+        [*sources, *parts],
+        results,
         turned,
         flops=40_000_000,
+        alias={len(sources) + n: n for n in range(5)},
     )
     return tuple(
         call(
             last_kernel,
             [k, f, geo, slab_l, slab_r, send_left, raw, keep, *parts, msg_a, msg_b],
             whole,
-            turned + [(2, 80, cols), (14, levels, cols), (12, levels, 8, cols)],
+            turned + [(2, 72, cols), (14, levels, cols), (12, levels, 8, cols)],
             sems=LAST_COPIES,
             hbm_out=True,
         )

time: 19.7 us -> 19.6 us (level)
  Pallas kernels: 7.54 us -> 6.69 us
  waiting for transfers between devices: 0.43 us -> 1.2 us
    pallas_call x5 -> x6, Pallas kernels: 7.54 us -> 6.69 us  [call(): pl.pallas_call(kernel, out_shape=[shape(s) for s in outs], in_specs=[ANY...]
    ppermute x2, waiting for transfers between devices: 0.12 us -> 0.63 us  [swap(): return lax.ppermute(x, axis, pairs)]
    ppermute x2, waiting for transfers between devices: 0.31 us -> 0.57 us  [shift(): return lax.ppermute(x, axis, [(i, (i + by) % n) for i in range(n)])]
  transfers between devices with their start and end apart: 4 -> 4, of which waited for: 2 -> 2; matrix products, arithmetic and copies ran while one was open for 0% -> 0% of each run, Pallas kernels for 17% -> 13%
where the time goes in v5:
time: 19.6 us; the launch traced here: 19.5 us
  starting transfers between devices  10.9 us (56%)
  Pallas kernels  6.69 us (34%)
  waiting for transfers between devices  1.2 us (6%)
  between operations  0.68 us (3%)
    pallas_call x6, Pallas kernels, call(): pl.pallas_call(kernel, out_shape=[shape(s) for s in outs], in_specs=[ANY...  6.69 us
    ppermute x2, starting transfers between devices, swap(): return lax.ppermute(x, axis, pairs)  6.53 us
    ppermute x2, starting transfers between devices, shift(): return lax.ppermute(x, axis, [(i, (i + by) % n) for i in range(n)])  4.37 us
    ppermute x2, waiting for transfers between devices, swap(): return lax.ppermute(x, axis, pairs)  0.63 us
    ppermute x2, waiting for transfers between devices, shift(): return lax.ppermute(x, axis, [(i, (i + by) % n) for i in range(n)])  0.57 us
  transfers between devices with their start and end apart: 4, of which 2 were waited for; matrix products, arithmetic and copies ran while one was open for 0% of the time, Pallas kernels for 13%

profile of v5, /device:TPU:0, one launch (start us, length us, event | category | flops | bytes accessed | tf_op | source)
XLA Modules:
  0.0 19.5 jit_solution(9213485638318420893)
XLA Ops:
  0.6 2.4 %shard_map.120 = (f32[32,128]{1,0:T(8,128)S(1)}, f32[32,128]{1,0:T(8,128)S(1)}, f32[3,8,32,256]{3,2,1,0:T(8,128)S(1)}, f32[8,32,256]{2,1,0:T(8,128)S(1)}, f32[3,...) custom-call(f32[3,8,32,256]{3,2,1,0:T(8,128)} %v.1, ...), custom_call_target="tpu_custom_call" | custom-call | tf_op jit(solution)/shard_map/pallas_call | solution.py:582
  3.0 2.1 %collective-permute-start = (f32[32,128]{1,0:T(8,128)S(1)}, f32[32,128]{1,0:T(8,128)S(1)}, u32[]{:S(2)}, u32[]{:S(2)}) collective-permute-start(f32[32,128]{1,0:T(8,128)S(1)} %get-tuple-element.40.refs_7_), channel_id=1, source_target_pairs={{0,16},{16,32},{32,48},{48,64},{64,80},{80,96},{96,112},{112,0},{1... | collective-permute-start | bytes 49160 | tf_op jit(solution)/shard_map/ppermute | solution.py:563
  5.1 2.3 %collective-permute-start.1 = (f32[32,128]{1,0:T(8,128)S(1)}, f32[32,128]{1,0:T(8,128)S(1)}, u32[]{:S(2)}, u32[]{:S(2)}) collective-permute-start(f32[32,128]{1,0:T(8,128)S(1)} %get-tuple-element.41.refs_6_.own0), channel_id=1, source_target_pairs={{0,112},{16,0},{32,16},{48,32},{64,48},{80,64},{96,80},{112,96},{1... | collective-permute-start | bytes 49160 | tf_op jit(solution)/shard_map/ppermute | solution.py:563
  7.4 1.1 %shard_map.121 = (f32[46,8,256]{2,1,0:T(8,128)S(1)}, f32[9,32,256]{2,1,0:T(8,128)S(1)}, f32[2,2,8,32,256]{4,3,2,1,0:T(8,128)S(1)}) custom-call(f32[3,8,32,256]{3,2,1,0:T(8,128)S(1)} %get-tuple-element.32.v.refs_0_, f32[8,32,256]{2,1,0:T(8,128)S(1)} %get-tuple-element.33.h, f32[3,8,32,256]{3,2,1,0:T(8,128)S(1)} %get-tuple-element.34.vt.refs_1_, ...), custom_call_target="tpu_custom_call" | custom-call | flops 40000000 | tf_op jit(solution)/shard_map/pallas_call | solution.py:582
  8.5 0.6 %collective-permute-done.refs_4_.slab_l = f32[32,128]{1,0:T(8,128)S(1)} collective-permute-done((f32[32,128]{1,0:T(8,128)S(1)}, f32[32,128]{1,0:T(8,128)S(1)}, u32[]{:S(2)}, u32[]{:S(2)}) %collective-permute-start) | collective-permute-done | bytes 16416 | tf_op jit(solution)/shard_map/ppermute | solution.py:563
  9.1 0.0 collective-permute-done.1.refs_5_.slab_r
  9.1 0.4 %shard_map.124 = (f32[72,256]{1,0:T(8,128)S(1)}, f32[72,256]{1,0:T(8,128)S(1)}) custom-call(f32[32,128]{1,0:T(8,128)S(1)} %collective-permute-done.refs_4_.slab_l, f32[32,128]{1,0:T(8,128)S(1)} %collective-permute-done.1.refs_5_.slab_r, f32[32,128]{1,0:T(8,128)S(1)} %get-tuple-element.41.refs_6_.own0, f32[46,8,256]{2,1,0:T(8,128)S(1)} %get-tuple-element.42.raw, ...), custom_call_target="tpu_custom_call" | custom-call | tf_op jit(solution)/shard_map/pallas_call | solution.py:582
  9.4 0.1 collective-permute-start.2
  9.5 6.4 %collective-permute-start.3 = (f32[72,256]{1,0:T(8,128)S(1)}, f32[72,256]{1,0:T(8,128)S(1)}, u32[]{:S(2)}, u32[]{:S(2)}) collective-permute-start(f32[72,256]{1,0:T(8,128)S(1)} %get-tuple-element.55), channel_id=1, source_target_pairs={{1,2},{2,1},{3,4},{4,3},{5,6},{6,5},{7,8},{8,7},{9,10},{10,9},{11,... | collective-permute-start | bytes 221192 | tf_op jit(solution)/shard_map/ppermute | solution.py:572
  16.0 1.4 %shard_map.123 = (f32[2,8,32,256]{3,2,1,0:T(8,128)S(1)}, f32[8,32,256]{2,1,0:T(8,128)S(1)}, f32[8,32,256]{2,1,0:T(8,128)S(1)}, f32[3,8,32,256]{3,2,1,0:T(8,128)S(1)}, f32[14,8,256]{2,1,0:T(8,128)S(1)}) custom-call(f32[3,8,32,256]{3,2,1,0:T(8,128)S(1)} %get-tuple-element.32.v.refs_0_, ...), custom_call_target="tpu_custom_call", output_to_operand_aliasing={{0}: (8, {}), {1}: (9, {}), {2}: (10, {}), {3}: (11, {}), {... | custom-call | flops 40000000 | tf_op jit(solution)/shard_map/pallas_call | solution.py:582
  17.4 0.0 collective-permute-done.2.msg_a
  17.4 0.6 %collective-permute-done.3.msg_b = f32[72,256]{1,0:T(8,128)S(1)} collective-permute-done((f32[72,256]{1,0:T(8,128)S(1)}, f32[72,256]{1,0:T(8,128)S(1)}, u32[]{:S(2)}, u32[]{:S(2)}) %collective-permute-start.3) | collective-permute-done | bytes 73760 | tf_op jit(solution)/shard_map/ppermute | solution.py:572
  18.0 1.5 %shard_map.125 = (f32[2,8,32,256]{3,2,1,0:T(8,128)}, f32[8,32,256]{2,1,0:T(8,128)}, f32[8,32,256]{2,1,0:T(8,128)}, f32[3,8,32,256]{3,2,1,0:T(8,128)}) custom-call(f32[2,3,32,256]{3,2,1,0:T(8,128)S(1)} %get-tuple-element.30.k, f32[2,32,256]{2,1,0:T(8,128)S(1)} %get-tuple-element.31.f, f32[9,32,256]{2,1,0:T(8,128)S(1)} %get-tuple-element.39.refs_2_.geo, ...), custom_call_target="tpu_custom_call" | custom-call | tf_op jit(solution)/shard_map/pallas_call | solution.py:582
  (1 shorter events, 0.0 us)
Async XLA Ops:
  3.0 6.0 %collective-permute-start = (f32[32,128]{1,0:T(8,128)S(1)}, f32[32,128]{1,0:T(8,128)S(1)}, u32[]{:S(2)}, u32[]{:S(2)}) collective-permute-start(f32[32,128]{1,0:T(8,128)S(1)} %get-tuple-element.40.refs_7_), channel_id=1, source_target_pairs={{0,16},{16,32},{32,48},{48,64},{64,80},{80,96},{96,112},{112,0},{1... | collective-permute-start | bytes 49160 | tf_op jit(solution)/shard_map/ppermute | solution.py:563
  5.1 3.9 %collective-permute-start.1 = (f32[32,128]{1,0:T(8,128)S(1)}, f32[32,128]{1,0:T(8,128)S(1)}, u32[]{:S(2)}, u32[]{:S(2)}) collective-permute-start(f32[32,128]{1,0:T(8,128)S(1)} %get-tuple-element.41.refs_6_.own0), channel_id=1, source_target_pairs={{0,112},{16,0},{32,16},{48,32},{64,48},{80,64},{96,80},{112,96},{1... | collective-permute-start | bytes 49160 | tf_op jit(solution)/shard_map/ppermute | solution.py:563
  9.4 7.9 %collective-permute-start.2 = (f32[72,256]{1,0:T(8,128)S(1)}, f32[72,256]{1,0:T(8,128)S(1)}, u32[]{:S(2)}, u32[]{:S(2)}) collective-permute-start(f32[72,256]{1,0:T(8,128)S(1)} %get-tuple-element.54), channel_id=1, source_target_pairs={{0,1},{1,0},{2,3},{3,2},{4,5},{5,4},{6,7},{7,6},{8,9},{9,8},{10,11... | collective-permute-start | bytes 221192 | tf_op jit(solution)/shard_map/ppermute | solution.py:572
  9.5 8.5 %collective-permute-start.3 = (f32[72,256]{1,0:T(8,128)S(1)}, f32[72,256]{1,0:T(8,128)S(1)}, u32[]{:S(2)}, u32[]{:S(2)}) collective-permute-start(f32[72,256]{1,0:T(8,128)S(1)} %get-tuple-element.55), channel_id=1, source_target_pairs={{1,2},{2,1},{3,4},{4,3},{5,6},{6,5},{7,8},{8,7},{9,10},{10,9},{11,... | collective-permute-start | bytes 221192 | tf_op jit(solution)/shard_map/ppermute | solution.py:572

commit v6 on v5

--- a/solution.py
+++ b/solution.py
@@ -11,6 +11,7 @@
 LV = 8
 BASE = 8
 UPB, DNB = BASE - 1, BASE + 32
+OWN = 64
 
 
 def iota(shape, dim):
@@ -53,10 +54,11 @@
 
 RGEO = 96
 LGEO, LEN, LFLD = 40, 48, 64
-(TH, THT, TH1, _, TU0, TU0T, TU1, TU1T, TU11, TU11T, TU2, TU2T, TU21, TU21T, TG2) = range(15)
-(BH, BHT, BH1, _, BU0, BU0T, BU01, BU01T, BU1, BU1T, BU11, BU11T, BU2, BU2T, BG0) = range(15, 30)
+(TH, THT, _, _, TU0, _, TU1, TU1T, TU11, _, TU2, TU2T, TU21, _, TG2) = range(15)
+(BH, BHT, _, _, BU0, BU0T, BU01, _, BU1, BU1T, BU11, _, BU2, _, BG0) = range(15, 30)
 RIM = ((0, 0), (1, 0), (2, 0), (2, 1), (0, -2), (0, -1), (1, -1), (2, -1))
-RAW = 30 + 2 * len(RIM)
+QROW = 30 + 2 * len(RIM)
+RAW = QROW + 8
 
 
 def pack_kernel(
@@ -137,7 +139,7 @@
 PACK_COPIES = 4 + 4 * 2 + 1
 
 
-def vertex_kernel(v, h, vt, ht, d, el, area, k, f, raw, geo, q):
+def vertex_kernel(v, h, vt, ht, d, el, area, k, f, raw, geo, q, msg_a, msg_b):
     rows = h.shape[1]
     end = rows - 1
     for x, n in ((h, TH), (ht, THT)):
@@ -189,6 +191,35 @@
         for t in range(2):
             q[t, 0, lev] = q0[t]
             q[t, 1, lev] = q1[t]
+            for n, x, r in ((0, q0, 0), (1, q1, 1), (2, q1, end), (3, q0, end - 1)):
+                raw[QROW + 2 * n + t, lev : lev + 1, :] = x[t][r : r + 1, :]
+
+    def fill(msg_up, msg_down):
+        for msg, parts, a, r in (
+            (msg_up, (TH, THT, TU1, TU1T, TU2, TU2T), 1, 0),
+            (msg_down, (BH, BHT, BU0, BU0T, BU1, BU1T), 0, end),
+        ):
+            for n, part in enumerate(parts):
+                msg[LV * (n + 2) : LV * (n + 3), :] = raw[part]
+            for n in range(3):
+                msg[64 + n : 65 + n, :] = k[a, n, r : r + 1, :]
+            msg[67:68, :] = af_row(k, f, a, r)
+            msg[69:70, :] = raw[BG0 if r else TG2, 0:1, :]
+            msg[70:72, :] = jnp.zeros((2, msg.shape[1]), F32)
+
+    by_parity(fill, msg_a, msg_b)
+
+
+def by_parity(body, first, second):
+    odd = lax.rem(lax.axis_index("py"), 2) == 1
+
+    @pl.when(odd)
+    def _():
+        body(first, second)
+
+    @pl.when(jnp.logical_not(odd))
+    def _():
+        body(second, first)
 
 
 def af_row(k, f, a, r):
@@ -246,86 +277,47 @@
     return q0, q1
 
 
-def lane_col(x, lane):
-    return x[:, lane : lane + 1]
-
-
-def merge_kernel(slab_l, slab_r, own0, raw, k, f, msg_a, msg_b, ext, turned):
-    odd_y = lax.rem(lax.axis_index("py"), 2) == 1
+def moved(x, lane, to):
+    y = pltpu.roll(x, (to - lane) % 128, 1) if to != lane else x
+    return jnp.concatenate([y, y], axis=1)
+
+
+def last_lane(x, lane):
+    return moved(x, lane, 127)
+
+
+def first_lane(x, lane):
+    return moved(x, lane, 0)
+
+
+def merge_kernel(slab_l, slab_r, own_l, own_r, raw, old_a, old_b, msg_a, msg_b, ext, turned):
     rows = slab_l.shape[0]
-    end = rows - 1
-    left, right = slab_l[...], slab_r[...]
-    ext[0, BASE : BASE + rows, :] = left
-    ext[1, BASE : BASE + rows, :] = right
-    ext[2, BASE : BASE + rows, :] = own0[...]
-    lt, rt, ot = turn(turned, *(ext[n] for n in range(3)))
-    q0l, q1l = column_left(lt, *(right_field(ot, n) for n in range(4)))
+    for n, pair in enumerate(((slab_l, own_r), (own_l, slab_r))):
+        for m, x in enumerate(pair):
+            ext[n, 16 * m : 16 * m + 8, :] = x[0:8, :]
+            ext[n, 16 * m + 8 : 16 * m + 16, :] = x[rows - 8 : rows, :]
+    lt, rt = turn(turned, ext[0], ext[1])
+    q0, q1 = column_left(lt, *(right_field(rt, n) for n in range(4)))
     q0r, q1r = column_right(rt)
-    r0, r1 = BASE, BASE + 1
-    e0, e1 = BASE + end, BASE + end - 1
-    krow = lambda a, b, r: k[a, b, r : r + 1, :]
-
-    h_0 = [left_shift(raw[TH + t], lane_col(right_field(rt, t), r0)) for t in range(2)]
-    h_1 = [left_shift(raw[TH1 + t], lane_col(right_field(rt, t), r1)) for t in range(2)]
-    u_0 = [left_shift(raw[TU0 + t], lane_col(right_field(rt, 2 + t), r0)) for t in range(2)]
-    up0 = section_sums(
-        af_row(k, f, 0, 0) + raw[TU0] - raw[TU1] + raw[TU21],
-        raw[TU0T] - raw[TU1T] + raw[TU21T],
-        *(krow(0, 0, 0) * raw[TH + t] + krow(0, 1, 0) * raw[TH1 + t] + krow(0, 2, 0) * h_0[t] for t in range(2)),
-    )
-    up1 = section_sums(
-        af_row(k, f, 1, 1) + raw[TU11] - raw[TU21] - u_0[0],
-        raw[TU11T] - raw[TU21T] - u_0[1],
-        *(krow(1, 0, 1) * raw[TH1 + t] + krow(1, 1, 1) * h_1[t] + krow(1, 2, 1) * h_0[t] for t in range(2)),
-    )
-    up = [
-        up0[t] + right_shift(up0[t] + up1[t], lane_col(q0l[t], r0) + lane_col(q1l[t], r1)) for t in range(2)
-    ]
-
-    hb_0 = [left_shift(raw[BH + t], lane_col(right_field(rt, t), e0)) for t in range(2)]
-    hb_1 = [left_shift(raw[BH1 + t], lane_col(right_field(rt, t), e1)) for t in range(2)]
-    ub_1 = [left_shift(raw[BU01 + t], lane_col(right_field(rt, 2 + t), e1)) for t in range(2)]
-    dn1 = section_sums(
-        af_row(k, f, 1, end) + raw[BU1] - raw[BU2] - ub_1[0],
-        raw[BU1T] - raw[BU2T] - ub_1[1],
-        *(krow(1, 0, end) * raw[BH + t] + krow(1, 1, end) * hb_0[t] + krow(1, 2, end) * hb_1[t] for t in range(2)),
-    )
-    dn0 = section_sums(
-        af_row(k, f, 0, end - 1) + raw[BU01] - raw[BU11] + raw[BU2],
-        raw[BU01T] - raw[BU11T] + raw[BU2T],
-        *(
-            krow(0, 0, end - 1) * raw[BH1 + t] + krow(0, 1, end - 1) * raw[BH + t] + krow(0, 2, end - 1) * hb_1[t]
-            for t in range(2)
-        ),
-    )
-    down = [
-        left_shift(dn1[t] + dn0[t], lane_col(q1r[t], e0) + lane_col(q0r[t], e1)) + dn1[t] for t in range(2)
-    ]
+    row = lambda n, t: raw[QROW + 2 * n + t]
+    last = iota((LV, raw.shape[2]), 1) == raw.shape[2] - 1
+    up, down = [], []
+    for t in range(2):
+        sums = row(0, t) + row(1, t)
+        first = jnp.where(last, last_lane(q0[t], 16), row(0, t))
+        up.append(first + right_shift(sums, first_lane(q0[t], 0) + first_lane(q1[t], 1)))
+        one = jnp.where(last, last_lane(q1[t], 31), row(2, t))
+        two = jnp.where(last, last_lane(q0[t], 30), row(3, t))
+        down.append(left_shift(one + two, last_lane(q1r[t], 31) + last_lane(q0r[t], 30)) + one)
 
     def store(msg_up, msg_down):
-        for msg, sums, parts, geo, r in (
-            (msg_up, up, (TH, THT, TU1, TU1T, TU2, TU2T, TG2), 1, 0),
-            (msg_down, down, (BH, BHT, BU0, BU0T, BU1, BU1T, BG0), 0, end),
-        ):
+        for msg, sums, r in ((msg_up, up, 0), (msg_down, down, rows - 1)):
             for n in range(2):
                 msg[LV * n : LV * n + LV, :] = sums[n]
-            for n, part in enumerate(parts[:6]):
-                msg[LV * (n + 2) : LV * (n + 3), :] = raw[part]
-            for n in range(3):
-                msg[64 + n : 65 + n, :] = krow(geo, n, r)
-            msg[67:68, :] = af_row(k, f, geo, r)
-            msg[68:69, 0:128] = left[r : r + 1, :]
-            msg[68:69, 128:256] = right[r : r + 1, :]
-            msg[69:70, :] = raw[parts[6], 0:1, :]
-            msg[70:72, :] = jnp.zeros((2, msg.shape[1]), F32)
-
-    @pl.when(odd_y)
-    def _():
-        store(msg_a, msg_b)
-
-    @pl.when(jnp.logical_not(odd_y))
-    def _():
-        store(msg_b, msg_a)
+            msg[68:69, 0:128] = slab_l[r : r + 1, :]
+            msg[68:69, 128:256] = slab_r[r : r + 1, :]
+
+    by_parity(store, msg_a, msg_b)
 
 
 (CY, _, CQ, CZ, CP, _, C0, _, C1, _) = range(10)
@@ -405,57 +397,28 @@
         kinetic[lev] = (en[0] + en[1] + en[2] + row_down(en[0], 0.0) + zz) * geo[8]
 
 
-def last_kernel(
-    k, f, geo, slab_l, slab_r, own0, raw, keep, vertex_v, kinetic_v, cell_v, edge_v, msg_a, msg_b,
-    vertex, kinetic, cell, edge, ext, turned, msgs, rim, tiles, sems,
-):
-    odd_y = lax.rem(lax.axis_index("py"), 2) == 1
-    rows = kinetic_v.shape[1]
+def rims(vertex, kinetic, cell, edge, ext, turned, k, f, geo, slab_l, slab_r, own0, raw, keep, up_msg, down_msg):
+    rows = slab_l.shape[0]
     end = rows - 1
-    arrays = (
-        [(vertex_v.at[n], vertex.at[n]) for n in range(2)]
-        + [(kinetic_v, kinetic), (cell_v, cell)]
-        + [(edge_v.at[n], edge.at[n]) for n in range(3)]
-    )
-    copies = []
-
-    def start(src, dst):
-        copy = pltpu.make_async_copy(src, dst, sems.at[len(copies)])
-        copy.start()
-        copies.append(copy)
-
-    top, bottom = slice(0, 8), slice(rows - 8, rows)
-    for n, (src, dst) in enumerate(arrays):
-        inner = slice(0 if n == 0 else 8, rows if n == 1 else rows - 8)
-        start(src.at[:, inner], dst.at[:, inner])
-
-    @pl.when(odd_y)
-    def _():
-        msgs[0] = msg_b[...]
-        msgs[1] = msg_a[...]
-
-    @pl.when(jnp.logical_not(odd_y))
-    def _():
-        msgs[0] = msg_a[...]
-        msgs[1] = msg_b[...]
-
-    above = lambda n: msgs[0, LV * n : LV * n + LV, :]
-    below = lambda n: msgs[1, LV * n : LV * n + LV, :]
-    ka = [msgs[0, 64 + n : 65 + n, :] for n in range(4)]
-    kb = [msgs[1, 64 + n : 65 + n, :] for n in range(4)]
+    above = lambda n: up_msg[LV * n : LV * n + LV, :]
+    below = lambda n: down_msg[LV * n : LV * n + LV, :]
+    ka = [up_msg[64 + n : 65 + n, :] for n in range(4)]
+    kb = [down_msg[64 + n : 65 + n, :] for n in range(4)]
     krow = lambda a, b, r: k[a, b, r : r + 1, :]
 
-    for n, x in enumerate((slab_l, slab_r, own0)):
-        ext[n, BASE : BASE + rows, :] = x[...]
-    ext[0, DNB : DNB + 1, :] = msgs[0, 68:69, 0:128]
-    ext[1, DNB : DNB + 1, :] = msgs[0, 68:69, 128:256]
-    ext[1, UPB : UPB + 1, :] = msgs[1, 68:69, 128:256]
-    lt, rt, ot = turn(turned, *(ext[n] for n in range(3)))
+    ext[0, BASE : BASE + rows, :] = slab_l[...]
+    ext[1, BASE : BASE + rows, :] = slab_r[...]
+    ext[1, OWN + BASE : OWN + BASE + rows, :] = own0[...]
+    ext[0, DNB : DNB + 1, :] = up_msg[68:69, 0:128]
+    ext[1, DNB : DNB + 1, :] = up_msg[68:69, 128:256]
+    ext[1, UPB : UPB + 1, :] = down_msg[68:69, 128:256]
+    lt, rt = turn(turned, ext[0], ext[1])
+    own = [pltpu.roll(right_field(rt, n), OWN, 1) for n in range(4)]
     lanes = iota((LV, 128), 1)
-    low = lambda x, row: jnp.where(lanes == UPB, row[:, 0:1], x)
-    high = lambda x, row: jnp.where(lanes == DNB, row[:, 0:1], x)
-    h0 = [high(low(right_field(ot, t), below(2 + t)), above(2 + t)) for t in range(2)]
-    u00 = [low(right_field(ot, 2 + t), below(4 + t)) for t in range(2)]
+    low = lambda x, row: jnp.where(lanes == UPB, pltpu.roll(row[:, 0:128], UPB, 1), x)
+    high = lambda x, row: jnp.where(lanes == DNB, pltpu.roll(row[:, 0:128], DNB, 1), x)
+    h0 = [high(low(own[t], below(2 + t)), above(2 + t)) for t in range(2)]
+    u00 = [low(own[2 + t], below(4 + t)) for t in range(2)]
     q0l, q1l = column_left(lt, *h0, *u00)
     q0r, q1r = column_right(rt)
     up = lambda x: pltpu.roll(x, 127, 1)
@@ -464,9 +427,9 @@
     pcol = [q0r[t] + q1r[t] + dn(q0r[t]) for t in range(2)]
     r0, re = BASE, BASE + end
 
-    hb1 = [left_shift(below(2 + t), lane_col(right_field(rt, t), UPB)) for t in range(2)]
-    ub1 = [left_shift(below(4 + t), lane_col(right_field(rt, 2 + t), UPB)) for t in range(2)]
-    h01 = [left_shift(raw[TH + t], lane_col(right_field(rt, t), BASE)) for t in range(2)]
+    hb1 = [left_shift(below(2 + t), last_lane(right_field(rt, t), UPB)) for t in range(2)]
+    ub1 = [left_shift(below(4 + t), last_lane(right_field(rt, 2 + t), UPB)) for t in range(2)]
+    h01 = [left_shift(raw[TH + t], last_lane(right_field(rt, t), BASE)) for t in range(2)]
     qb = section_sums(
         kb[3] + below(4) - below(6) + raw[TU2],
         below(5) - below(7) + raw[TU2T],
@@ -477,9 +440,9 @@
         raw[TU1T] - raw[TU2T] - ub1[1],
         *(krow(1, 0, 0) * raw[TH + t] + krow(1, 1, 0) * h01[t] + krow(1, 2, 0) * hb1[t] for t in range(2)),
     )
-    ha1 = [left_shift(above(2 + t), lane_col(right_field(rt, t), DNB)) for t in range(2)]
-    he1 = [left_shift(raw[BH + t], lane_col(right_field(rt, t), re)) for t in range(2)]
-    ue1 = [left_shift(raw[BU0 + t], lane_col(right_field(rt, 2 + t), re)) for t in range(2)]
+    ha1 = [left_shift(above(2 + t), last_lane(right_field(rt, t), DNB)) for t in range(2)]
+    he1 = [left_shift(raw[BH + t], last_lane(right_field(rt, t), re)) for t in range(2)]
+    ue1 = [left_shift(raw[BU0 + t], last_lane(right_field(rt, 2 + t), re)) for t in range(2)]
     qa = section_sums(
         ka[3] + above(4) - above(6) - ue1[0],
         above(5) - above(7) - ue1[1],
@@ -490,16 +453,23 @@
         raw[BU0T] - raw[BU1T] + above(7),
         *(krow(0, 0, end) * raw[BH + t] + krow(0, 1, end) * above(2 + t) + krow(0, 2, end) * he1[t] for t in range(2)),
     )
+    vertex[1, :, 0, :] = q1f[0]
+    vertex[0, :, end, :] = q0e[0]
+    low_energy = energy(down_msg[69:70, :], below(4), below(5))
+    high_energy = energy(up_msg[69:70, :], above(6), above(7))
+    high_energy = right_shift(high_energy, first_lane(lt[LEN + LV : LEN + 2 * LV, :], DNB))
+    kinetic[:, 0, :] = kinetic[:, 0, :] + low_energy * geo[8, 0:1, :]
+    kinetic[:, end, :] = kinetic[:, end, :] + high_energy * geo[8, end : end + 1, :]
     grads = []
     for t in range(2):
         p0, y0 = keep[K00 + t] + q1f[t] + qb[t], keep[K00 + t] + q1f[t] + keep[K11 + t]
         pe, ye = q0e[t] + keep[K1E + t] + keep[K0B + t], q0e[t] + keep[K1E + t] + qa[t]
-        m0 = p0 + right_shift(y0, lane_col(ycol[t], r0))
-        m0r = left_shift(p0, lane_col(pcol[t], r0)) + y0
-        me = pe + right_shift(ye, lane_col(ycol[t], re))
-        mer = left_shift(pe, lane_col(pcol[t], re)) + ye
-        m_above = above(t) + qa[t] + right_shift(qa[t], lane_col(q1l[t], DNB)) + q0e[t]
-        m_below = below(t) + qb[t] + left_shift(qb[t], lane_col(q0r[t], UPB)) + q1f[t]
+        m0 = p0 + right_shift(y0, first_lane(ycol[t], r0))
+        m0r = left_shift(p0, last_lane(pcol[t], r0)) + y0
+        me = pe + right_shift(ye, first_lane(ycol[t], re))
+        mer = left_shift(pe, last_lane(pcol[t], re)) + ye
+        m_above = above(t) + qa[t] + right_shift(qa[t], first_lane(q1l[t], DNB)) + q0e[t]
+        m_below = below(t) + qb[t] + left_shift(qb[t], last_lane(q0r[t], UPB)) + q1f[t]
         grads.append(
             (
                 keep[KM1 + t] - m0,
@@ -513,49 +483,60 @@
             )
         )
         if t == 0:
-            rim[8] = q1f[0]
-            rim[9] = m0 * (1.0 / 6.0)
-            rim[10] = q0e[0]
-            rim[11] = me * (1.0 / 6.0)
+            cell[:, 0, :] = m0 * (1.0 / 6.0)
+            cell[:, end, :] = me * (1.0 / 6.0)
             means = (
-                keep[K00] + right_shift(keep[K11], lane_col(q1l[0], r0 + 1)),
+                keep[K00] + right_shift(keep[K11], first_lane(q1l[0], r0 + 1)),
                 keep[K00] + q1f[0],
                 q1f[0] + qb[0],
                 keep[K11] + keep[K00],
-                keep[K0B] + right_shift(keep[K1E], lane_col(q1l[0], re)),
-                q0e[0] + right_shift(qa[0], lane_col(q1l[0], DNB)),
+                keep[K0B] + right_shift(keep[K1E], first_lane(q1l[0], re)),
+                q0e[0] + right_shift(qa[0], first_lane(q1l[0], DNB)),
                 q0e[0] + keep[K1E],
                 keep[K1E] + keep[K0B],
             )
     for n, (e, r) in enumerate(RIM):
         r = r % rows
-        rim[n] = 0.5 * means[n] - geo[2 + e, r : r + 1, :] * (
+        edge[e, :, r, :] = 0.5 * means[n] - geo[2 + e, r : r + 1, :] * (
             raw[30 + 2 * n] * grads[0][n] + raw[31 + 2 * n] * grads[1][n]
         )
-    rim[12] = energy(msgs[1, 69:70, :], below(4), below(5)) * geo[8, 0:1, :]
-    rim[13] = right_shift(energy(msgs[0, 69:70, :], above(6), above(7)), lane_col(lt[LEN + LV : LEN + 2 * LV, :], DNB)) * geo[8, end : end + 1, :]
-
-    spot = iota((8, kinetic_v.shape[2]), 0)
-    tile = 0
-    for part, patches in (
-        (top, ((1, ((0, 8),)), (2, ((0, 12),)), (3, ((0, 9),)), (4, ((0, 0),)), (5, ((0, 1),)), (6, ((0, 2), (1, 3))))),
-        (bottom, ((0, ((7, 10),)), (2, ((7, 13),)), (3, ((7, 11),)), (4, ((6, 4), (7, 5))), (5, ((7, 6),)), (6, ((7, 7),)))),
-    ):
-        for n, changes in patches:
-            src, dst = arrays[n]
-            for lev in range(LV):
-                x = src[lev, part, :]
-                for r, m in changes:
-                    new = rim[m, lev : lev + 1, :]
-                    x = jnp.where(spot == r, x + new if n == 2 else new, x)
-                tiles[tile, lev] = x
-            start(tiles.at[tile], dst.at[:, part])
-            tile += 1
+
+
+def last_kernel(
+    k, f, geo, slab_l, slab_r, own0, raw, keep, vertex_i, kinetic_i, cell_i, edge_i, msg_a, msg_b,
+    vertex, kinetic, cell, edge, vertex_v, kinetic_v, cell_v, edge_v, ext, turned, sems,
+):
+    rows = kinetic_v.shape[1]
+    copies = []
+
+    def start(src, dst):
+        copy = pltpu.make_async_copy(src, dst, sems.at[len(copies)])
+        copy.start()
+        copies.append(copy)
+
+    def start_rows(low, high, vertices):
+        part = slice(low, high)
+        for n, part_n in vertices:
+            start(vertex_v.at[n, :, part_n], vertex.at[n, :, part_n])
+        start(kinetic_v.at[:, part], kinetic.at[:, part])
+        start(cell_v.at[:, part], cell.at[:, part])
+        start(edge_v.at[:, :, part], edge.at[:, :, part])
+
+    start_rows(8, rows - 8, ((0, slice(0, rows - 8)), (1, slice(8, rows))))
+    by_parity(
+        functools.partial(
+            rims, vertex_v, kinetic_v, cell_v, edge_v, ext, turned, k, f, geo, slab_l, slab_r, own0, raw, keep
+        ),
+        msg_b,
+        msg_a,
+    )
+    start_rows(0, 8, ((1, slice(0, 8)),))
+    start_rows(rows - 8, rows, ((0, slice(rows - 8, rows)),))
     for copy in copies:
         copy.wait()
 
 
-LAST_COPIES = 7 + 12
+LAST_COPIES = 5 + 4 + 4
 
 
 def shift(x, axis, by):
@@ -576,14 +557,13 @@
 ANY = pl.BlockSpec(memory_space=pl.ANY)
 
 
-def call(kernel, args, outs, scratch=(), sems=0, hbm_in=False, hbm_out=False, flops=0, alias=None):
+def call(kernel, args, outs, scratch=(), sems=0, hbm_in=False, hbm_out=0, flops=0, alias=None):
     args = [pltpu.with_memory_space_constraint(x, pltpu.HBM if hbm_in else pltpu.VMEM) for x in args]
-    shape = (lambda s: jax.ShapeDtypeStruct(s, F32)) if hbm_out else (lambda s: pltpu.VMEM(s, F32))
     return pl.pallas_call(
         kernel,
-        out_shape=[shape(s) for s in outs],
+        out_shape=[jax.ShapeDtypeStruct(s, F32) if n < hbm_out else pltpu.VMEM(s, F32) for n, s in enumerate(outs)],
         in_specs=[ANY if hbm_in else VM] * len(args),
-        out_specs=[ANY if hbm_out else VM] * len(outs),
+        out_specs=[ANY if n < hbm_out else VM for n in range(len(outs))],
         scratch_shapes=[pltpu.VMEM(s, F32) for s in scratch]
         + ([pltpu.SemaphoreType.DMA((sems,))] if sems else []),
         input_output_aliases=alias or {},
@@ -602,15 +582,19 @@
     slab_l = shift(send_right, "px", 1)
     slab_r = shift(send_left, "px", -1)
     whole = [(2, levels, rows, cols), (levels, rows, cols), (levels, rows, cols), (3, levels, rows, cols)]
-    raw, geo, q = call(
+    raw, geo, q, msg_a, msg_b = call(
         vertex_kernel,
         held,
-        [(RAW, levels, cols), (9, rows, cols), (2, 2, levels, rows, cols)],
+        [(RAW, levels, cols), (9, rows, cols), (2, 2, levels, rows, cols), (72, cols), (72, cols)],
         flops=40_000_000,
     )
     turned = [(4, 128, 128), (4, 128, 128)]
     msg_a, msg_b = call(
-        merge_kernel, [slab_l, slab_r, send_left, raw, k, f], [(72, cols), (72, cols)], turned
+        merge_kernel,
+        [slab_l, slab_r, send_left, send_right, raw, msg_a, msg_b],
+        [(72, cols), (72, cols)],
+        [(2, 128, 128), (2, 128, 128)],
+        alias={5: 0, 6: 1},
     )
     msg_b = swap(msg_b, "py", 1)
     msg_a = swap(msg_a, "py", 0)
@@ -625,16 +609,16 @@
         flops=40_000_000,
         alias={len(sources) + n: n for n in range(5)},
     )
-    return tuple(
-        call(
-            last_kernel,
-            [k, f, geo, slab_l, slab_r, send_left, raw, keep, *parts, msg_a, msg_b],
-            whole,
-            turned + [(2, 72, cols), (14, levels, cols), (12, levels, 8, cols)],
-            sems=LAST_COPIES,
-            hbm_out=True,
-        )
-    )
+    outs = call(
+        last_kernel,
+        [k, f, geo, slab_l, slab_r, send_left, raw, keep, *parts, msg_a, msg_b],
+        whole + whole,
+        [(2, 128, 128), (2, 128, 128)],
+        sems=LAST_COPIES,
+        hbm_out=4,
+        alias={8 + n: 4 + n for n in range(4)},
+    )
+    return tuple(outs[:4])
 
 
 def solution(mesh):

time: 19.6 us -> 19.6 us (level)
  no operation moved by 1% of the time
where the time goes in v6:
time: 19.6 us; the launch traced here: 19.4 us
  starting transfers between devices  10.9 us (56%)
  Pallas kernels  6.74 us (34%)
  waiting for transfers between devices  1.14 us (6%)
  between operations  0.68 us (3%)
    pallas_call x6, Pallas kernels, call(): pl.pallas_call(kernel, out_shape=[jax.ShapeDtypeStruct(s, F32) if n < hbm...  6.74 us
    ppermute x2, starting transfers between devices, swap(): return lax.ppermute(x, axis, pairs)  6.52 us
    ppermute x2, starting transfers between devices, shift(): return lax.ppermute(x, axis, [(i, (i + by) % n) for i in range(n)])  4.37 us
    ppermute x2, waiting for transfers between devices, swap(): return lax.ppermute(x, axis, pairs)  0.63 us
    ppermute x2, waiting for transfers between devices, shift(): return lax.ppermute(x, axis, [(i, (i + by) % n) for i in range(n)])  0.51 us
  transfers between devices with their start and end apart: 4, of which 2 were waited for; matrix products, arithmetic and copies ran while one was open for 0% of the time, Pallas kernels for 13%

profile of v6, /device:TPU:0, one launch (start us, length us, event | category | flops | bytes accessed | tf_op | source)
XLA Modules:
  0.0 19.4 jit_solution(8535851503342417006)
XLA Ops:
  0.6 2.4 %shard_map.120 = (f32[32,128]{1,0:T(8,128)S(1)}, f32[32,128]{1,0:T(8,128)S(1)}, f32[3,8,32,256]{3,2,1,0:T(8,128)S(1)}, f32[8,32,256]{2,1,0:T(8,128)S(1)}, f32[3,...) custom-call(f32[3,8,32,256]{3,2,1,0:T(8,128)} %v.1, ...), custom_call_target="tpu_custom_call" | custom-call | tf_op jit(solution)/shard_map/pallas_call | solution.py:562
  3.0 2.1 %collective-permute-start = (f32[32,128]{1,0:T(8,128)S(1)}, f32[32,128]{1,0:T(8,128)S(1)}, u32[]{:S(2)}, u32[]{:S(2)}) collective-permute-start(f32[32,128]{1,0:T(8,128)S(1)} %get-tuple-element.46.refs_7_.own_r), channel_id=1, source_target_pairs={{0,16},{16,32},{32,48},{48,64},{64,80},{80,96},{96,112},{112,0},{1... | collective-permute-start | bytes 49160 | tf_op jit(solution)/shard_map/ppermute | solution.py:544
  5.1 2.3 %collective-permute-start.1 = (f32[32,128]{1,0:T(8,128)S(1)}, f32[32,128]{1,0:T(8,128)S(1)}, u32[]{:S(2)}, u32[]{:S(2)}) collective-permute-start(f32[32,128]{1,0:T(8,128)S(1)} %get-tuple-element.47.refs_6_.own_l.own0), channel_id=1, source_target_pairs={{0,112},{16,0},{32,16},{48,32},{64,48},{80,64},{96,80},{112,96},{1... | collective-permute-start | bytes 49160 | tf_op jit(solution)/shard_map/ppermute | solution.py:544
  7.4 1.1 %shard_map.121 = (f32[54,8,256]{2,1,0:T(8,128)S(1)}, f32[9,32,256]{2,1,0:T(8,128)S(1)}, f32[2,2,8,32,256]{4,3,2,1,0:T(8,128)S(1)}, f32[72,256]{1,0:T(8,128)S(1)}, f32[72,256]{1,0:T(8,128)S(1)}) custom-call(f32[3,8,32,256]{3,2,1,0:T(8,128)S(1)} %get-tuple-element.38.v.refs_0_, f32[8,32,256]{2,1,0:T(8,128)S(1)} %get-tuple-element.39.h, ...), custom_call_target="tpu_custom_call" | custom-call | flops 40000000 | tf_op jit(solution)/shard_map/pallas_call | solution.py:562
  8.5 0.5 %collective-permute-done.refs_4_.slab_l = f32[32,128]{1,0:T(8,128)S(1)} collective-permute-done((f32[32,128]{1,0:T(8,128)S(1)}, f32[32,128]{1,0:T(8,128)S(1)}, u32[]{:S(2)}, u32[]{:S(2)}) %collective-permute-start) | collective-permute-done | bytes 16416 | tf_op jit(solution)/shard_map/ppermute | solution.py:544
  9.1 0.0 collective-permute-done.1.refs_5_.slab_r
  9.1 0.3 %shard_map.124 = (f32[72,256]{1,0:T(8,128)S(1)}, f32[72,256]{1,0:T(8,128)S(1)}) custom-call(f32[32,128]{1,0:T(8,128)S(1)} %collective-permute-done.refs_4_.slab_l, f32[32,128]{1,0:T(8,128)S(1)} %collective-permute-done.1.refs_5_.slab_r, f32[32,128]{1,0:T(8,128)S(1)} %get-tuple-element.47.refs_6_.own_l.own0, ...), custom_call_target="tpu_custom_call", output_to_operand_aliasing={{0}: (5, {}), {1}: (6, {})} | custom-call | tf_op jit(solution)/shard_map/pallas_call | solution.py:562
  9.4 0.1 collective-permute-start.2
  9.5 6.4 %collective-permute-start.3 = (f32[72,256]{1,0:T(8,128)S(1)}, f32[72,256]{1,0:T(8,128)S(1)}, u32[]{:S(2)}, u32[]{:S(2)}) collective-permute-start(f32[72,256]{1,0:T(8,128)S(1)} %get-tuple-element.63), channel_id=1, source_target_pairs={{1,2},{2,1},{3,4},{4,3},{5,6},{6,5},{7,8},{8,7},{9,10},{10,9},{11,... | collective-permute-start | bytes 221192 | tf_op jit(solution)/shard_map/ppermute | solution.py:553
  15.9 1.4 %shard_map.123 = (f32[2,8,32,256]{3,2,1,0:T(8,128)S(1)}, f32[8,32,256]{2,1,0:T(8,128)S(1)}, f32[8,32,256]{2,1,0:T(8,128)S(1)}, f32[3,8,32,256]{3,2,1,0:T(8,128)S(1)}, f32[14,8,256]{2,1,0:T(8,128)S(1)}) custom-call(f32[3,8,32,256]{3,2,1,0:T(8,128)S(1)} %get-tuple-element.38.v.refs_0_, ...), custom_call_target="tpu_custom_call", output_to_operand_aliasing={{0}: (8, {}), {1}: (9, {}), {2}: (10, {}), {3}: (11, {}), {... | custom-call | flops 40000000 | tf_op jit(solution)/shard_map/pallas_call | solution.py:562
  17.3 0.0 collective-permute-done.2.msg_a
  17.3 0.6 %collective-permute-done.3.msg_b = f32[72,256]{1,0:T(8,128)S(1)} collective-permute-done((f32[72,256]{1,0:T(8,128)S(1)}, f32[72,256]{1,0:T(8,128)S(1)}, u32[]{:S(2)}, u32[]{:S(2)}) %collective-permute-start.3) | collective-permute-done | bytes 73760 | tf_op jit(solution)/shard_map/ppermute | solution.py:553
  18.0 1.5 %shard_map.125 = (f32[2,8,32,256]{3,2,1,0:T(8,128)}, f32[8,32,256]{2,1,0:T(8,128)}, f32[8,32,256]{2,1,0:T(8,128)}, f32[3,8,32,256]{3,2,1,0:T(8,128)}, f32[2,8,32...) custom-call(f32[2,3,32,256]{3,2,1,0:T(8,128)S(1)} %get-tuple-element, ...), custom_call_target="tpu_custom_call", output_to_operand_aliasing={{4}: (8, {}), {5}: (9, {}), {6}: (10, {}), {7}: (11, {})} | custom-call | tf_op jit(solution)/shard_map/pallas_call | solution.py:562
  (1 shorter events, 0.0 us)
Async XLA Ops:
  3.0 6.0 %collective-permute-start = (f32[32,128]{1,0:T(8,128)S(1)}, f32[32,128]{1,0:T(8,128)S(1)}, u32[]{:S(2)}, u32[]{:S(2)}) collective-permute-start(f32[32,128]{1,0:T(8,128)S(1)} %get-tuple-element.46.refs_7_.own_r), channel_id=1, source_target_pairs={{0,16},{16,32},{32,48},{48,64},{64,80},{80,96},{96,112},{112,0},{1... | collective-permute-start | bytes 49160 | tf_op jit(solution)/shard_map/ppermute | solution.py:544
  5.1 3.9 %collective-permute-start.1 = (f32[32,128]{1,0:T(8,128)S(1)}, f32[32,128]{1,0:T(8,128)S(1)}, u32[]{:S(2)}, u32[]{:S(2)}) collective-permute-start(f32[32,128]{1,0:T(8,128)S(1)} %get-tuple-element.47.refs_6_.own_l.own0), channel_id=1, source_target_pairs={{0,112},{16,0},{32,16},{48,32},{64,48},{80,64},{96,80},{112,96},{1... | collective-permute-start | bytes 49160 | tf_op jit(solution)/shard_map/ppermute | solution.py:544
  9.4 7.9 %collective-permute-start.2 = (f32[72,256]{1,0:T(8,128)S(1)}, f32[72,256]{1,0:T(8,128)S(1)}, u32[]{:S(2)}, u32[]{:S(2)}) collective-permute-start(f32[72,256]{1,0:T(8,128)S(1)} %get-tuple-element.62), channel_id=1, source_target_pairs={{0,1},{1,0},{2,3},{3,2},{4,5},{5,4},{6,7},{7,6},{8,9},{9,8},{10,11... | collective-permute-start | bytes 221192 | tf_op jit(solution)/shard_map/ppermute | solution.py:553
  9.5 8.5 %collective-permute-start.3 = (f32[72,256]{1,0:T(8,128)S(1)}, f32[72,256]{1,0:T(8,128)S(1)}, u32[]{:S(2)}, u32[]{:S(2)}) collective-permute-start(f32[72,256]{1,0:T(8,128)S(1)} %get-tuple-element.63), channel_id=1, source_target_pairs={{1,2},{2,1},{3,4},{4,3},{5,6},{6,5},{7,8},{8,7},{9,10},{10,9},{11,... | collective-permute-start | bytes 221192 | tf_op jit(solution)/shard_map/ppermute | solution.py:553
